TPU v7x, 512 devices: a whole 4x8x8 slice. The times are simulated.
512 devices in a mesh: gx: 8 (over z), gy: 8 (over y_lo, x), gz: 8 (over y_hi, core).
Axes of the slice: x: 4, y: 8 (y_hi: 4, y_lo: 2; y = y_hi * 2 + y_lo), z: 8, core: 2. Of those that a mesh axis runs over, the one named last changes fastest.
Arguments:
- orbitals: bfloat16 [8, 256, 65536], P(None, 'gx', ('gy', 'gz')), may hold values from -6 to 6
- potential: float32 [128, 128, 128], P('gx', 'gy', 'gz'), may hold values from -3 to 0
- ion_potential: float32 [128, 128, 128], P('gx', 'gy', 'gz'), may hold values from -2 to 0
- occupations: float32 [8], replicated, may hold values from 0.005 to 0.08
Outputs:
- new_orbitals: bfloat16 [8, 256, 65536], P(None, 'gx', ('gy', 'gz'))
- density: float32 [128, 128, 128], P('gx', 'gy', 'gz')
- new_potential: float32 [256, 65536], P('gx', ('gy', 'gz'))
All inputs are finite; a program needn't handle non-finite values.
Results may differ from a plain program's by a relative error of at most 0.001.
Values sent between devices are 32-bit elements; how exact they have to be, the bound alone decides.
No kernel may reach another device: no remote copies, remote signals or barrier semaphores. Data moves between devices by JAX's collectives and lax.ppermute only.
A program may use at most 64 MiB of HBM per device.

v0:
```python
import math

import jax
import jax.numpy as jnp
from jax import lax
from jax.sharding import PartitionSpec as P

BUF = 8
DEGREE = 10


spacing = 0.2
kinetic = 0.5 / (spacing * spacing)
filter_low = 6.0
filter_high = 12.0 * kinetic
centre_value = 0.5 * (filter_low + filter_high)
half_width = 0.5 * (filter_high - filter_low)


def padded_2(x, sides, width):
    for axis, dim in sides:
        count, length = (lax.axis_size(axis), x.shape[dim])
        up = [(i, (i + 1) % count) for i in range(count)]
        down = [(j, i) for i, j in up]
        last = lax.slice_in_dim(x, length - width, length, axis=dim)
        first = lax.slice_in_dim(x, 0, width, axis=dim)
        before = lax.ppermute(last, axis, up)
        after = lax.ppermute(first, axis, down)
        x = jnp.concatenate([before, x, after], axis=dim)
    return x


def shifted(x, axis, by):
    count = lax.axis_size(axis)
    return lax.ppermute(x, axis, [(i, (i + by) % count) for i in range(count)])


def in_one_piece(arrays, axis, split_dim, concat_dim, along):
    ends, at = ([], 0)
    for a in arrays[:-1]:
        at += a.shape[along]
        ends.append(at)
    both = jnp.concatenate(arrays, axis=along)
    return tuple(
        jnp.split(
            lax.all_to_all(both, axis, split_axis=split_dim, concat_axis=concat_dim, tiled=True),
            ends,
            axis=along,
        )
    )


def hamiltonian(vectors, potential_ext, edge_len):
    extent = vectors.shape[2]
    padded = jnp.pad(vectors, ((0, 0), (1, 1), (0, 0)))
    beside = padded[:, 2:] + padded[:, :-2]
    padded = jnp.pad(vectors, ((0, 0), (0, 0), (edge_len, edge_len)))
    beside = beside + padded[:, :, 2 * edge_len :] + padded[:, :, : -2 * edge_len]
    padded = jnp.pad(vectors, ((0, 0), (0, 0), (1, 1)))
    column = jnp.arange(extent, dtype=jnp.int32) % edge_len
    up_mask = (column < edge_len - 1).astype(vectors.dtype)
    down_mask = (column > 0).astype(vectors.dtype)
    beside = beside + padded[:, :, 2:] * up_mask + padded[:, :, :-2] * down_mask
    return -kinetic * (beside - 6.0 * vectors) + potential_ext * vectors


def chebyshev(initial, potential_ext, edge_len):
    leading = (hamiltonian(initial, potential_ext, edge_len) - centre_value * initial) / half_width

    def advance(counter, states):
        previous, current = states
        following = (
            2.0
            * (hamiltonian(current, potential_ext, edge_len) - centre_value * current)
            / half_width
            - previous
        )
        return (current, following)

    return lax.fori_loop(1, DEGREE, advance, (initial, leading))[1]


def orthonormal(filtered):
    orbital_count = filtered.shape[0]
    flattened = filtered.reshape(orbital_count, -1)
    intersection = (
        jnp.dot(flattened, flattened.T, precision=lax.Precision.HIGHEST) / flattened.shape[1]
    )
    factor = jnp.linalg.cholesky(intersection)
    identity = jnp.eye(orbital_count, dtype=filtered.dtype)
    inverse = lax.linalg.triangular_solve(factor, identity, left_side=True, lower=True)
    return jnp.dot(inverse, flattened, precision=lax.Precision.HIGHEST).reshape(filtered.shape)


def ramp(extent):
    position = jnp.arange(extent, dtype=jnp.float32)
    rising = jnp.clip((position + 0.5 - 0.5 * BUF) / BUF, 0.0, 1.0)
    falling = jnp.clip((extent - 0.5 * BUF - 0.5 - position) / BUF, 0.0, 1.0)
    return rising * falling


def window_weight(edge_len):
    profile = ramp(edge_len)
    return profile[:, None] * (profile[:, None] * profile[None, :]).reshape(1, edge_len * edge_len)


def exchange_correlation(density):
    cube_root = jnp.cbrt(density)
    slater = -((3.0 / math.pi) ** (1.0 / 3.0)) * cube_root
    radius = (3.0 / (4.0 * math.pi)) ** (1.0 / 3.0)
    bottom = radius + 7.8 * cube_root
    wigner = -0.44 * cube_root / bottom * (1.0 + radius / (3.0 * bottom))
    return slater + wigner


def wave_term(extent, initial, period):
    indices = (initial + jnp.arange(extent, dtype=jnp.int32)).astype(jnp.float32)
    return 4.0 / (spacing * spacing) * jnp.sin(math.pi * indices / period) ** 2


def kernel(extents, starts, periods):
    eigen_sum = (
        wave_term(extents[0], starts[0], periods[0])[:, None, None]
        + wave_term(extents[1], starts[1], periods[1])[None, :, None]
        + wave_term(extents[2], starts[2], periods[2])[None, None, :]
    )
    positive = eigen_sum > 0.0
    return jnp.where(positive, 4.0 * math.pi / jnp.where(positive, eigen_sum, 1.0), 0.0)


def twiddle(extent):
    indices = jnp.arange(extent, dtype=jnp.int32)
    angles = (indices[:, None] * indices[None, :] % extent).astype(jnp.float32) * (
        2.0 * math.pi / extent
    )
    return (jnp.cos(angles), jnp.sin(angles))


def contract(values, matrix, axis_dim):
    product = jnp.tensordot(
        values, matrix, axes=((axis_dim,), (0,)), precision=lax.Precision.HIGHEST
    )
    return jnp.moveaxis(product, -1, axis_dim)


def transform(real_part, imag_part, axis_dim, direction):
    cosine, sine_table = twiddle(real_part.shape[axis_dim])
    if imag_part is None:
        return (
            contract(real_part, cosine, axis_dim),
            -direction * contract(real_part, sine_table, axis_dim),
        )
    return (
        contract(real_part, cosine, axis_dim)
        + direction * contract(imag_part, sine_table, axis_dim),
        contract(imag_part, cosine, axis_dim)
        - direction * contract(real_part, sine_table, axis_dim),
    )


def real_back(real_part, imag_part, axis_dim):
    cosine, sine_table = twiddle(real_part.shape[axis_dim])
    return contract(real_part, cosine, axis_dim) - contract(imag_part, sine_table, axis_dim)


def refill(interior):
    return padded_2(interior, (("gx", 0), ("gy", 1), ("gz", 2)), BUF)


def fold(partial_value):
    layers = BUF // 2
    core_len = partial_value.shape[0] - 2 * BUF
    shift_pad = core_len - layers
    from_next = shifted(partial_value[BUF - layers : BUF], "gx", -1)
    from_prev = shifted(partial_value[BUF + core_len : BUF + core_len + layers], "gx", 1)
    folded = (
        partial_value[BUF : BUF + core_len]
        + jnp.pad(from_next, ((shift_pad, 0), (0, 0), (0, 0)))
        + jnp.pad(from_prev, ((0, shift_pad), (0, 0), (0, 0)))
    )
    from_next = shifted(folded[:, BUF - layers : BUF], "gy", -1)
    from_prev = shifted(folded[:, BUF + core_len : BUF + core_len + layers], "gy", 1)
    folded = (
        folded[:, BUF : BUF + core_len]
        + jnp.pad(from_next, ((0, 0), (shift_pad, 0), (0, 0)))
        + jnp.pad(from_prev, ((0, 0), (0, shift_pad), (0, 0)))
    )
    from_next = shifted(folded[:, :, BUF - layers : BUF], "gz", -1)
    from_prev = shifted(folded[:, :, BUF + core_len : BUF + core_len + layers], "gz", 1)
    return (
        folded[:, :, BUF : BUF + core_len]
        + jnp.pad(from_next, ((0, 0), (0, 0), (shift_pad, 0)))
        + jnp.pad(from_prev, ((0, 0), (0, 0), (0, shift_pad)))
    )


def poisson(density):
    core_len = density.shape[0]
    periods = (
        core_len * lax.axis_size("gx"),
        core_len * lax.axis_size("gy"),
        core_len * lax.axis_size("gz"),
    )
    scaling = 1.0 / (periods[0] * periods[1] * periods[2])
    pencil = lax.all_to_all(density, "gz", split_axis=0, concat_axis=2, tiled=True)
    real_part, imag_part = transform(pencil, None, 2, 1.0)
    real_part, imag_part = in_one_piece((real_part, imag_part), "gy", 2, 1, 0)
    real_part, imag_part = transform(real_part, imag_part, 1, 1.0)
    real_part, imag_part = in_one_piece((real_part, imag_part), ("gx", "gz"), 1, 0, 2)
    real_part, imag_part = transform(real_part, imag_part, 0, 1.0)
    extents = real_part.shape
    starts = (0, lax.axis_index(("gx", "gz")) * extents[1], lax.axis_index("gy") * extents[2])
    weights_k = kernel(extents, starts, periods) * scaling
    real_part, imag_part = transform(real_part * weights_k, imag_part * weights_k, 0, -1.0)
    real_part, imag_part = in_one_piece((real_part, imag_part), ("gx", "gz"), 0, 1, 2)
    real_part, imag_part = transform(real_part, imag_part, 1, -1.0)
    real_part, imag_part = in_one_piece((real_part, imag_part), "gy", 1, 2, 0)
    z_field = real_back(real_part, imag_part, 2)
    return lax.all_to_all(z_field, "gz", split_axis=2, concat_axis=0, tiled=True)


def on_device(orbitals, potential, ion_potential, occupations):
    window_edge = orbitals.shape[1]
    plane_cells = window_edge * window_edge
    potential_ext = refill(potential).reshape(window_edge, plane_cells)
    filtered = chebyshev(orbitals.astype(jnp.float32), potential_ext, window_edge)
    normal_set = orthonormal(filtered)
    new_orbitals = normal_set.astype(jnp.bfloat16)
    partial_value = window_weight(window_edge) * jnp.sum(
        occupations[:, None, None] * normal_set * normal_set, axis=0
    )
    density = fold(partial_value.reshape(window_edge, window_edge, window_edge))
    hartree = poisson(density)
    interior = ion_potential + hartree + exchange_correlation(density)
    new_potential = refill(interior).reshape(window_edge, plane_cells)
    return (new_orbitals, density, new_potential)


def solution(mesh):
    placed = (P(None, "gx", ("gy", "gz")), P("gx", "gy", "gz"), P("gx", "gy", "gz"), P())
    return jax.shard_map(
        on_device,
        mesh=mesh,
        in_specs=placed,
        out_specs=(P(None, "gx", ("gy", "gz")), P("gx", "gy", "gz"), P("gx", ("gy", "gz"))),
        check_vma=False,
    )
```

profile of v0, /device:TPU:1, one launch (start us, length us, event | category | flops | bytes accessed | tf_op | source)
XLA Modules:
  0.0 245.1 jit_solution(1450375219269822736)
XLA Ops:
  1.5 4.8 %collective-permute-start = (f32[8,16,16]{2,1,0:T(8,128)S(1)}, f32[8,16,16]{2,1,0:T(8,128)S(1)}, u32[]{:S(2)}, u32[]{:S(2)}) collective-permute-start(f32[8,16,16]{2,1,0:T(8,128)S(1)} %get-tuple-element.104), channel_id=1, source_target_pairs={{0,64},{64,128},{128,192},{192,256},{256,320},{320,384},{384,448},... | collective-permute-start | bytes 24584 | tf_op jit(solution)/shard_map/ppermute | solution.py:27
  6.3 8.6 %collective-permute-start.1 = (f32[8,16,16]{2,1,0:T(8,128)S(1)}, f32[8,16,16]{2,1,0:T(8,128)S(1)}, u32[]{:S(2)}, u32[]{:S(2)}) collective-permute-start(f32[8,16,16]{2,1,0:T(8,128)S(1)} %get-tuple-element.103), channel_id=1, source_target_pairs={{64,0},{128,64},{192,128},{256,192},{320,256},{384,320},{448,384},... | collective-permute-start | bytes 24584 | tf_op jit(solution)/shard_map/ppermute | solution.py:28
  16.3 5.4 %collective-permute-start.3 = (f32[32,8,16]{2,1,0:T(8,128)S(1)}, f32[32,8,16]{2,1,0:T(8,128)S(1)}, u32[]{:S(2)}, u32[]{:S(2)}) collective-permute-start(f32[32,8,16]{2,1,0:T(8,128)S(1)} %get-tuple-element.94), channel_id=1, source_target_pairs={{8,0},{16,8},{24,16},{32,24},{40,32},{48,40},{56,48},{0,56},{9,1},... | collective-permute-start | bytes 49160 | tf_op jit(solution)/shard_map/ppermute | solution.py:28
  23.7 5.8 %collective-permute-done.2 = f32[32,8,16]{2,1,0:T(8,128)S(1)} collective-permute-done((f32[32,8,16]{2,1,0:T(8,128)S(1)}, f32[32,8,16]{2,1,0:T(8,128)S(1)}, u32[]{:S(2)}, u32[]{:S(2)}) %collective-permute-start.2) | collective-permute-done | bytes 16416 | tf_op jit(solution)/shard_map/ppermute | solution.py:27
  30.5 4.9 %collective-permute-start.5 = (f32[32,32,8]{2,1,0:T(8,128)}, f32[32,32,8]{2,1,0:T(8,128)S(1)}, u32[]{:S(2)}, u32[]{:S(2)}) collective-permute-start(f32[32,32,8]{2,1,0:T(8,128)} %get-tuple-element.84), channel_id=1, source_target_pairs={{1,0},{2,1},{3,2},{4,3},{5,4},{6,5},{7,6},{0,7},{9,8},{10,9},{11,1... | collective-permute-start | bytes 98312 | tf_op jit(solution)/shard_map/ppermute | solution.py:28
  35.4 4.1 %collective-permute-start.4 = (f32[32,32,8]{2,1,0:T(8,128)S(1)}, f32[32,32,8]{2,1,0:T(8,128)}, u32[]{:S(2)}, u32[]{:S(2)}) collective-permute-start(f32[32,32,8]{2,1,0:T(8,128)S(1)} %get-tuple-element.83), channel_id=1, source_target_pairs={{0,1},{1,2},{2,3},{3,4},{4,5},{5,6},{6,7},{7,0},{8,9},{9,10},{10,1... | collective-permute-start | bytes 98312 | tf_op jit(solution)/shard_map/ppermute | solution.py:27
  39.7 10.5 %collective-permute-done.5 = f32[32,32,8]{2,1,0:T(8,128)S(1)} collective-permute-done((f32[32,32,8]{2,1,0:T(8,128)}, f32[32,32,8]{2,1,0:T(8,128)S(1)}, u32[]{:S(2)}, u32[]{:S(2)}) %collective-permute-start.5) | collective-permute-done | bytes 32800 | tf_op jit(solution)/shard_map/ppermute | solution.py:28
  53.2 12.4 %while.15 = (s32[]{:T(128)}, f32[8,32,1024]{2,1,0:T(8,128)S(1)}, f32[8,32,1024]{2,1,0:T(8,128)S(1)}, f32[32,32,32]{2,1,0:T(8,128)}, f32[32,1024]{1,0:T(8,128)S(1)}, /*index=5*/s32[]{:T(128)}) while((s32[]{:T(128)}, f32[8,32,1024]{2,1,0:T(8,128)S(1)}, f32[8,32,1024]{2,1,0:T(8,128)S(1)}, f32[32,32,32]{2,1,0:T(8,128)}, ...), condition=%wide.wide.region_1.2_spmd, body=%wide.wide.region_0.1_spmd.sunk | while | flops 4204546 | bytes 7487557 | solution.py:80
  65.7 2.6 %convolution_bitcast_fusion.1 = f32[8,8]{1,0:T(8,128)S(1)} fusion(f32[8,32,1024]{2,1,0:T(8,128)S(1)} %get-tuple-element.59), kind=kOutput, calls=%fused_computation.48 | convolution fusion | flops 25165824 | bytes 1048832 | tf_op jit(solution)/shard_map/dot_general | solution.py:87
  75.2 5.2 %collective-permute-start.6 = (f32[4,32,32]{2,1,0:T(8,128)S(1)}, f32[4,32,32]{2,1,0:T(8,128)S(1)}, u32[]{:S(2)}, u32[]{:S(2)}) collective-permute-start(f32[4,32,32]{2,1,0:T(8,128)S(1)} %slice.155), channel_id=1, source_target_pairs={{0,448},{64,0},{128,64},{192,128},{256,192},{320,256},{384,320},{4... | collective-permute-start | bytes 49160 | tf_op jit(solution)/shard_map/ppermute | solution.py:35
  81.8 1.9 collective-permute-start.9
  83.7 5.5 %collective-permute-start.8 = (f32[16,4,32]{2,1,0:T(4,128)S(1)}, f32[16,4,32]{2,1,0:T(4,128)S(1)}, u32[]{:S(2)}, u32[]{:S(2)}) collective-permute-start(f32[16,4,32]{2,1,0:T(4,128)S(1)} %get-tuple-element.91), channel_id=1, source_target_pairs={{0,56},{8,0},{16,8},{24,16},{32,24},{40,32},{48,40},{56,48},{1,57}... | collective-permute-start | bytes 24584 | tf_op jit(solution)/shard_map/ppermute | solution.py:35
  90.3 3.9 %collective-permute-start.11 = (f32[16,16,4]{2,1,0:T(8,128)S(1)}, f32[16,16,4]{2,1,0:T(8,128)S(1)}, u32[]{:S(2)}, u32[]{:S(2)}) collective-permute-start(f32[16,16,4]{2,1,0:T(8,128)S(1)} %get-tuple-element.100), channel_id=1, source_target_pairs={{0,1},{1,2},{2,3},{3,4},{4,5},{5,6},{6,7},{7,0},{8,9},{9,10},{10,1... | collective-permute-start | bytes 12296 | tf_op jit(solution)/shard_map/ppermute | solution.py:35
  96.2 5.2 %collective-permute-done.10 = f32[16,16,4]{2,1,0:T(8,128)S(1)} collective-permute-done((f32[16,16,4]{2,1,0:T(8,128)S(1)}, f32[16,16,4]{2,1,0:T(8,128)S(1)}, u32[]{:S(2)}, u32[]{:S(2)}) %collective-permute-start.10) | collective-permute-done | bytes 4128 | tf_op jit(solution)/shard_map/ppermute | solution.py:35
  102.2 10.4 %all-to-all-start = ((f32[8,1,512]{2,1,0:T(1,128)}), f32[8,1,512]{2,1,0:T(1,128)S(1)}, u32[]{:S(2)}, u32[]{:S(2)}) async-start(f32[8,1,512]{2,1,0:T(1,128)} %reshape.181), calls=%async_computation | async-start | bytes 32768 | tf_op jit(solution)/shard_map/all_to_all | solution.py:205
  112.7 7.0 %all-to-all-done = f32[8,1,512]{2,1,0:T(1,128)S(1)} async-done(((f32[8,1,512]{2,1,0:T(1,128)}), f32[8,1,512]{2,1,0:T(1,128)S(1)}, u32[]{:S(2)}, u32[]{:S(2)}) %all-to-all-start) | async-done | bytes 16416 | tf_op jit(solution)/shard_map/all_to_all | solution.py:205
  123.1 7.0 %all-to-all-start.1 = ((f32[8,1,1024]{2,1,0:T(1,128)}), f32[8,1,1024]{2,1,0:T(1,128)S(1)}, u32[]{:S(2)}, u32[]{:S(2)}) async-start(f32[8,1,1024]{2,1,0:T(1,128)} %reshape.183), calls=%async_computation.1 | async-start | bytes 65536 | tf_op jit(solution)/shard_map/all_to_all | solution.py:46
  130.1 5.0 %all-to-all-done.1 = f32[8,1,1024]{2,1,0:T(1,128)S(1)} async-done(((f32[8,1,1024]{2,1,0:T(1,128)}), f32[8,1,1024]{2,1,0:T(1,128)S(1)}, u32[]{:S(2)}, u32[]{:S(2)}) %all-to-all-start.1) | async-done | bytes 32800 | tf_op jit(solution)/shard_map/all_to_all | solution.py:46
  139.1 8.3 %all-to-all-start.2 = ((f32[64,1,128]{2,1,0:T(1,128)}), f32[64,1,128]{2,1,0:T(1,128)S(1)}, u32[]{:S(2)}, u32[]{:S(2)}) async-start(f32[64,1,128]{2,1,0:T(1,128)} %reshape.185), calls=%async_computation.2 | async-start | bytes 65536 | tf_op jit(solution)/shard_map/all_to_all | solution.py:46
  147.5 11.7 %all-to-all-done.2 = f32[64,1,128]{2,1,0:T(1,128)S(1)} async-done(((f32[64,1,128]{2,1,0:T(1,128)}), f32[64,1,128]{2,1,0:T(1,128)S(1)}, u32[]{:S(2)}, u32[]{:S(2)}) %all-to-all-start.2) | async-done | bytes 32800 | tf_op jit(solution)/shard_map/all_to_all | solution.py:46
  164.4 15.8 %all_to_all.102 = f32[64,1,128]{2,1,0:T(1,128)S(1)} all-to-all(f32[64,1,128]{2,1,0:T(1,128)S(1)} %reshape.187), channel_id=1, replica_groups=mesh['gx'=8,'gy'=8,'gz'=8] {'gx','gz'}, dimensions={0} | all-to-all | bytes 65536 | tf_op jit(solution)/shard_map/all_to_all | solution.py:46
  183.6 7.5 %all_to_all.103 = f32[8,1,1024]{2,1,0:T(1,128)S(1)} all-to-all(f32[8,1,1024]{2,1,0:T(1,128)S(1)} %reshape.189), channel_id=1, replica_groups=mesh['gx'=8,'gy'=8,'gz'=8] {'gy'}, dimensions={0} | all-to-all | bytes 65536 | tf_op jit(solution)/shard_map/all_to_all | solution.py:46
  193.6 11.2 %all_to_all.104 = f32[8,1,512]{2,1,0:T(1,128)S(1)} all-to-all(f32[8,1,512]{2,1,0:T(1,128)S(1)} %reshape.191), channel_id=1, replica_groups=mesh['gx'=8,'gy'=8,'gz'=8] {'gz'}, dimensions={0} | all-to-all | bytes 32768 | tf_op jit(solution)/shard_map/all_to_all | solution.py:219
  206.1 2.1 collective-permute-start.13
  208.2 3.1 %collective-permute-start.12 = (f32[8,16,16]{2,1,0:T(8,128)S(1)}, f32[8,16,16]{2,1,0:T(8,128)S(1)}, u32[]{:S(2)}, u32[]{:S(2)}) collective-permute-start(f32[8,16,16]{2,1,0:T(8,128)S(1)} %get-tuple-element.95), channel_id=1, source_target_pairs={{0,64},{64,128},{128,192},{192,256},{256,320},{320,384},{384,448},... | collective-permute-start | bytes 24584 | tf_op jit(solution)/shard_map/ppermute | solution.py:27
  211.4 3.1 %collective-permute-done.12 = f32[8,16,16]{2,1,0:T(8,128)S(1)} collective-permute-done((f32[8,16,16]{2,1,0:T(8,128)S(1)}, f32[8,16,16]{2,1,0:T(8,128)S(1)}, u32[]{:S(2)}, u32[]{:S(2)}) %collective-permute-start.12) | collective-permute-done | bytes 8224 | tf_op jit(solution)/shard_map/ppermute | solution.py:27
  214.5 2.9 %collective-permute-start.15 = (f32[32,8,16]{2,1,0:T(8,128)S(1)}, f32[32,8,16]{2,1,0:T(8,128)S(1)}, u32[]{:S(2)}, u32[]{:S(2)}) collective-permute-start(f32[32,8,16]{2,1,0:T(8,128)S(1)} %get-tuple-element.86), channel_id=1, source_target_pairs={{8,0},{16,8},{24,16},{32,24},{40,32},{48,40},{56,48},{0,56},{9,1},... | collective-permute-start | bytes 49160 | tf_op jit(solution)/shard_map/ppermute | solution.py:28
  217.4 2.4 collective-permute-start.14
  220.2 5.0 %collective-permute-done.14 = f32[32,8,16]{2,1,0:T(8,128)S(1)} collective-permute-done((f32[32,8,16]{2,1,0:T(8,128)S(1)}, f32[32,8,16]{2,1,0:T(8,128)S(1)}, u32[]{:S(2)}, u32[]{:S(2)}) %collective-permute-start.14) | collective-permute-done | bytes 16416 | tf_op jit(solution)/shard_map/ppermute | solution.py:27
  225.5 5.5 %collective-permute-start.17 = (f32[32,32,8]{2,1,0:T(8,128)S(1)}, f32[32,32,8]{2,1,0:T(8,128)S(1)}, u32[]{:S(2)}, u32[]{:S(2)}) collective-permute-start(f32[32,32,8]{2,1,0:T(8,128)S(1)} %get-tuple-element.82), channel_id=1, source_target_pairs={{1,0},{2,1},{3,2},{4,3},{5,4},{6,5},{7,6},{0,7},{9,8},{10,9},{11,1... | collective-permute-start | bytes 98312 | tf_op jit(solution)/shard_map/ppermute | solution.py:28
  231.0 2.1 collective-permute-start.16
  234.1 9.8 %collective-permute-done.17 = f32[32,32,8]{2,1,0:T(8,128)S(1)} collective-permute-done((f32[32,32,8]{2,1,0:T(8,128)S(1)}, f32[32,32,8]{2,1,0:T(8,128)S(1)}, u32[]{:S(2)}, u32[]{:S(2)}) %collective-permute-start.17) | collective-permute-done | bytes 32800 | tf_op jit(solution)/shard_map/ppermute | solution.py:28
  (179 shorter events, 54.9 us)
Async XLA Ops:
  1.5 13.4 %collective-permute-start = (f32[8,16,16]{2,1,0:T(8,128)S(1)}, f32[8,16,16]{2,1,0:T(8,128)S(1)}, u32[]{:S(2)}, u32[]{:S(2)}) collective-permute-start(f32[8,16,16]{2,1,0:T(8,128)S(1)} %get-tuple-element.104), channel_id=1, source_target_pairs={{0,64},{64,128},{128,192},{192,256},{256,320},{320,384},{384,448},... | collective-permute-start | bytes 24584 | tf_op jit(solution)/shard_map/ppermute | solution.py:27
  6.3 9.9 %collective-permute-start.1 = (f32[8,16,16]{2,1,0:T(8,128)S(1)}, f32[8,16,16]{2,1,0:T(8,128)S(1)}, u32[]{:S(2)}, u32[]{:S(2)}) collective-permute-start(f32[8,16,16]{2,1,0:T(8,128)S(1)} %get-tuple-element.103), channel_id=1, source_target_pairs={{64,0},{128,64},{192,128},{256,192},{320,256},{384,320},{448,384},... | collective-permute-start | bytes 24584 | tf_op jit(solution)/shard_map/ppermute | solution.py:28
  16.3 7.4 %collective-permute-start.3 = (f32[32,8,16]{2,1,0:T(8,128)S(1)}, f32[32,8,16]{2,1,0:T(8,128)S(1)}, u32[]{:S(2)}, u32[]{:S(2)}) collective-permute-start(f32[32,8,16]{2,1,0:T(8,128)S(1)} %get-tuple-element.94), channel_id=1, source_target_pairs={{8,0},{16,8},{24,16},{32,24},{40,32},{48,40},{56,48},{0,56},{9,1},... | collective-permute-start | bytes 49160 | tf_op jit(solution)/shard_map/ppermute | solution.py:28
  21.7 7.8 %collective-permute-start.2 = (f32[32,8,16]{2,1,0:T(8,128)S(1)}, f32[32,8,16]{2,1,0:T(8,128)S(1)}, u32[]{:S(2)}, u32[]{:S(2)}) collective-permute-start(f32[32,8,16]{2,1,0:T(8,128)S(1)} %get-tuple-element.93), channel_id=1, source_target_pairs={{0,8},{8,16},{16,24},{24,32},{32,40},{40,48},{48,56},{56,0},{1,9},... | collective-permute-start | bytes 49160 | tf_op jit(solution)/shard_map/ppermute | solution.py:27
  29.6 10.0 %copy-start.2 = (bf16[8,32,1024]{2,1,0:T(8,128)(2,1)S(1)}, bf16[8,32,1024]{2,1,0:T(8,128)(2,1)}, u32[]{:S(2)}) copy-start(bf16[8,32,1024]{2,1,0:T(8,128)(2,1)} %param.6) | copy-start | bytes 1572868
  30.5 19.7 %collective-permute-start.5 = (f32[32,32,8]{2,1,0:T(8,128)}, f32[32,32,8]{2,1,0:T(8,128)S(1)}, u32[]{:S(2)}, u32[]{:S(2)}) collective-permute-start(f32[32,32,8]{2,1,0:T(8,128)} %get-tuple-element.84), channel_id=1, source_target_pairs={{1,0},{2,1},{3,2},{4,3},{5,4},{6,5},{7,6},{0,7},{9,8},{10,9},{11,1... | collective-permute-start | bytes 98312 | tf_op jit(solution)/shard_map/ppermute | solution.py:28
  35.4 14.8 %collective-permute-start.4 = (f32[32,32,8]{2,1,0:T(8,128)S(1)}, f32[32,32,8]{2,1,0:T(8,128)}, u32[]{:S(2)}, u32[]{:S(2)}) collective-permute-start(f32[32,32,8]{2,1,0:T(8,128)S(1)} %get-tuple-element.83), channel_id=1, source_target_pairs={{0,1},{1,2},{2,3},{3,4},{4,5},{5,6},{6,7},{7,0},{8,9},{9,10},{10,1... | collective-permute-start | bytes 98312 | tf_op jit(solution)/shard_map/ppermute | solution.py:27
  51.6 1.7 copy-start
  65.7 5.5 %copy-start.4 = (f32[8]{0:T(128)S(1)}, f32[8]{0:T(128)}, u32[]{:S(2)}) copy-start(f32[8]{0:T(128)} %param.9) | copy-start | bytes 100
  73.2 7.3 %collective-permute-start.7 = (f32[4,32,32]{2,1,0:T(8,128)S(1)}, f32[4,32,32]{2,1,0:T(8,128)S(1)}, u32[]{:S(2)}, u32[]{:S(2)}) collective-permute-start(f32[4,32,32]{2,1,0:T(8,128)S(1)} %slice.157), channel_id=1, source_target_pairs={{0,64},{64,128},{128,192},{192,256},{256,320},{320,384},{384,448},... | collective-permute-start | bytes 49160 | tf_op jit(solution)/shard_map/ppermute | solution.py:35
  75.2 6.5 %collective-permute-start.6 = (f32[4,32,32]{2,1,0:T(8,128)S(1)}, f32[4,32,32]{2,1,0:T(8,128)S(1)}, u32[]{:S(2)}, u32[]{:S(2)}) collective-permute-start(f32[4,32,32]{2,1,0:T(8,128)S(1)} %slice.155), channel_id=1, source_target_pairs={{0,448},{64,0},{128,64},{192,128},{256,192},{320,256},{384,320},{4... | collective-permute-start | bytes 49160 | tf_op jit(solution)/shard_map/ppermute | solution.py:35
  81.8 7.4 %collective-permute-start.9 = (f32[16,4,32]{2,1,0:T(4,128)S(1)}, f32[16,4,32]{2,1,0:T(4,128)S(1)}, u32[]{:S(2)}, u32[]{:S(2)}) collective-permute-start(f32[16,4,32]{2,1,0:T(4,128)S(1)} %get-tuple-element.92), channel_id=1, source_target_pairs={{0,8},{8,16},{16,24},{24,32},{32,40},{40,48},{48,56},{56,0},{1,9},... | collective-permute-start | bytes 24584 | tf_op jit(solution)/shard_map/ppermute | solution.py:35
  83.7 6.5 %collective-permute-start.8 = (f32[16,4,32]{2,1,0:T(4,128)S(1)}, f32[16,4,32]{2,1,0:T(4,128)S(1)}, u32[]{:S(2)}, u32[]{:S(2)}) collective-permute-start(f32[16,4,32]{2,1,0:T(4,128)S(1)} %get-tuple-element.91), channel_id=1, source_target_pairs={{0,56},{8,0},{16,8},{24,16},{32,24},{40,32},{48,40},{56,48},{1,57}... | collective-permute-start | bytes 24584 | tf_op jit(solution)/shard_map/ppermute | solution.py:35
  90.3 5.8 %collective-permute-start.11 = (f32[16,16,4]{2,1,0:T(8,128)S(1)}, f32[16,16,4]{2,1,0:T(8,128)S(1)}, u32[]{:S(2)}, u32[]{:S(2)}) collective-permute-start(f32[16,16,4]{2,1,0:T(8,128)S(1)} %get-tuple-element.100), channel_id=1, source_target_pairs={{0,1},{1,2},{2,3},{3,4},{4,5},{5,6},{6,7},{7,0},{8,9},{9,10},{10,1... | collective-permute-start | bytes 12296 | tf_op jit(solution)/shard_map/ppermute | solution.py:35
  94.2 7.2 %collective-permute-start.10 = (f32[16,16,4]{2,1,0:T(8,128)S(1)}, f32[16,16,4]{2,1,0:T(8,128)S(1)}, u32[]{:S(2)}, u32[]{:S(2)}) collective-permute-start(f32[16,16,4]{2,1,0:T(8,128)S(1)} %get-tuple-element.99), channel_id=1, source_target_pairs={{0,7},{1,0},{2,1},{3,2},{4,3},{5,4},{6,5},{7,6},{8,15},{9,8},{10,9... | collective-permute-start | bytes 12296 | tf_op jit(solution)/shard_map/ppermute | solution.py:35
  101.5 104.3 %copy-start.1 = (f32[16,16,16]{2,1,0:T(8,128)}, f32[16,16,16]{2,1,0:T(8,128)S(1)}, u32[]{:S(2)}) copy-start(f32[16,16,16]{2,1,0:T(8,128)S(1)} %fusion.40) | copy-start | bytes 49156
  102.2 17.5 %all-to-all-start = ((f32[8,1,512]{2,1,0:T(1,128)}), f32[8,1,512]{2,1,0:T(1,128)S(1)}, u32[]{:S(2)}, u32[]{:S(2)}) async-start(f32[8,1,512]{2,1,0:T(1,128)} %reshape.181), calls=%async_computation | async-start | bytes 32768 | tf_op jit(solution)/shard_map/all_to_all | solution.py:205
  123.1 12.1 %all-to-all-start.1 = ((f32[8,1,1024]{2,1,0:T(1,128)}), f32[8,1,1024]{2,1,0:T(1,128)S(1)}, u32[]{:S(2)}, u32[]{:S(2)}) async-start(f32[8,1,1024]{2,1,0:T(1,128)} %reshape.183), calls=%async_computation.1 | async-start | bytes 65536 | tf_op jit(solution)/shard_map/all_to_all | solution.py:46
  139.1 20.1 %all-to-all-start.2 = ((f32[64,1,128]{2,1,0:T(1,128)}), f32[64,1,128]{2,1,0:T(1,128)S(1)}, u32[]{:S(2)}, u32[]{:S(2)}) async-start(f32[64,1,128]{2,1,0:T(1,128)} %reshape.185), calls=%async_computation.2 | async-start | bytes 65536 | tf_op jit(solution)/shard_map/all_to_all | solution.py:46
  192.2 13.7 %copy-start.3 = (f32[16,16,16]{2,1,0:T(8,128)S(1)}, f32[16,16,16]{2,1,0:T(8,128)}, u32[]{:S(2)}) copy-start(f32[16,16,16]{2,1,0:T(8,128)} %param.8) | copy-start | bytes 49156
  206.1 5.3 %collective-permute-start.13 = (f32[8,16,16]{2,1,0:T(8,128)S(1)}, f32[8,16,16]{2,1,0:T(8,128)S(1)}, u32[]{:S(2)}, u32[]{:S(2)}) collective-permute-start(f32[8,16,16]{2,1,0:T(8,128)S(1)} %get-tuple-element.96), channel_id=1, source_target_pairs={{64,0},{128,64},{192,128},{256,192},{320,256},{384,320},{448,384},... | collective-permute-start | bytes 24584 | tf_op jit(solution)/shard_map/ppermute | solution.py:28
  208.2 6.2 %collective-permute-start.12 = (f32[8,16,16]{2,1,0:T(8,128)S(1)}, f32[8,16,16]{2,1,0:T(8,128)S(1)}, u32[]{:S(2)}, u32[]{:S(2)}) collective-permute-start(f32[8,16,16]{2,1,0:T(8,128)S(1)} %get-tuple-element.95), channel_id=1, source_target_pairs={{0,64},{64,128},{128,192},{192,256},{256,320},{320,384},{384,448},... | collective-permute-start | bytes 24584 | tf_op jit(solution)/shard_map/ppermute | solution.py:27
  214.5 5.7 %collective-permute-start.15 = (f32[32,8,16]{2,1,0:T(8,128)S(1)}, f32[32,8,16]{2,1,0:T(8,128)S(1)}, u32[]{:S(2)}, u32[]{:S(2)}) collective-permute-start(f32[32,8,16]{2,1,0:T(8,128)S(1)} %get-tuple-element.86), channel_id=1, source_target_pairs={{8,0},{16,8},{24,16},{32,24},{40,32},{48,40},{56,48},{0,56},{9,1},... | collective-permute-start | bytes 49160 | tf_op jit(solution)/shard_map/ppermute | solution.py:28
  217.4 7.8 %collective-permute-start.14 = (f32[32,8,16]{2,1,0:T(8,128)S(1)}, f32[32,8,16]{2,1,0:T(8,128)S(1)}, u32[]{:S(2)}, u32[]{:S(2)}) collective-permute-start(f32[32,8,16]{2,1,0:T(8,128)S(1)} %get-tuple-element.85), channel_id=1, source_target_pairs={{0,8},{8,16},{16,24},{24,32},{32,40},{40,48},{48,56},{56,0},{1,9},... | collective-permute-start | bytes 49160 | tf_op jit(solution)/shard_map/ppermute | solution.py:27
  225.5 18.4 %collective-permute-start.17 = (f32[32,32,8]{2,1,0:T(8,128)S(1)}, f32[32,32,8]{2,1,0:T(8,128)S(1)}, u32[]{:S(2)}, u32[]{:S(2)}) collective-permute-start(f32[32,32,8]{2,1,0:T(8,128)S(1)} %get-tuple-element.82), channel_id=1, source_target_pairs={{1,0},{2,1},{3,2},{4,3},{5,4},{6,5},{7,6},{0,7},{9,8},{10,9},{11,1... | collective-permute-start | bytes 98312 | tf_op jit(solution)/shard_map/ppermute | solution.py:28
  231.0 12.9 %collective-permute-start.16 = (f32[32,32,8]{2,1,0:T(8,128)S(1)}, f32[32,32,8]{2,1,0:T(8,128)S(1)}, u32[]{:S(2)}, u32[]{:S(2)}) collective-permute-start(f32[32,32,8]{2,1,0:T(8,128)S(1)} %get-tuple-element.81), channel_id=1, source_target_pairs={{0,1},{1,2},{2,3},{3,4},{4,5},{5,6},{6,7},{7,0},{8,9},{9,10},{10,1... | collective-permute-start | bytes 98312 | tf_op jit(solution)/shard_map/ppermute | solution.py:27
where the time goes:
time: 249 us; the launch traced here: 245 us
  starting transfers between devices  93.9 us (38%)
  waiting for transfers between devices  66 us (27%)
  blocking collectives  34.5 us (14%)
  other arithmetic  21.4 us (9%)
  local copies, waits for them, and re-layouts  14.2 us (6%)
  matrix products  13.2 us (5%)
    ppermute x6, starting transfers between devices, padded_2(): after = lax.ppermute(first, axis, down)  29.4 us
    all_to_all x2, blocking collectives, in_one_piece(): lax.all_to_all(both, axis, split_axis=split_dim, concat_axis=concat_dim,...  23.3 us
    ppermute x6, waiting for transfers between devices, padded_2(): after = lax.ppermute(first, axis, down)  21 us
    ppermute x6, starting transfers between devices, shifted(): return lax.ppermute(x, axis, [(i, (i + by) % count) for i in range(count)])  20.3 us
    ppermute x6, starting transfers between devices, padded_2(): before = lax.ppermute(last, axis, up)  18.4 us
    all_to_all x2, waiting for transfers between devices, in_one_piece(): lax.all_to_all(both, axis, split_axis=split_dim, concat_axis=concat_dim,...  16.7 us
    all_to_all x2, starting transfers between devices, in_one_piece(): lax.all_to_all(both, axis, split_axis=split_dim, concat_axis=concat_dim,...  15.3 us
    ppermute x6, waiting for transfers between devices, padded_2(): before = lax.ppermute(last, axis, up)  13.9 us
  transfers between devices with their start and end apart: 21, of which 13 were waited for; matrix products, arithmetic and copies ran while one was open for 1% of the time, Pallas kernels for 0%

commit v1 on v0

v1 whole, which is shorter than its diff:
```python
import functools
import math

import jax
import jax.numpy as jnp
import numpy as np
from jax import lax
from jax.experimental import pallas as pl
from jax.experimental.pallas import tpu as pltpu
from jax.sharding import PartitionSpec as P

BUF = 8
DEGREE = 10
N = 128
CORE = 16
LX = 32
NORB = 8
PARTS = 8
FIRST, LAST = 4, 28
KEPT = LAST - FIRST
LANES = 128
PER = LANES // LX

spacing = 0.2
kinetic = 0.5 / (spacing * spacing)
filter_low = 6.0
filter_high = 12.0 * kinetic
centre_value = 0.5 * (filter_low + filter_high)
half_width = 0.5 * (filter_high - filter_low)

F32, BF16 = jnp.float32, jnp.bfloat16
VMEM = pl.BlockSpec(memory_space=pltpu.VMEM)
SMEM = pl.BlockSpec(memory_space=pltpu.SMEM)
INTERPRET = False


def call(kernel, out_shape, in_specs, scratch=(), flops=1000000, name=None):
    many = isinstance(out_shape, (tuple, list))
    return pl.pallas_call(
        kernel,
        out_shape=out_shape,
        in_specs=in_specs,
        out_specs=tuple(VMEM for _ in out_shape) if many else VMEM,
        scratch_shapes=scratch,
        compiler_params=pltpu.CompilerParams(vmem_limit_bytes=40 * 1024 * 1024),
        cost_estimate=pl.CostEstimate(flops=flops, bytes_accessed=1000000, transcendentals=0),
        interpret=INTERPRET,
        name=name,
    )


def _basis():
    n = np.arange(N, dtype=np.float64)
    angle = 2.0 * np.pi * np.mod(np.outer(n, n), N) / N
    return (np.cos(angle) + np.sin(angle)) / math.sqrt(N)


def _pair(table):
    high = np.asarray(table, np.float32).astype(jnp.bfloat16)
    low = (np.asarray(table, np.float64) - high.astype(np.float64)).astype(jnp.bfloat16)
    return high, low


def _cell(part, a):
    return np.mod(CORE * part + a - BUF, N)


def _tables():
    basis = _basis()
    parts = np.arange(PARTS)
    along = np.zeros((PARTS, CORE + LX, PARTS * KEPT))
    for i in range(PARTS):
        for other in range(PARTS):
            for xx in range(KEPT):
                column = other * KEPT + xx
                cell = _cell(other, xx + FIRST)
                along[i, :CORE, column] = basis[CORE * i : CORE * (i + 1), cell]
                for a in range(LX):
                    if _cell(i, a) == cell and min((other - i) % PARTS, (i - other) % PARTS) <= 1:
                        along[i, CORE + a, column] = 1.0
    lane = np.arange(PARTS * LANES)
    z_cell = _cell(lane // LANES, lane % LX)
    z_table = basis[z_cell, :]
    y_lo, y_hi, j = np.meshgrid(np.arange(PER), np.arange(KEPT // PER), parts, indexing="ij")
    y_table = basis[:, _cell(j, FIRST + PER * y_hi + y_lo).reshape(-1)]
    back = np.zeros((4, 64, N))
    for q in range(4):
        y_lo, y_half, j = np.meshgrid(np.arange(PER), np.arange(2), parts, indexing="ij")
        back[q] = basis[_cell(j, 8 * q + PER * y_half + y_lo).reshape(-1), :]
    last = np.stack([basis[_cell(i, np.arange(LX)), :] for i in range(PARTS)])
    wave = 4.0 / (spacing * spacing) * np.sin(np.pi * np.arange(N) / N) ** 2
    return dict(
        along=_pair(along),
        z_table=_pair(z_table),
        z_back=_pair(z_table.T),
        y_table=_pair(y_table),
        y_back=_pair(back),
        last=_pair(last),
        wave=wave.astype(np.float32),
        wave_yz=(wave[:, None] + wave[None, :]).astype(np.float32),
    )


def _weight():
    position = np.arange(LX, dtype=np.float32)
    rising = np.clip((position + 0.5 - 0.5 * BUF) / BUF, 0.0, 1.0)
    falling = np.clip((LX - 0.5 * BUF - 0.5 - position) / BUF, 0.0, 1.0)
    profile = (rising * falling).astype(np.float32)
    return profile[:, None] * (profile[:, None] * profile[None, :]).reshape(1, LX * LX)


TABLES = _tables()
WEIGHT = _weight().astype(np.float32)


def halves(value):
    high = value.astype(BF16)
    return high, (value - high.astype(F32)).astype(BF16)


def dot3(left, right):
    def one(a, b):
        return jnp.dot(a, b, preferred_element_type=F32)

    return one(left[0], right[0]) + (one(left[0], right[1]) + one(left[1], right[0]))


def iota(shape, dim):
    return lax.broadcasted_iota(jnp.int32, shape, dim)


def filter_kernel(occ_ref, orb_ref, pot_ref, weight_ref, new_ref, send_ref, ya, yb, coef, dens):
    tiles, chunks = LX // 8, LX * LX // LANES
    lane = iota((8, LANES), 1)
    row = iota((8, LANES), 0)
    low_z, high_z = lane % LX == 0, lane % LX == LX - 1
    first_y, last_y = lane < LX, lane >= LANES - LX
    first_x, last_x = row == 0, row == 7
    zero = jnp.zeros((8, LANES), F32)

    coef[...] = (2.0 / half_width) * pot_ref[...] + (2.0 / half_width) * (
        6.0 * kinetic - centre_value
    )
    alpha = -2.0 * kinetic / half_width

    def fill(n, carry):
        for buffer in (ya, yb):
            buffer[n, 0:8, :] = jnp.zeros((8, (chunks + 2) * LANES), F32)
            buffer[n, 8 + LX : 16 + LX, :] = jnp.zeros((8, (chunks + 2) * LANES), F32)
            buffer[n, :, 0:LANES] = jnp.zeros((16 + LX, LANES), F32)
            buffer[n, :, (chunks + 1) * LANES :] = jnp.zeros((16 + LX, LANES), F32)
        ya[n, 8 : 8 + LX, LANES : (chunks + 1) * LANES] = orb_ref[n].astype(F32)
        return carry

    lax.fori_loop(0, NORB, fill, 0)

    def advance(src, dst, start):
        def one(n, carry):
            for c in range(chunks):
                here = slice((c + 1) * LANES, (c + 2) * LANES)
                for t in range(tiles):
                    rows = slice(8 + 8 * t, 16 + 8 * t)
                    cur = src[n, rows, here]
                    above = src[n, 8 * t : 8 + 8 * t, here]
                    below = src[n, 16 + 8 * t : 24 + 8 * t, here]
                    before = src[n, rows, c * LANES : (c + 1) * LANES]
                    after = src[n, rows, (c + 2) * LANES : (c + 3) * LANES]
                    total = pltpu.roll(jnp.where(last_x, above, cur), 1, 0)
                    total += pltpu.roll(jnp.where(first_x, below, cur), 7, 0)
                    total += pltpu.roll(jnp.where(last_y, before, cur), LX, 1)
                    total += pltpu.roll(jnp.where(first_y, after, cur), LANES - LX, 1)
                    total += jnp.where(low_z, zero, pltpu.roll(cur, 1, 1))
                    total += jnp.where(high_z, zero, pltpu.roll(cur, LANES - 1, 1))
                    w = coef[8 * t : 8 + 8 * t, c * LANES : (c + 1) * LANES]
                    result = alpha * total + w * cur
                    if start:
                        dst[n, rows, here] = 0.5 * result
                    else:
                        dst[n, rows, here] = result - dst[n, rows, here]
            return carry

        lax.fori_loop(0, NORB, one, 0)

    advance(ya, yb, True)

    def two(m, carry):
        advance(yb, ya, False)
        advance(ya, yb, False)
        return carry

    lax.fori_loop(0, (DEGREE - 2) // 2, two, 0)
    advance(yb, ya, False)

    pairs = [(n, m) for n in range(NORB) for m in range(n + 1)]

    def gather(t, sums):
        sums = list(sums)
        start = pl.multiple_of(8 + 8 * t, 8)
        for c in range(chunks):
            f = [ya[n, pl.ds(start, 8), (c + 1) * LANES : (c + 2) * LANES] for n in range(NORB)]
            for at, (n, m) in enumerate(pairs):
                sums[at] = sums[at] + f[n] * f[m]
        return tuple(sums)

    sums = lax.fori_loop(0, tiles, gather, tuple(zero for _ in pairs))
    gram = {
        pair: jnp.sum(jnp.sum(s, axis=0, keepdims=True), axis=1, keepdims=True) / float(LX**3)
        for pair, s in zip(pairs, sums)
    }
    factor, inverse, recip = {}, {}, {}
    for j in range(NORB):
        rest = gram[j, j]
        for k in range(j):
            rest = rest - factor[j, k] * factor[j, k]
        recip[j] = 1.0 / jnp.sqrt(rest)
        for n in range(j + 1, NORB):
            value = gram[n, j]
            for k in range(j):
                value = value - factor[n, k] * factor[j, k]
            factor[n, j] = value * recip[j]
    for j in range(NORB):
        inverse[j, j] = recip[j]
        for n in range(j + 1, NORB):
            value = factor[n, j] * inverse[j, j]
            for k in range(j + 1, n):
                value = value + factor[n, k] * inverse[k, j]
            inverse[n, j] = -recip[n] * value
    wide = {pair: jnp.broadcast_to(inverse[pair], (8, LANES)) for pair in pairs}

    def normal(t, carry):
        start = pl.multiple_of(8 + 8 * t, 8)
        rows = pl.ds(pl.multiple_of(8 * t, 8), 8)
        for c in range(chunks):
            here = slice((c + 1) * LANES, (c + 2) * LANES)
            f = [ya[n, pl.ds(start, 8), here] for n in range(NORB)]
            total = zero
            for n in range(NORB):
                value = wide[n, 0] * f[0]
                for m in range(1, n + 1):
                    value = value + wide[n, m] * f[m]
                yb[n, pl.ds(start, 8), here] = value
                total = total + occ_ref[n] * (value * value)
            there = slice(c * LANES, (c + 1) * LANES)
            dens[rows, there] = total * weight_ref[rows, there]
        return carry

    lax.fori_loop(0, tiles, normal, 0)

    def finish(n, carry):
        new_ref[n] = yb[n, 8 : 8 + LX, LANES : (chunks + 1) * LANES].astype(BF16)
        return carry

    lax.fori_loop(0, NORB, finish, 0)

    kept = KEPT // PER
    for c in range(kept):
        value = dens[FIRST:LAST, (c + 1) * LANES : (c + 2) * LANES]
        for s in range(PARTS):
            send_ref[pl.ds(s * KEPT * kept + c, KEPT, stride=kept), :] = value


def filtered_set(occupations, orbitals, potential_ext):
    wide = LX * LX + 2 * LANES
    return call(
        filter_kernel,
        (
            jax.ShapeDtypeStruct((NORB, LX, LX * LX), BF16),
            jax.ShapeDtypeStruct((PARTS * KEPT * KEPT // PER, LANES), F32),
        ),
        [SMEM, VMEM, VMEM, VMEM],
        [
            pltpu.VMEM((NORB, LX + 16, wide), F32),
            pltpu.VMEM((NORB, LX + 16, wide), F32),
            pltpu.VMEM((LX, LX * LX), F32),
            pltpu.VMEM((LX, LX * LX), F32),
        ],
        flops=60000000,
        name="filter",
    )(occupations, orbitals, potential_ext, jnp.asarray(WEIGHT))


def x_kernel(place_ref, got_ref, high_ref, low_ref, send_ref):
    kept = KEPT // PER
    at = place_ref[0]
    table = (high_ref[at], low_ref[at])
    for c in range(kept):
        lines = got_ref[pl.ds(c, PARTS * KEPT, stride=kept), :]
        value = dot3(table, halves(lines))
        for q in range(2):
            send_ref[pl.ds(q * 2 * kept + c, LX, stride=4 * kept), :] = value[CORE:]
        for q in range(4):
            send_ref[pl.ds(q * 2 * kept + kept + c, CORE, stride=8 * kept), :] = value[:CORE]


def along_x(place, got):
    return call(
        x_kernel,
        jax.ShapeDtypeStruct((64 * 2 * KEPT // PER, LANES), F32),
        [SMEM, VMEM, VMEM, VMEM],
        name="along_x",
    )(place, got, *map(jnp.asarray, TABLES["along"]))


def plane_kernel(
    place_ref,
    lx_ref,
    got_ref,
    zh_ref,
    zl_ref,
    yh_ref,
    yl_ref,
    wave_ref,
    bh_ref,
    bl_ref,
    th_ref,
    tl_ref,
    send_ref,
    work,
):
    kept = KEPT // PER
    chunk = 2 * kept
    out_chunk = 6
    wide = PARTS * LANES
    blocks = []
    for k in range(PARTS):
        rows = [
            got_ref[pl.ds(chunk * k + kept + c, PARTS, stride=chunk * PARTS), :]
            for c in range(kept)
        ]
        blocks.append(jnp.concatenate(rows, axis=0))
    lines = jnp.concatenate(blocks, axis=1)
    which = (iota(lines.shape, 1) % LANES) // LX
    spread = jnp.concatenate([jnp.where(which == y, lines, 0.0) for y in range(PER)], axis=0)
    along_z = dot3(halves(spread), (zh_ref[...], zl_ref[...]))
    spectrum = dot3((yh_ref[...], yl_ref[...]), halves(along_z))
    eigen = wave_ref[...] + lx_ref[0]
    positive = eigen > 0.0
    green = jnp.where(positive, 4.0 * math.pi / jnp.where(positive, eigen, 1.0), 0.0)
    spectrum = spectrum * green
    quarter = place_ref[1]
    lines = dot3((bh_ref[quarter], bl_ref[quarter]), halves(spectrum))
    spread = dot3(halves(lines), (th_ref[...], tl_ref[...]))
    which = (iota((16, wide), 1) % LANES) // LX
    packed = jnp.zeros((16, wide), F32)
    for y in range(PER):
        packed = jnp.where(which == y, spread[16 * y : 16 * (y + 1)], packed)
    for k in range(PARTS):
        for half in range(2):
            send_ref[pl.ds(out_chunk * k + half, PARTS, stride=out_chunk * PARTS), :] = packed[
                8 * half : 8 * half + 8, k * LANES : (k + 1) * LANES
            ]
    row = iota((8, LANES), 0)
    lane = iota((8, LANES), 1) % LX
    inside = (row >= 1) & (row <= kept)
    upper = row < 4
    left = lane < LX // 2
    second = place_ref[2] == 1

    def load(j, k):
        at = chunk * (PARTS * j + k)
        return jnp.where(inside, pltpu.roll(got_ref[at : at + 8, :], 1, 0), 0.0)

    for k in range(PARTS):
        column = [load(j, k) for j in range(PARTS)]
        for j in range(PARTS):
            beside = jnp.where(upper, column[(j + 1) % PARTS], column[(j - 1) % PARTS])
            at = 8 * (PARTS * j + k)
            work[at : at + 8, :] = column[j] + pltpu.roll(beside, 4, 0)
    for j in range(PARTS):
        line = [work[8 * (PARTS * j + k) : 8 * (PARTS * j + k) + 8, :] for k in range(PARTS)]
        for k in range(PARTS):
            beside = jnp.where(left, line[(k + 1) % PARTS], line[(k - 1) % PARTS])
            half = LX // 2
            value = line[k] + jnp.where(
                left, pltpu.roll(beside, LANES - half, 1), pltpu.roll(beside, half, 1)
            )
            value = jnp.where(second, pltpu.roll(value, 4, 0), value)
            at = out_chunk * (PARTS * j + k) + 2
            send_ref[at : at + 4, :] = value[0:4]


def on_plane(place, lx, got):
    t = TABLES
    return call(
        plane_kernel,
        jax.ShapeDtypeStruct((64 * 6, LANES), F32),
        [SMEM, SMEM] + [VMEM] * 10,
        [pltpu.VMEM((64 * 8, LANES), F32)],
        name="on_plane",
    )(
        place,
        lx,
        got,
        *map(jnp.asarray, t["z_table"]),
        *map(jnp.asarray, t["y_table"]),
        jnp.asarray(t["wave_yz"]),
        *map(jnp.asarray, t["y_back"]),
        *map(jnp.asarray, t["z_back"]),
    )


def cube_root(value):
    safe = jnp.maximum(value, 1e-30)
    root = jnp.exp(jnp.log(safe) * (1.0 / 3.0))
    root = root - (root - safe / (root * root)) * (1.0 / 3.0)
    return jnp.where(value > 0.0, root, 0.0)


def exchange_correlation(density):
    root = cube_root(density)
    slater = -((3.0 / math.pi) ** (1.0 / 3.0)) * root
    radius = (3.0 / (4.0 * math.pi)) ** (1.0 / 3.0)
    bottom = radius + 7.8 * root
    wigner = -0.44 * root / bottom * (1.0 + radius / (3.0 * bottom))
    return slater + wigner


def window_kernel(got_ref, ion_ref, send_ref, dens_ref, base_ref):
    for half in range(2):
        value = got_ref[pl.ds(half, 64, stride=6), :]
        for s in range(PARTS):
            send_ref[pl.ds(s * LANES + half, 64, stride=2), :] = value
    for q in range(2):
        for y in range(4):
            here = slice((4 * q + y) * LANES, (4 * q + y + 1) * LANES)
            value = got_ref[pl.ds(6 * q + 2 + y, LX, stride=12), :]
            dens_ref[:, here] = value
            base_ref[:, here] = ion_ref[:, here] + exchange_correlation(value)


def on_window(got, ion_ext):
    return call(
        window_kernel,
        (
            jax.ShapeDtypeStruct((PARTS * LANES, LANES), F32),
            jax.ShapeDtypeStruct((LX, LX * LX), F32),
            jax.ShapeDtypeStruct((LX, LX * LX), F32),
        ),
        [VMEM, VMEM],
        name="on_window",
    )(got, ion_ext)


def last_kernel(place_ref, got_ref, base_ref, high_ref, low_ref, out_ref):
    at = place_ref[0]
    table = (high_ref[at], low_ref[at])
    for y in range(8):
        here = slice(y * LANES, (y + 1) * LANES)
        lines = got_ref[pl.ds(y, N, stride=8), :]
        out_ref[:, here] = base_ref[:, here] + dot3(table, halves(lines))


def last_step(place, got, base):
    return call(
        last_kernel,
        jax.ShapeDtypeStruct((LX, LX * LX), F32),
        [SMEM, VMEM, VMEM, VMEM, VMEM],
        name="last_step",
    )(place, got, base, *map(jnp.asarray, TABLES["last"]))


def both_sides(first, last, axis):
    count = lax.axis_size(axis)
    up = [(i, (i + 1) % count) for i in range(count)]
    down = [(j, i) for i, j in up]
    return lax.ppermute(last, axis, up), lax.ppermute(first, axis, down)


def refill(fields):
    both = jnp.stack(fields)
    count = both.shape[0] * CORE
    slab = (count, CORE * BUF)
    before, after = both_sides(
        both[..., :BUF].reshape(slab), both[..., CORE - BUF :].reshape(slab), "gz"
    )
    shape = (len(fields), CORE, CORE, BUF)
    both = jnp.concatenate([before.reshape(shape), both, after.reshape(shape)], axis=3)
    both = both.reshape(count, CORE * LX)
    width = BUF * LX
    before, after = both_sides(both[:, :width], both[:, CORE * LX - width :], "gy")
    both = jnp.concatenate([before, both, after], axis=1).reshape(len(fields), CORE, LX * LX)
    before, after = both_sides(both[:, :BUF], both[:, CORE - BUF :], "gx")
    return jnp.concatenate([before, both, after], axis=1)


def exchange(value, axis, rows):
    parts = value.shape[0] // rows
    tile = math.gcd(rows, 8)
    shaped = value.reshape(value.shape[0] // tile, tile, LANES)
    return lax.all_to_all(shaped, axis, split_axis=0, concat_axis=0, tiled=True).reshape(
        value.shape
    )


def on_device(orbitals, potential, ion_potential, occupations):
    gx, member = lax.axis_index("gx"), lax.axis_index(("gy", "gz"))
    place = jnp.stack([gx, member % 4, member % 2]).astype(jnp.int32)
    lx = jnp.asarray(TABLES["wave"])[gx * CORE + member // 4].reshape(1)
    window = refill((potential, ion_potential))
    new_orbitals, send = filtered_set(occupations, orbitals, window[0])
    got = exchange(send, "gx", KEPT * KEPT // PER)
    send = along_x(place, got)
    got = exchange(send, ("gy", "gz"), 2 * KEPT // PER)
    send = on_plane(place, lx, got)
    got = exchange(send, ("gy", "gz"), 6)
    send, dens, base = on_window(got, window[1])
    density = dens[BUF : BUF + CORE].reshape(CORE, LX, LX)[
        :, BUF : BUF + CORE, BUF : BUF + CORE
    ]
    got = exchange(send, "gx", LANES)
    new_potential = last_step(place, got, base)
    return (new_orbitals, density, new_potential)


def solution(mesh):
    placed = (P(None, "gx", ("gy", "gz")), P("gx", "gy", "gz"), P("gx", "gy", "gz"), P())
    return jax.shard_map(
        on_device,
        mesh=mesh,
        in_specs=placed,
        out_specs=(P(None, "gx", ("gy", "gz")), P("gx", "gy", "gz"), P("gx", ("gy", "gz"))),
        check_vma=False,
    )
```

time: 249 us -> 151 us (0.61)
  starting transfers between devices: 93.9 us -> 54.2 us
  Pallas kernels: 0 us -> 26 us
  waiting for transfers between devices: 66 us -> 45 us
  other arithmetic: 21.4 us -> 1.53 us
  blocking collectives: 34.5 us -> 16.4 us
  matrix products: 13.2 us -> 0 us
  local copies, waits for them, and re-layouts: 14.2 us -> 5.22 us
    ppermute x18 -> x6, starting transfers between devices: 68.1 us -> 28.5 us  [both_sides(): return (lax.ppermute(last, axis, up), lax.ppermute(first, axis, down))]
    ppermute x18 -> x6, waiting for transfers between devices: 42.3 us -> 3.15 us  [both_sides(): return (lax.ppermute(last, axis, up), lax.ppermute(first, axis, down))]
    pallas_call x0 -> x5, Pallas kernels: none -> 26 us  [the longest x1 19.5 us: filtered_set(): call(filter_kernel, (jax.ShapeDtypeStruct((NORB, LX, LX * LX), BF16), jax...]
    all_to_all x3, waiting for transfers between devices: 23.7 us -> 41.9 us  [exchange(): lax.all_to_all(shaped, axis, split_axis=0, concat_axis=0, tiled=True)]
    all_to_all x3 -> x1, blocking collectives: 34.5 us -> 16.4 us  [exchange(): lax.all_to_all(shaped, axis, split_axis=0, concat_axis=0, tiled=True)]
    sub x10 -> x0, other arithmetic: 10.4 us -> none  [the longest x9 10.4 us: advance(): 2.0 * (hamiltonian(current, potential_ext, edge_len) - centre_value * cur...]
    dot_general x14 -> x0, matrix products: 9.63 us -> none  [the longest x12 5.29 us: contract(): jnp.tensordot(values, matrix, axes=((axis_dim,), (0,)), precision=lax.Pre...]
    all_to_all x6 -> x0, other arithmetic: 4.24 us -> none  [the longest x4 2.88 us: in_one_piece(): lax.all_to_all(both, axis, split_axis=split_dim, concat_axis=concat_dim,...]
  transfers between devices with their start and end apart: 21 -> 9, of which waited for: 13 -> 6; matrix products, arithmetic and copies ran while one was open for 1% -> 1% of each run, Pallas kernels for 0% -> 0%
where the time goes in v1:
time: 151 us; the launch traced here: 149 us
  starting transfers between devices  54.2 us (36%)
  waiting for transfers between devices  45 us (30%)
  Pallas kernels  26 us (17%)
  blocking collectives  16.4 us (11%)
  local copies, waits for them, and re-layouts  5.22 us (3%)
  other arithmetic  1.53 us (1%)
    all_to_all x3, waiting for transfers between devices, exchange(): lax.all_to_all(shaped, axis, split_axis=0, concat_axis=0, tiled=True)  41.9 us
    ppermute x6, starting transfers between devices, both_sides(): return (lax.ppermute(last, axis, up), lax.ppermute(first, axis, down))  28.5 us
    all_to_all x3, starting transfers between devices, exchange(): lax.all_to_all(shaped, axis, split_axis=0, concat_axis=0, tiled=True)  25.7 us
    pallas_call x1, Pallas kernels, filtered_set(): call(filter_kernel, (jax.ShapeDtypeStruct((NORB, LX, LX * LX), BF16), jax...  19.5 us
    all_to_all x1, blocking collectives, exchange(): lax.all_to_all(shaped, axis, split_axis=0, concat_axis=0, tiled=True)  16.4 us
    ppermute x6, waiting for transfers between devices, both_sides(): return (lax.ppermute(last, axis, up), lax.ppermute(first, axis, down))  3.15 us
  transfers between devices with their start and end apart: 9, of which 6 were waited for; matrix products, arithmetic and copies ran while one was open for 1% of the time, Pallas kernels for 0%

profile of v1, /device:TPU:1, one launch (start us, length us, event | category | flops | bytes accessed | tf_op | source)
XLA Modules:
  0.0 149.4 jit_solution(2182611334409337909)
XLA Ops:
  0.6 1.2 slice_maximum_fusion
  1.9 0.1 reshape.68
  2.1 8.7 %collective-permute-start.1 = (f32[32,128]{0,1:T(8,128)S(1)}, f32[32,128]{0,1:T(8,128)S(1)}, u32[]{:S(2)}, u32[]{:S(2)}) collective-permute-start(f32[32,128]{0,1:T(8,128)S(1)} %copy.27), channel_id=1, source_target_pairs={{1,0},{2,1},{3,2},{4,3},{5,4},{6,5},{7,6},{0,7},{9,8},{10,9},{11,1... | collective-permute-start | bytes 49160 | tf_op jit(solution)/shard_map/ppermute | solution.py:466
  10.9 0.1 reshape.67
  11.1 1.9 %collective-permute-start = (f32[32,128]{0,1:T(8,128)S(1)}, f32[32,128]{0,1:T(8,128)S(1)}, u32[]{:S(2)}, u32[]{:S(2)}) collective-permute-start(f32[32,128]{0,1:T(8,128)S(1)} %copy.26), channel_id=1, source_target_pairs={{0,1},{1,2},{2,3},{3,4},{4,5},{5,6},{6,7},{7,0},{8,9},{9,10},{10,1... | collective-permute-start | bytes 49160 | tf_op jit(solution)/shard_map/ppermute | solution.py:466
  13.2 0.2 copy.25
  13.4 1.0 collective-permute-done
  14.5 0.2 copy.24
  14.7 0.7 copy-done.16
  15.5 0.2 pad_maximum_fusion.1
  15.8 1.9 %collective-permute-start.2 = (f32[32,256]{1,0:T(8,128)S(1)}, f32[32,256]{1,0:T(8,128)S(1)}, u32[]{:S(2)}, u32[]{:S(2)}) collective-permute-start(f32[32,256]{1,0:T(8,128)S(1)} %get-tuple-element.19), channel_id=1, source_target_pairs={{0,8},{8,16},{16,24},{24,32},{32,40},{40,48},{48,56},{56,0},{1,9},... | collective-permute-start | bytes 98312 | tf_op jit(solution)/shard_map/ppermute | solution.py:466
  17.7 5.5 %collective-permute-start.3 = (f32[32,256]{1,0:T(8,128)S(1)}, f32[32,256]{1,0:T(8,128)S(1)}, u32[]{:S(2)}, u32[]{:S(2)}) collective-permute-start(f32[32,256]{1,0:T(8,128)S(1)} %get-tuple-element.20), channel_id=1, source_target_pairs={{8,0},{16,8},{24,16},{32,24},{40,32},{48,40},{56,48},{0,56},{9,1},... | collective-permute-start | bytes 98312 | tf_op jit(solution)/shard_map/ppermute | solution.py:466
  23.4 0.9 collective-permute-done.3
  24.3 1.9 %collective-permute-start.4 = (f32[2,8,1024]{2,1,0:T(8,128)S(1)}, f32[2,8,1024]{2,1,0:T(8,128)S(1)}, u32[]{:S(2)}, u32[]{:S(2)}) collective-permute-start(f32[2,8,1024]{2,1,0:T(8,128)S(1)} %get-tuple-element.17), channel_id=1, source_target_pairs={{0,64},{64,128},{128,192},{192,256},{256,320},{320,384},{384,448},... | collective-permute-start | bytes 196616 | tf_op jit(solution)/shard_map/ppermute | solution.py:466
  26.2 8.6 %collective-permute-start.5 = (f32[2,8,1024]{2,1,0:T(8,128)S(1)}, f32[2,8,1024]{2,1,0:T(8,128)S(1)}, u32[]{:S(2)}, u32[]{:S(2)}) collective-permute-start(f32[2,8,1024]{2,1,0:T(8,128)S(1)} %get-tuple-element.18), channel_id=1, source_target_pairs={{64,0},{128,64},{192,128},{256,192},{320,256},{384,320},{448,384},... | collective-permute-start | bytes 196616 | tf_op jit(solution)/shard_map/ppermute | solution.py:466
  34.8 1.3 collective-permute-done.5
  36.2 0.8 copy-done.7
  37.0 19.5 %filter.1 = (bf16[8,32,1024]{2,1,0:T(8,128)(2,1)}, f32[1152,128]{1,0:T(8,128)}) custom-call(f32[8]{0:T(128)S(1)} %copy-done.15, bf16[8,32,1024]{2,1,0:T(8,128)(2,1)S(1)} %copy-done, f32[32,1024]{1,0:T(8,128)S(1)} %get-tuple-element.14.pot_ref, f32[32,1024]{1,0:T(8,128)S(1)} %copy-done.7), custom_call_target="tpu_custom_call" | custom-call | flops 60000000 | bytes 1000000 | tf_op jit(solution)/shard_map/filter/pallas_call | solution.py:264
  56.5 4.6 %all-to-all-start = ((f32[144,8,128]{2,1,0:T(8,128)}), f32[144,8,128]{2,1,0:T(8,128)S(1)}, u32[]{:S(2)}, u32[]{:S(2)}) async-start(f32[144,8,128]{2,1,0:T(8,128)} %bitcast.8), calls=%async_computation | async-start | bytes 1179648 | tf_op jit(solution)/shard_map/all_to_all | solution.py:490
  61.2 12.8 %all-to-all-done = f32[144,8,128]{2,1,0:T(8,128)S(1)} async-done(((f32[144,8,128]{2,1,0:T(8,128)}), f32[144,8,128]{2,1,0:T(8,128)S(1)}, u32[]{:S(2)}, u32[]{:S(2)}) %all-to-all-start) | async-done | bytes 589856 | tf_op jit(solution)/shard_map/all_to_all | solution.py:490
  74.0 1.7 %along_x.1 = f32[768,128]{1,0:T(8,128)} custom-call(s32[3]{0:T(128)S(1)} %pad_add_fusion.place_ref, f32[1152,128]{1,0:T(8,128)S(1)} %bitcast.31, bf16[8,48,192]{2,1,0:T(8,128)(2,1)S(1)} %copy-done.6, bf16[8,48,192]{2,1,0:T(8,128)(2,1)S(1)} %copy-done.5), custom_call_target="tpu_custom_call" | custom-call | flops 1000000 | bytes 1000000 | tf_op jit(solution)/shard_map/along_x/pallas_call | solution.py:296
  75.8 17.6 %all-to-all-start.1 = ((f32[192,4,128]{2,1,0:T(4,128)}), f32[192,4,128]{2,1,0:T(4,128)S(1)}, u32[]{:S(2)}, u32[]{:S(2)}) async-start(f32[192,4,128]{2,1,0:T(4,128)} %bitcast.10), calls=%async_computation.1 | async-start | bytes 786432 | tf_op jit(solution)/shard_map/all_to_all | solution.py:490
  93.4 0.6 copy-done.18
  94.0 0.6 dynamic_slice.3.lx_ref
  94.6 14.1 %all-to-all-done.1 = f32[192,4,128]{2,1,0:T(4,128)S(1)} async-done(((f32[192,4,128]{2,1,0:T(4,128)}), f32[192,4,128]{2,1,0:T(4,128)S(1)}, u32[]{:S(2)}, u32[]{:S(2)}) %all-to-all-start.1) | async-done | bytes 393248 | tf_op jit(solution)/shard_map/all_to_all | solution.py:490
  108.8 2.4 %on_plane.1 = f32[384,128]{1,0:T(8,128)S(1)} custom-call(s32[3]{0:T(128)S(1)} %pad_add_fusion.place_ref, f32[1]{0:T(128)} %dynamic_slice.3.lx_ref, f32[768,128]{1,0:T(8,128)S(1)} %bitcast.33, bf16[1024,128]{1,0:T(8,128)(2,1)S(1)} %copy-done.4, bf16[1024,128]{1,0:T(8,128)(2,1)S(1)} %copy-done.3, bf16[128,192]{1,0:T(8,128)(2,1)S(1)} %copy-done.14, ...), custom_call_target="tpu_custom_call" | custom-call | flops 1000000 | bytes 1000000 | tf_op jit(solution)/shard_map/on_plane/pallas_call | solution.py:384
  111.2 16.4 %all_to_all.20 = f32[192,2,128]{2,1,0:T(2,128)S(1)} all-to-all(f32[192,2,128]{2,1,0:T(2,128)S(1)} %bitcast.34), channel_id=1, replica_groups=mesh['gx'=8,'gy'=8,'gz'=8] {'gy','gz'}, dimensions={0} | all-to-all | bytes 393216 | tf_op jit(solution)/shard_map/all_to_all | solution.py:490
  127.6 0.9 on_window.1
  128.5 3.5 %all-to-all-start.3 = ((f32[128,8,128]{2,1,0:T(8,128)}), f32[128,8,128]{2,1,0:T(8,128)S(1)}, u32[]{:S(2)}, u32[]{:S(2)}) async-start(f32[128,8,128]{2,1,0:T(8,128)} %bitcast.15), calls=%async_computation.3 | async-start | bytes 1048576 | tf_op jit(solution)/shard_map/all_to_all | solution.py:490
  132.1 0.8 slice.48
  132.9 15.0 %all-to-all-done.3 = f32[128,8,128]{2,1,0:T(8,128)S(1)} async-done(((f32[128,8,128]{2,1,0:T(8,128)}), f32[128,8,128]{2,1,0:T(8,128)S(1)}, u32[]{:S(2)}, u32[]{:S(2)}) %all-to-all-start.3) | async-done | bytes 524320 | tf_op jit(solution)/shard_map/all_to_all | solution.py:490
  147.9 1.5 %last_step.1 = f32[32,1024]{1,0:T(8,128)} custom-call(s32[3]{0:T(128)S(1)} %pad_add_fusion.place_ref, f32[1024,128]{1,0:T(8,128)S(1)} %bitcast.32, f32[32,1024]{1,0:T(8,128)S(1)} %get-tuple-element.12.base_ref, bf16[8,32,128]{2,1,0:T(8,128)(2,1)S(1)} %copy-done.9, bf16[8,32,128]{2,1,0:T(8,128)(2,1)S(1)} %copy-done.8), custom_call_target="tpu_custom_call" | custom-call | flops 1000000 | bytes 1000000 | tf_op jit(solution)/shard_map/last_step/pallas_call | solution.py:454
  (52 shorter events, 1.2 us)
Async XLA Ops:
  2.1 10.9 %collective-permute-start.1 = (f32[32,128]{0,1:T(8,128)S(1)}, f32[32,128]{0,1:T(8,128)S(1)}, u32[]{:S(2)}, u32[]{:S(2)}) collective-permute-start(f32[32,128]{0,1:T(8,128)S(1)} %copy.27), channel_id=1, source_target_pairs={{1,0},{2,1},{3,2},{4,3},{5,4},{6,5},{7,6},{0,7},{9,8},{10,9},{11,1... | collective-permute-start | bytes 49160 | tf_op jit(solution)/shard_map/ppermute | solution.py:466
  11.1 3.2 %collective-permute-start = (f32[32,128]{0,1:T(8,128)S(1)}, f32[32,128]{0,1:T(8,128)S(1)}, u32[]{:S(2)}, u32[]{:S(2)}) collective-permute-start(f32[32,128]{0,1:T(8,128)S(1)} %copy.26), channel_id=1, source_target_pairs={{0,1},{1,2},{2,3},{3,4},{4,5},{5,6},{6,7},{7,0},{8,9},{9,10},{10,1... | collective-permute-start | bytes 49160 | tf_op jit(solution)/shard_map/ppermute | solution.py:466
  14.5 0.9 copy-start.16
  14.5 1.0 copy-start.17
  15.8 7.6 %collective-permute-start.2 = (f32[32,256]{1,0:T(8,128)S(1)}, f32[32,256]{1,0:T(8,128)S(1)}, u32[]{:S(2)}, u32[]{:S(2)}) collective-permute-start(f32[32,256]{1,0:T(8,128)S(1)} %get-tuple-element.19), channel_id=1, source_target_pairs={{0,8},{8,16},{16,24},{24,32},{32,40},{40,48},{48,56},{56,0},{1,9},... | collective-permute-start | bytes 98312 | tf_op jit(solution)/shard_map/ppermute | solution.py:466
  17.7 6.5 %collective-permute-start.3 = (f32[32,256]{1,0:T(8,128)S(1)}, f32[32,256]{1,0:T(8,128)S(1)}, u32[]{:S(2)}, u32[]{:S(2)}) collective-permute-start(f32[32,256]{1,0:T(8,128)S(1)} %get-tuple-element.20), channel_id=1, source_target_pairs={{8,0},{16,8},{24,16},{32,24},{40,32},{48,40},{56,48},{0,56},{9,1},... | collective-permute-start | bytes 98312 | tf_op jit(solution)/shard_map/ppermute | solution.py:466
  24.3 10.5 %collective-permute-start.4 = (f32[2,8,1024]{2,1,0:T(8,128)S(1)}, f32[2,8,1024]{2,1,0:T(8,128)S(1)}, u32[]{:S(2)}, u32[]{:S(2)}) collective-permute-start(f32[2,8,1024]{2,1,0:T(8,128)S(1)} %get-tuple-element.17), channel_id=1, source_target_pairs={{0,64},{64,128},{128,192},{192,256},{256,320},{320,384},{384,448},... | collective-permute-start | bytes 196616 | tf_op jit(solution)/shard_map/ppermute | solution.py:466
  26.2 10.0 %copy-start = (bf16[8,32,1024]{2,1,0:T(8,128)(2,1)S(1)}, bf16[8,32,1024]{2,1,0:T(8,128)(2,1)}, u32[]{:S(2)}) copy-start(bf16[8,32,1024]{2,1,0:T(8,128)(2,1)} %orb_ref.1) | copy-start | bytes 1572868
  26.2 9.9 %collective-permute-start.5 = (f32[2,8,1024]{2,1,0:T(8,128)S(1)}, f32[2,8,1024]{2,1,0:T(8,128)S(1)}, u32[]{:S(2)}, u32[]{:S(2)}) collective-permute-start(f32[2,8,1024]{2,1,0:T(8,128)S(1)} %get-tuple-element.18), channel_id=1, source_target_pairs={{64,0},{128,64},{192,128},{256,192},{320,256},{384,320},{448,384},... | collective-permute-start | bytes 196616 | tf_op jit(solution)/shard_map/ppermute | solution.py:466
  36.1 0.9 copy-start.7
  36.1 0.9 copy-start.15
  56.5 17.5 %copy-start.5 = (bf16[8,48,192]{2,1,0:T(8,128)(2,1)S(1)}, bf16[8,48,192]{2,1,0:T(8,128)(2,1)}, u32[]{:S(2)}) copy-start(bf16[8,48,192]{2,1,0:T(8,128)(2,1)} %constant.85.clone.low_ref) | copy-start | bytes 442372
  56.5 17.5 %copy-start.6 = (bf16[8,48,192]{2,1,0:T(8,128)(2,1)S(1)}, bf16[8,48,192]{2,1,0:T(8,128)(2,1)}, u32[]{:S(2)}) copy-start(bf16[8,48,192]{2,1,0:T(8,128)(2,1)} %constant.84.clone.high_ref) | copy-start | bytes 442372
  56.5 17.5 %all-to-all-start = ((f32[144,8,128]{2,1,0:T(8,128)}), f32[144,8,128]{2,1,0:T(8,128)S(1)}, u32[]{:S(2)}, u32[]{:S(2)}) async-start(f32[144,8,128]{2,1,0:T(8,128)} %bitcast.8), calls=%async_computation | async-start | bytes 1179648 | tf_op jit(solution)/shard_map/all_to_all | solution.py:490
  74.0 34.8 %copy-start.4 = (bf16[1024,128]{1,0:T(8,128)(2,1)S(1)}, bf16[1024,128]{1,0:T(8,128)(2,1)}, u32[]{:S(2)}) copy-start(bf16[1024,128]{1,0:T(8,128)(2,1)} %constant.86.clone.zh_ref) | copy-start | bytes 786436
  74.0 34.8 %copy-start.10 = (bf16[4,64,128]{2,1,0:T(8,128)(2,1)S(1)}, bf16[4,64,128]{2,1,0:T(8,128)(2,1)}, u32[]{:S(2)}) copy-start(bf16[4,64,128]{2,1,0:T(8,128)(2,1)} %constant.92.clone.bl_ref) | copy-start | bytes 196612
  74.0 34.8 %copy-start.11 = (bf16[4,64,128]{2,1,0:T(8,128)(2,1)S(1)}, bf16[4,64,128]{2,1,0:T(8,128)(2,1)}, u32[]{:S(2)}) copy-start(bf16[4,64,128]{2,1,0:T(8,128)(2,1)} %constant.91.clone.bh_ref) | copy-start | bytes 196612
  74.0 34.8 %copy-start.12 = (f32[128,128]{1,0:T(8,128)S(1)}, f32[128,128]{1,0:T(8,128)}, u32[]{:S(2)}) copy-start(f32[128,128]{1,0:T(8,128)} %constant.90.clone.wave_ref) | copy-start | bytes 196612
  74.0 34.8 %copy-start.13 = (bf16[128,192]{1,0:T(8,128)(2,1)S(1)}, bf16[128,192]{1,0:T(8,128)(2,1)}, u32[]{:S(2)}) copy-start(bf16[128,192]{1,0:T(8,128)(2,1)} %constant.89.clone.yl_ref) | copy-start | bytes 147460
  74.0 34.8 %copy-start.14 = (bf16[128,192]{1,0:T(8,128)(2,1)S(1)}, bf16[128,192]{1,0:T(8,128)(2,1)}, u32[]{:S(2)}) copy-start(bf16[128,192]{1,0:T(8,128)(2,1)} %constant.88.clone.yh_ref) | copy-start | bytes 147460
  75.8 33.0 %copy-start.1 = (bf16[128,1024]{1,0:T(8,128)(2,1)S(1)}, bf16[128,1024]{1,0:T(8,128)(2,1)}, u32[]{:S(2)}) copy-start(bf16[128,1024]{1,0:T(8,128)(2,1)} %constant.94.clone.tl_ref) | copy-start | bytes 786436
  75.8 33.0 %copy-start.2 = (bf16[128,1024]{1,0:T(8,128)(2,1)S(1)}, bf16[128,1024]{1,0:T(8,128)(2,1)}, u32[]{:S(2)}) copy-start(bf16[128,1024]{1,0:T(8,128)(2,1)} %constant.93.clone.th_ref) | copy-start | bytes 786436
  75.8 33.0 %copy-start.3 = (bf16[1024,128]{1,0:T(8,128)(2,1)S(1)}, bf16[1024,128]{1,0:T(8,128)(2,1)}, u32[]{:S(2)}) copy-start(bf16[1024,128]{1,0:T(8,128)(2,1)} %constant.87.clone.zl_ref) | copy-start | bytes 786436
  75.8 33.0 %all-to-all-start.1 = ((f32[192,4,128]{2,1,0:T(4,128)}), f32[192,4,128]{2,1,0:T(4,128)S(1)}, u32[]{:S(2)}, u32[]{:S(2)}) async-start(f32[192,4,128]{2,1,0:T(4,128)} %bitcast.10), calls=%async_computation.1 | async-start | bytes 786432 | tf_op jit(solution)/shard_map/all_to_all | solution.py:490
  93.4 0.7 copy-start.18
  128.5 19.4 %all-to-all-start.3 = ((f32[128,8,128]{2,1,0:T(8,128)}), f32[128,8,128]{2,1,0:T(8,128)S(1)}, u32[]{:S(2)}, u32[]{:S(2)}) async-start(f32[128,8,128]{2,1,0:T(8,128)} %bitcast.15), calls=%async_computation.3 | async-start | bytes 1048576 | tf_op jit(solution)/shard_map/all_to_all | solution.py:490
  132.1 15.8 %copy-start.8 = (bf16[8,32,128]{2,1,0:T(8,128)(2,1)S(1)}, bf16[8,32,128]{2,1,0:T(8,128)(2,1)}, u32[]{:S(2)}) copy-start(bf16[8,32,128]{2,1,0:T(8,128)(2,1)} %constant.96.clone.low_ref) | copy-start | bytes 196612
  132.1 15.8 %copy-start.9 = (bf16[8,32,128]{2,1,0:T(8,128)(2,1)S(1)}, bf16[8,32,128]{2,1,0:T(8,128)(2,1)}, u32[]{:S(2)}) copy-start(bf16[8,32,128]{2,1,0:T(8,128)(2,1)} %constant.95.clone.high_ref) | copy-start | bytes 196612

commit v2 on v1

--- a/solution.py
+++ b/solution.py
@@ -19,6 +19,7 @@
 FIRST, LAST = 4, 28
 KEPT = LAST - FIRST
 LANES = 128
+GROUP = 16
 PER = LANES // LX
 
 spacing = 0.2
@@ -129,57 +130,96 @@
     return lax.broadcasted_iota(jnp.int32, shape, dim)
 
 
-def filter_kernel(occ_ref, orb_ref, pot_ref, weight_ref, new_ref, send_ref, ya, yb, coef, dens):
+def swap_four(v, lane):
+    low, even = lane < 2 * LX, (lane // LX) % 2 == 0
+    w = [None] * 4
+    for g in range(2):
+        w[g] = jnp.where(low, v[g], pltpu.roll(v[g + 2], 2 * LX, 1))
+        w[g + 2] = jnp.where(low, pltpu.roll(v[g], 2 * LX, 1), v[g + 2])
+    out = []
+    for g in (0, 2):
+        out.append(jnp.where(even, w[g], pltpu.roll(w[g + 1], LX, 1)))
+        out.append(jnp.where(even, pltpu.roll(w[g], 3 * LX, 1), w[g + 1]))
+    return out
+
+
+def swap_inner(v, row, lane):
+    a, b = row % 4, lane // LX
+    turned = pltpu.roll(v, 2 * LX, 1)
+    v = jnp.where(
+        a // 2 == b // 2,
+        v,
+        jnp.where(a < 2, pltpu.roll(turned, 6, 0), pltpu.roll(turned, 2, 0)),
+    )
+    return jnp.where(
+        a % 2 == b % 2,
+        v,
+        jnp.where(
+            a % 2 == 0,
+            pltpu.roll(pltpu.roll(v, LX, 1), 7, 0),
+            pltpu.roll(pltpu.roll(v, 3 * LX, 1), 1, 0),
+        ),
+    )
+
+
+def filter_kernel(occ_ref, orb_ref, pot_ref, weight_ref, new_ref, send_ref, ya, yb, coef, flat):
     tiles, chunks = LX // 8, LX * LX // LANES
+    line = LX + 2
     lane = iota((8, LANES), 1)
     row = iota((8, LANES), 0)
     low_z, high_z = lane % LX == 0, lane % LX == LX - 1
-    first_y, last_y = lane < LX, lane >= LANES - LX
     first_x, last_x = row == 0, row == 7
     zero = jnp.zeros((8, LANES), F32)
-
-    coef[...] = (2.0 / half_width) * pot_ref[...] + (2.0 / half_width) * (
-        6.0 * kinetic - centre_value
-    )
     alpha = -2.0 * kinetic / half_width
-
-    def fill(n, carry):
-        for buffer in (ya, yb):
-            buffer[n, 0:8, :] = jnp.zeros((8, (chunks + 2) * LANES), F32)
-            buffer[n, 8 + LX : 16 + LX, :] = jnp.zeros((8, (chunks + 2) * LANES), F32)
-            buffer[n, :, 0:LANES] = jnp.zeros((16 + LX, LANES), F32)
-            buffer[n, :, (chunks + 1) * LANES :] = jnp.zeros((16 + LX, LANES), F32)
-        ya[n, 8 : 8 + LX, LANES : (chunks + 1) * LANES] = orb_ref[n].astype(F32)
+    scale, shift = 2.0 / half_width, (2.0 / half_width) * (6.0 * kinetic - centre_value)
+
+    for buffer in (ya, yb):
+        for h in range(2):
+            buffer[h * line] = jnp.zeros((LX, LANES), F32)
+            buffer[h * line + line - 1] = jnp.zeros((LX, LANES), F32)
+
+    def bring(c, carry):
+        here = pl.ds(pl.multiple_of(c * LANES, LANES), LANES)
+        for t in range(tiles):
+            rows = slice(8 * t, 8 * t + 8)
+            for h in range(2):
+                v = [orb_ref[4 * h + g, rows, here].astype(F32) for g in range(4)]
+                for y, value in enumerate(swap_four(v, lane)):
+                    ya[h * line + 1 + PER * c + y, rows, :] = value
+            v = scale * pot_ref[rows, here] + shift
+            for y in range(PER):
+                value = jnp.where(lane // LX == y, v, 0.0)
+                value = value + pltpu.roll(value, LX, 1)
+                coef[PER * c + y, rows, :] = value + pltpu.roll(value, 2 * LX, 1)
         return carry
 
-    lax.fori_loop(0, NORB, fill, 0)
+    lax.fori_loop(0, chunks, bring, 0)
 
     def advance(src, dst, start):
-        def one(n, carry):
-            for c in range(chunks):
-                here = slice((c + 1) * LANES, (c + 2) * LANES)
-                for t in range(tiles):
-                    rows = slice(8 + 8 * t, 16 + 8 * t)
-                    cur = src[n, rows, here]
-                    above = src[n, 8 * t : 8 + 8 * t, here]
-                    below = src[n, 16 + 8 * t : 24 + 8 * t, here]
-                    before = src[n, rows, c * LANES : (c + 1) * LANES]
-                    after = src[n, rows, (c + 2) * LANES : (c + 3) * LANES]
-                    total = pltpu.roll(jnp.where(last_x, above, cur), 1, 0)
-                    total += pltpu.roll(jnp.where(first_x, below, cur), 7, 0)
-                    total += pltpu.roll(jnp.where(last_y, before, cur), LX, 1)
-                    total += pltpu.roll(jnp.where(first_y, after, cur), LANES - LX, 1)
-                    total += jnp.where(low_z, zero, pltpu.roll(cur, 1, 1))
-                    total += jnp.where(high_z, zero, pltpu.roll(cur, LANES - 1, 1))
-                    w = coef[8 * t : 8 + 8 * t, c * LANES : (c + 1) * LANES]
-                    result = alpha * total + w * cur
-                    if start:
-                        dst[n, rows, here] = 0.5 * result
-                    else:
-                        dst[n, rows, here] = result - dst[n, rows, here]
+        def one(b, carry):
+            for yy in range(GROUP):
+                y = GROUP * b + yy
+                for h in range(2):
+                    at = h * line + 1 + y
+                    cells = [src[at, 8 * t : 8 * t + 8, :] for t in range(tiles)]
+                    for t in range(tiles):
+                        rows = slice(8 * t, 8 * t + 8)
+                        cur = cells[t]
+                        above = cells[t - 1] if t > 0 else zero
+                        below = cells[t + 1] if t < tiles - 1 else zero
+                        total = jnp.where(low_z, zero, pltpu.roll(cur, 1, 1))
+                        total += jnp.where(high_z, zero, pltpu.roll(cur, LANES - 1, 1))
+                        total += pltpu.roll(jnp.where(last_x, above, cur), 1, 0)
+                        total += pltpu.roll(jnp.where(first_x, below, cur), 7, 0)
+                        total += src[at - 1, rows, :] + src[at + 1, rows, :]
+                        result = alpha * total + coef[y, rows, :] * cur
+                        if start:
+                            dst[at, rows, :] = 0.5 * result
+                        else:
+                            dst[at, rows, :] = result - dst[at, rows, :]
             return carry
 
-        lax.fori_loop(0, NORB, one, 0)
+        lax.fori_loop(0, LX // GROUP, one, 0)
 
     advance(ya, yb, True)
 
@@ -193,11 +233,23 @@
 
     pairs = [(n, m) for n in range(NORB) for m in range(n + 1)]
 
+    def take(c, carry):
+        here = pl.ds(pl.multiple_of(c * LANES, LANES), LANES)
+        for t in range(tiles):
+            rows = slice(8 * t, 8 * t + 8)
+            for h in range(2):
+                v = [ya[h * line + 1 + PER * c + y, rows, :] for y in range(PER)]
+                for g, value in enumerate(swap_four(v, lane)):
+                    flat[4 * h + g, rows, here] = value
+        return carry
+
+    lax.fori_loop(0, chunks, take, 0)
+
     def gather(t, sums):
         sums = list(sums)
-        start = pl.multiple_of(8 + 8 * t, 8)
+        rows = pl.ds(pl.multiple_of(8 * t, 8), 8)
         for c in range(chunks):
-            f = [ya[n, pl.ds(start, 8), (c + 1) * LANES : (c + 2) * LANES] for n in range(NORB)]
+            f = [flat[n, rows, c * LANES : (c + 1) * LANES] for n in range(NORB)]
             for at, (n, m) in enumerate(pairs):
                 sums[at] = sums[at] + f[n] * f[m]
         return tuple(sums)
@@ -227,40 +279,41 @@
             inverse[n, j] = -recip[n] * value
     wide = {pair: jnp.broadcast_to(inverse[pair], (8, LANES)) for pair in pairs}
 
+    kept = KEPT // PER
+
     def normal(t, carry):
-        start = pl.multiple_of(8 + 8 * t, 8)
         rows = pl.ds(pl.multiple_of(8 * t, 8), 8)
         for c in range(chunks):
-            here = slice((c + 1) * LANES, (c + 2) * LANES)
-            f = [ya[n, pl.ds(start, 8), here] for n in range(NORB)]
+            here = slice(c * LANES, (c + 1) * LANES)
+            f = [flat[n, rows, here] for n in range(NORB)]
             total = zero
             for n in range(NORB):
                 value = wide[n, 0] * f[0]
                 for m in range(1, n + 1):
                     value = value + wide[n, m] * f[m]
-                yb[n, pl.ds(start, 8), here] = value
+                flat[n, rows, here] = value
                 total = total + occ_ref[n] * (value * value)
-            there = slice(c * LANES, (c + 1) * LANES)
-            dens[rows, there] = total * weight_ref[rows, there]
+            if 1 <= c <= kept:
+                coef[c, rows, :] = swap_inner(total * weight_ref[rows, here], row, lane)
         return carry
 
     lax.fori_loop(0, tiles, normal, 0)
 
     def finish(n, carry):
-        new_ref[n] = yb[n, 8 : 8 + LX, LANES : (chunks + 1) * LANES].astype(BF16)
+        new_ref[n] = flat[n].astype(BF16)
         return carry
 
     lax.fori_loop(0, NORB, finish, 0)
 
-    kept = KEPT // PER
     for c in range(kept):
-        value = dens[FIRST:LAST, (c + 1) * LANES : (c + 2) * LANES]
-        for s in range(PARTS):
-            send_ref[pl.ds(s * KEPT * kept + c, KEPT, stride=kept), :] = value
+        for x in range(kept):
+            value = coef[c + 1, PER * (x + 1) : PER * (x + 2), :]
+            for s in range(PARTS):
+                start = s * KEPT * kept + PER * c * kept + x
+                send_ref[pl.ds(start, PER, stride=kept), :] = value
 
 
 def filtered_set(occupations, orbitals, potential_ext):
-    wide = LX * LX + 2 * LANES
     return call(
         filter_kernel,
         (
@@ -269,17 +322,17 @@
         ),
         [SMEM, VMEM, VMEM, VMEM],
         [
-            pltpu.VMEM((NORB, LX + 16, wide), F32),
-            pltpu.VMEM((NORB, LX + 16, wide), F32),
-            pltpu.VMEM((LX, LX * LX), F32),
-            pltpu.VMEM((LX, LX * LX), F32),
+            pltpu.VMEM((2 * (LX + 2), LX, LANES), F32),
+            pltpu.VMEM((2 * (LX + 2), LX, LANES), F32),
+            pltpu.VMEM((LX, LX, LANES), F32),
+            pltpu.VMEM((NORB, LX, LX * LX), F32),
         ],
         flops=60000000,
         name="filter",
     )(occupations, orbitals, potential_ext, jnp.asarray(WEIGHT))
 
 
-def x_kernel(place_ref, got_ref, high_ref, low_ref, send_ref):
+def y_kernel(place_ref, got_ref, high_ref, low_ref, send_ref):
     kept = KEPT // PER
     at = place_ref[0]
     table = (high_ref[at], low_ref[at])
@@ -292,18 +345,18 @@
             send_ref[pl.ds(q * 2 * kept + kept + c, CORE, stride=8 * kept), :] = value[:CORE]
 
 
-def along_x(place, got):
+def along_y(place, got):
     return call(
-        x_kernel,
+        y_kernel,
         jax.ShapeDtypeStruct((64 * 2 * KEPT // PER, LANES), F32),
         [SMEM, VMEM, VMEM, VMEM],
-        name="along_x",
+        name="along_y",
     )(place, got, *map(jnp.asarray, TABLES["along"]))
 
 
 def plane_kernel(
     place_ref,
-    lx_ref,
+    own_ref,
     got_ref,
     zh_ref,
     zl_ref,
@@ -333,7 +386,7 @@
     spread = jnp.concatenate([jnp.where(which == y, lines, 0.0) for y in range(PER)], axis=0)
     along_z = dot3(halves(spread), (zh_ref[...], zl_ref[...]))
     spectrum = dot3((yh_ref[...], yl_ref[...]), halves(along_z))
-    eigen = wave_ref[...] + lx_ref[0]
+    eigen = wave_ref[...] + own_ref[0]
     positive = eigen > 0.0
     green = jnp.where(positive, 4.0 * math.pi / jnp.where(positive, eigen, 1.0), 0.0)
     spectrum = spectrum * green
@@ -379,7 +432,7 @@
             send_ref[at : at + 4, :] = value[0:4]
 
 
-def on_plane(place, lx, got):
+def on_plane(place, wave, got):
     t = TABLES
     return call(
         plane_kernel,
@@ -389,7 +442,7 @@
         name="on_plane",
     )(
         place,
-        lx,
+        wave,
         got,
         *map(jnp.asarray, t["z_table"]),
         *map(jnp.asarray, t["y_table"]),
@@ -415,17 +468,28 @@
     return slater + wigner
 
 
-def window_kernel(got_ref, ion_ref, send_ref, dens_ref, base_ref):
+def window_kernel(got_ref, ion_ref, send_ref, dens_ref, base_ref, work):
     for half in range(2):
         value = got_ref[pl.ds(half, 64, stride=6), :]
         for s in range(PARTS):
             send_ref[pl.ds(s * LANES + half, 64, stride=2), :] = value
+    row, lane = iota((8, LANES), 0), iota((8, LANES), 1)
     for q in range(2):
-        for y in range(4):
-            here = slice((4 * q + y) * LANES, (4 * q + y + 1) * LANES)
-            value = got_ref[pl.ds(6 * q + 2 + y, LX, stride=12), :]
-            dens_ref[:, here] = value
-            base_ref[:, here] = ion_ref[:, here] + exchange_correlation(value)
+        for h in range(4):
+            x = 4 * q + h
+            value = got_ref[pl.ds(6 * q + 2 + h, LX, stride=12), :]
+            if 2 <= x < 6:
+                for low in range(PER):
+                    core = pltpu.roll(value[BUF : BUF + CORE], LANES - LX * low - BUF, 1)
+                    dens_ref[PER * (x - 2) + low] = core[:, :CORE]
+            for t in range(4):
+                piece = swap_inner(value[8 * t : 8 * t + 8], row, lane)
+                for half in range(2):
+                    y = 2 * t + half
+                    work[PER * x : PER * x + PER, y * LANES : (y + 1) * LANES] = piece[
+                        PER * half : PER * half + PER
+                    ]
+    base_ref[...] = ion_ref[...] + exchange_correlation(work[...])
 
 
 def on_window(got, ion_ext):
@@ -433,10 +497,11 @@
         window_kernel,
         (
             jax.ShapeDtypeStruct((PARTS * LANES, LANES), F32),
-            jax.ShapeDtypeStruct((LX, LX * LX), F32),
+            jax.ShapeDtypeStruct((CORE, CORE, CORE), F32),
             jax.ShapeDtypeStruct((LX, LX * LX), F32),
         ),
         [VMEM, VMEM],
+        [pltpu.VMEM((LX, LX * LX), F32)],
         name="on_window",
     )(got, ion_ext)
 
@@ -444,10 +509,17 @@
 def last_kernel(place_ref, got_ref, base_ref, high_ref, low_ref, out_ref):
     at = place_ref[0]
     table = (high_ref[at], low_ref[at])
-    for y in range(8):
-        here = slice(y * LANES, (y + 1) * LANES)
-        lines = got_ref[pl.ds(y, N, stride=8), :]
-        out_ref[:, here] = base_ref[:, here] + dot3(table, halves(lines))
+    row, lane = iota((8, LANES), 0), iota((8, LANES), 1)
+    for x in range(8):
+        lines = got_ref[pl.ds(x, N, stride=8), :]
+        value = dot3(table, halves(lines))
+        rows = slice(PER * x, PER * x + PER)
+        for t in range(4):
+            piece = swap_inner(value[8 * t : 8 * t + 8], row, lane)
+            for half in range(2):
+                y = 2 * t + half
+                here = slice(y * LANES, (y + 1) * LANES)
+                out_ref[rows, here] = base_ref[rows, here] + piece[PER * half : PER * half + PER]
 
 
 def last_step(place, got, base):
@@ -493,21 +565,19 @@
 
 
 def on_device(orbitals, potential, ion_potential, occupations):
-    gx, member = lax.axis_index("gx"), lax.axis_index(("gy", "gz"))
-    place = jnp.stack([gx, member % 4, member % 2]).astype(jnp.int32)
-    lx = jnp.asarray(TABLES["wave"])[gx * CORE + member // 4].reshape(1)
+    gy, member = lax.axis_index("gy"), lax.axis_index(("gx", "gz"))
+    place = jnp.stack([gy, member % 4, member % 2]).astype(jnp.int32)
+    wave = jnp.asarray(TABLES["wave"])[gy * CORE + member // 4].reshape(1)
     window = refill((potential, ion_potential))
+    window, place, wave = lax.optimization_barrier((window, place, wave))
     new_orbitals, send = filtered_set(occupations, orbitals, window[0])
-    got = exchange(send, "gx", KEPT * KEPT // PER)
-    send = along_x(place, got)
-    got = exchange(send, ("gy", "gz"), 2 * KEPT // PER)
-    send = on_plane(place, lx, got)
-    got = exchange(send, ("gy", "gz"), 6)
-    send, dens, base = on_window(got, window[1])
-    density = dens[BUF : BUF + CORE].reshape(CORE, LX, LX)[
-        :, BUF : BUF + CORE, BUF : BUF + CORE
-    ]
-    got = exchange(send, "gx", LANES)
+    got = exchange(send, "gy", KEPT * KEPT // PER)
+    send = along_y(place, got)
+    got = exchange(send, ("gx", "gz"), 2 * KEPT // PER)
+    send = on_plane(place, wave, got)
+    got = exchange(send, ("gx", "gz"), 6)
+    send, density, base = on_window(got, window[1])
+    got = exchange(send, "gy", LANES)
     new_potential = last_step(place, got, base)
     return (new_orbitals, density, new_potential)
 

time: 151 us -> 135 us (0.89)
  blocking collectives: 16.4 us -> 77.8 us
  waiting for transfers between devices: 45 us -> 2.22 us
  starting transfers between devices: 54.2 us -> 28.4 us
  Pallas kernels: 26 us -> 18.7 us
    all_to_all x1 -> x4, blocking collectives: 16.4 us -> 77.8 us  [exchange(): lax.all_to_all(shaped, axis, split_axis=0, concat_axis=0, tiled=True)]
    all_to_all x3 -> x0, waiting for transfers between devices: 41.9 us -> none  [exchange(): lax.all_to_all(shaped, axis, split_axis=0, concat_axis=0, tiled=True)]
    all_to_all x3 -> x0, starting transfers between devices: 25.7 us -> none  [exchange(): lax.all_to_all(shaped, axis, split_axis=0, concat_axis=0, tiled=True)]
    pallas_call x1, Pallas kernels: 19.5 us -> 12.8 us  [filtered_set(): call(filter_kernel, (jax.ShapeDtypeStruct((NORB, LX, LX * LX), BF16), jax...]
  transfers between devices with their start and end apart: 9 -> 6, of which waited for: 6 -> 2; matrix products, arithmetic and copies ran while one was open for 1% -> 1% of each run, Pallas kernels for 0% -> 0%
where the time goes in v2:
time: 135 us; the launch traced here: 134 us
  blocking collectives  77.8 us (58%)
  starting transfers between devices  28.4 us (21%)
  Pallas kernels  18.7 us (14%)
  local copies, waits for them, and re-layouts  4.38 us (3%)
  waiting for transfers between devices  2.22 us (2%)
  other arithmetic  1.54 us (1%)
    all_to_all x4, blocking collectives, exchange(): lax.all_to_all(shaped, axis, split_axis=0, concat_axis=0, tiled=True)  77.8 us
    ppermute x6, starting transfers between devices, both_sides(): return (lax.ppermute(last, axis, up), lax.ppermute(first, axis, down))  28.4 us
    pallas_call x1, Pallas kernels, filtered_set(): call(filter_kernel, (jax.ShapeDtypeStruct((NORB, LX, LX * LX), BF16), jax...  12.8 us
  transfers between devices with their start and end apart: 6, of which 2 were waited for; matrix products, arithmetic and copies ran while one was open for 1% of the time, Pallas kernels for 0%

profile of v2, /device:TPU:1, one launch (start us, length us, event | category | flops | bytes accessed | tf_op | source)
XLA Modules:
  0.0 134.1 jit_solution(12752888874798187311)
XLA Ops:
  0.6 1.2 slice_maximum_fusion
  1.9 0.1 reshape.64
  2.1 8.7 %collective-permute-start.1 = (f32[32,128]{0,1:T(8,128)S(1)}, f32[32,128]{0,1:T(8,128)S(1)}, u32[]{:S(2)}, u32[]{:S(2)}) collective-permute-start(f32[32,128]{0,1:T(8,128)S(1)} %copy.27), channel_id=1, source_target_pairs={{1,0},{2,1},{3,2},{4,3},{5,4},{6,5},{7,6},{0,7},{9,8},{10,9},{11,1... | collective-permute-start | bytes 49160 | tf_op jit(solution)/shard_map/ppermute | solution.py:538
  10.9 0.1 reshape.63
  11.0 0.1 copy.26
  11.1 1.9 %collective-permute-start = (f32[32,128]{0,1:T(8,128)S(1)}, f32[32,128]{0,1:T(8,128)S(1)}, u32[]{:S(2)}, u32[]{:S(2)}) collective-permute-start(f32[32,128]{0,1:T(8,128)S(1)} %copy.26), channel_id=1, source_target_pairs={{0,1},{1,2},{2,3},{3,4},{4,5},{5,6},{6,7},{7,0},{8,9},{9,10},{10,1... | collective-permute-start | bytes 49160 | tf_op jit(solution)/shard_map/ppermute | solution.py:538
  13.1 0.1 reshape.53
  13.2 0.2 copy.25
  13.4 1.0 collective-permute-done
  14.4 0.1 reshape.51
  14.5 0.2 copy.24
  14.7 0.7 copy-done.16
  15.5 0.2 pad_maximum_fusion.1
  15.7 0.1 reshape.54
  15.8 1.9 %collective-permute-start.2 = (f32[32,256]{1,0:T(8,128)S(1)}, f32[32,256]{1,0:T(8,128)S(1)}, u32[]{:S(2)}, u32[]{:S(2)}) collective-permute-start(f32[32,256]{1,0:T(8,128)S(1)} %get-tuple-element.25), channel_id=1, source_target_pairs={{0,8},{8,16},{16,24},{24,32},{32,40},{40,48},{48,56},{56,0},{1,9},... | collective-permute-start | bytes 98312 | tf_op jit(solution)/shard_map/ppermute | solution.py:538
  17.7 5.5 %collective-permute-start.3 = (f32[32,256]{1,0:T(8,128)S(1)}, f32[32,256]{1,0:T(8,128)S(1)}, u32[]{:S(2)}, u32[]{:S(2)}) collective-permute-start(f32[32,256]{1,0:T(8,128)S(1)} %get-tuple-element.26), channel_id=1, source_target_pairs={{8,0},{16,8},{24,16},{32,24},{40,32},{48,40},{56,48},{0,56},{9,1},... | collective-permute-start | bytes 98312 | tf_op jit(solution)/shard_map/ppermute | solution.py:538
  23.3 0.6 copy-done.18
  23.9 0.6 dynamic_slice.3.own_ref
  24.5 0.1 concatenate.18
  24.7 1.9 %collective-permute-start.4 = (f32[2,8,1024]{2,1,0:T(8,128)S(1)}, f32[2,8,1024]{2,1,0:T(8,128)S(1)}, u32[]{:S(2)}, u32[]{:S(2)}) collective-permute-start(f32[2,8,1024]{2,1,0:T(8,128)S(1)} %get-tuple-element.23), channel_id=1, source_target_pairs={{0,64},{64,128},{128,192},{192,256},{256,320},{320,384},{384,448},... | collective-permute-start | bytes 196616 | tf_op jit(solution)/shard_map/ppermute | solution.py:538
  26.7 8.4 %collective-permute-start.5 = (f32[2,8,1024]{2,1,0:T(8,128)S(1)}, f32[2,8,1024]{2,1,0:T(8,128)S(1)}, u32[]{:S(2)}, u32[]{:S(2)}) collective-permute-start(f32[2,8,1024]{2,1,0:T(8,128)S(1)} %get-tuple-element.24), channel_id=1, source_target_pairs={{64,0},{128,64},{192,128},{256,192},{320,256},{384,320},{448,384},... | collective-permute-start | bytes 196616 | tf_op jit(solution)/shard_map/ppermute | solution.py:538
  35.2 1.2 collective-permute-done.5
  36.5 0.8 copy-done.7
  37.3 12.8 %filter.1 = (bf16[8,32,1024]{2,1,0:T(8,128)(2,1)}, f32[1152,128]{1,0:T(8,128)S(1)}) custom-call(f32[8]{0:T(128)S(1)} %copy-done.15, bf16[8,32,1024]{2,1,0:T(8,128)(2,1)S(1)} %copy-done, f32[32,1024]{1,0:T(8,128)S(1)} %get-tuple-element.20.pot_ref, f32[32,1024]{1,0:T(8,128)S(1)} %copy-done.7), custom_call_target="tpu_custom_call" | custom-call | flops 60000000 | bytes 1000000 | tf_op jit(solution)/shard_map/filter/pallas_call | solution.py:317
  50.1 12.6 %all_to_all.20 = f32[144,8,128]{2,1,0:T(8,128)S(1)} all-to-all(f32[144,8,128]{2,1,0:T(8,128)S(1)} %bitcast.37), channel_id=1, replica_groups=mesh['gx'=8,'gy'=8,'gz'=8] {'gy'}, dimensions={0} | all-to-all | bytes 1179648 | tf_op jit(solution)/shard_map/all_to_all | solution.py:562
  62.8 1.0 along_y.1
  63.8 34.7 %all_to_all.21 = f32[192,4,128]{2,1,0:T(4,128)S(1)} all-to-all(f32[192,4,128]{2,1,0:T(4,128)S(1)} %bitcast.34), channel_id=1, replica_groups=mesh['gx'=8,'gy'=8,'gz'=8] {'gx','gz'}, dimensions={0} | all-to-all | bytes 786432 | tf_op jit(solution)/shard_map/all_to_all | solution.py:562
  98.5 2.4 %on_plane.1 = f32[384,128]{1,0:T(8,128)S(1)} custom-call(s32[3]{0:T(128)S(1)} %pad_add_fusion.place_ref, f32[1]{0:T(128)} %dynamic_slice.3.own_ref, f32[768,128]{1,0:T(8,128)S(1)} %bitcast.33, bf16[1024,128]{1,0:T(8,128)(2,1)S(1)} %copy-done.4, bf16[1024,128]{1,0:T(8,128)(2,1)S(1)} %copy-done.3, bf16[128,192]{1,0:T(8,128)(2,1)S(1)} %copy-done.14, ...), custom_call_target="tpu_custom_call" | custom-call | flops 1000000 | bytes 1000000 | tf_op jit(solution)/shard_map/on_plane/pallas_call | solution.py:437
  100.9 19.2 %all_to_all.22 = f32[192,2,128]{2,1,0:T(2,128)S(1)} all-to-all(f32[192,2,128]{2,1,0:T(2,128)S(1)} %bitcast.35), channel_id=1, replica_groups=mesh['gx'=8,'gy'=8,'gz'=8] {'gx','gz'}, dimensions={0} | all-to-all | bytes 393216 | tf_op jit(solution)/shard_map/all_to_all | solution.py:562
  120.1 0.9 on_window.1
  121.1 11.3 %all_to_all.23 = f32[128,8,128]{2,1,0:T(8,128)S(1)} all-to-all(f32[128,8,128]{2,1,0:T(8,128)S(1)} %bitcast.38), channel_id=1, replica_groups=mesh['gx'=8,'gy'=8,'gz'=8] {'gy'}, dimensions={0} | all-to-all | bytes 1048576 | tf_op jit(solution)/shard_map/all_to_all | solution.py:562
  132.4 1.7 %last_step.1 = f32[32,1024]{1,0:T(8,128)} custom-call(s32[3]{0:T(128)S(1)} %pad_add_fusion.place_ref, f32[1024,128]{1,0:T(8,128)S(1)} %bitcast.32, f32[32,1024]{1,0:T(8,128)S(1)} %get-tuple-element.18.base_ref, bf16[8,32,128]{2,1,0:T(8,128)(2,1)S(1)} %copy-done.9, bf16[8,32,128]{2,1,0:T(8,128)(2,1)S(1)} %copy-done.8), custom_call_target="tpu_custom_call" | custom-call | flops 1000000 | bytes 1000000 | tf_op jit(solution)/shard_map/last_step/pallas_call | solution.py:526
  (46 shorter events, 0.4 us)
Async XLA Ops:
  2.1 10.9 %collective-permute-start.1 = (f32[32,128]{0,1:T(8,128)S(1)}, f32[32,128]{0,1:T(8,128)S(1)}, u32[]{:S(2)}, u32[]{:S(2)}) collective-permute-start(f32[32,128]{0,1:T(8,128)S(1)} %copy.27), channel_id=1, source_target_pairs={{1,0},{2,1},{3,2},{4,3},{5,4},{6,5},{7,6},{0,7},{9,8},{10,9},{11,1... | collective-permute-start | bytes 49160 | tf_op jit(solution)/shard_map/ppermute | solution.py:538
  11.1 3.2 %collective-permute-start = (f32[32,128]{0,1:T(8,128)S(1)}, f32[32,128]{0,1:T(8,128)S(1)}, u32[]{:S(2)}, u32[]{:S(2)}) collective-permute-start(f32[32,128]{0,1:T(8,128)S(1)} %copy.26), channel_id=1, source_target_pairs={{0,1},{1,2},{2,3},{3,4},{4,5},{5,6},{6,7},{7,0},{8,9},{9,10},{10,1... | collective-permute-start | bytes 49160 | tf_op jit(solution)/shard_map/ppermute | solution.py:538
  14.5 0.9 copy-start.16
  14.5 1.0 copy-start.17
  15.8 8.9 %collective-permute-start.2 = (f32[32,256]{1,0:T(8,128)S(1)}, f32[32,256]{1,0:T(8,128)S(1)}, u32[]{:S(2)}, u32[]{:S(2)}) collective-permute-start(f32[32,256]{1,0:T(8,128)S(1)} %get-tuple-element.25), channel_id=1, source_target_pairs={{0,8},{8,16},{16,24},{24,32},{32,40},{40,48},{48,56},{56,0},{1,9},... | collective-permute-start | bytes 98312 | tf_op jit(solution)/shard_map/ppermute | solution.py:538
  17.7 6.9 %collective-permute-start.3 = (f32[32,256]{1,0:T(8,128)S(1)}, f32[32,256]{1,0:T(8,128)S(1)}, u32[]{:S(2)}, u32[]{:S(2)}) collective-permute-start(f32[32,256]{1,0:T(8,128)S(1)} %get-tuple-element.26), channel_id=1, source_target_pairs={{8,0},{16,8},{24,16},{32,24},{40,32},{48,40},{56,48},{0,56},{9,1},... | collective-permute-start | bytes 98312 | tf_op jit(solution)/shard_map/ppermute | solution.py:538
  23.3 0.7 copy-start.18
  24.7 10.4 %collective-permute-start.4 = (f32[2,8,1024]{2,1,0:T(8,128)S(1)}, f32[2,8,1024]{2,1,0:T(8,128)S(1)}, u32[]{:S(2)}, u32[]{:S(2)}) collective-permute-start(f32[2,8,1024]{2,1,0:T(8,128)S(1)} %get-tuple-element.23), channel_id=1, source_target_pairs={{0,64},{64,128},{128,192},{192,256},{256,320},{320,384},{384,448},... | collective-permute-start | bytes 196616 | tf_op jit(solution)/shard_map/ppermute | solution.py:538
  26.7 9.7 %collective-permute-start.5 = (f32[2,8,1024]{2,1,0:T(8,128)S(1)}, f32[2,8,1024]{2,1,0:T(8,128)S(1)}, u32[]{:S(2)}, u32[]{:S(2)}) collective-permute-start(f32[2,8,1024]{2,1,0:T(8,128)S(1)} %get-tuple-element.24), channel_id=1, source_target_pairs={{64,0},{128,64},{192,128},{256,192},{320,256},{384,320},{448,384},... | collective-permute-start | bytes 196616 | tf_op jit(solution)/shard_map/ppermute | solution.py:538
  35.2 1.3 copy-start
  36.4 0.9 copy-start.7
  36.5 0.9 copy-start.15
  50.1 12.6 %copy-start.5 = (bf16[8,48,192]{2,1,0:T(8,128)(2,1)S(1)}, bf16[8,48,192]{2,1,0:T(8,128)(2,1)}, u32[]{:S(2)}) copy-start(bf16[8,48,192]{2,1,0:T(8,128)(2,1)} %constant.85.clone.low_ref) | copy-start | bytes 442372
  50.1 12.6 %copy-start.6 = (bf16[8,48,192]{2,1,0:T(8,128)(2,1)S(1)}, bf16[8,48,192]{2,1,0:T(8,128)(2,1)}, u32[]{:S(2)}) copy-start(bf16[8,48,192]{2,1,0:T(8,128)(2,1)} %constant.84.clone.high_ref) | copy-start | bytes 442372
  62.7 35.8 %copy-start.4 = (bf16[1024,128]{1,0:T(8,128)(2,1)S(1)}, bf16[1024,128]{1,0:T(8,128)(2,1)}, u32[]{:S(2)}) copy-start(bf16[1024,128]{1,0:T(8,128)(2,1)} %constant.86.clone.zh_ref) | copy-start | bytes 786436
  62.7 35.8 %copy-start.10 = (bf16[4,64,128]{2,1,0:T(8,128)(2,1)S(1)}, bf16[4,64,128]{2,1,0:T(8,128)(2,1)}, u32[]{:S(2)}) copy-start(bf16[4,64,128]{2,1,0:T(8,128)(2,1)} %constant.92.clone.bl_ref) | copy-start | bytes 196612
  62.7 35.8 %copy-start.11 = (bf16[4,64,128]{2,1,0:T(8,128)(2,1)S(1)}, bf16[4,64,128]{2,1,0:T(8,128)(2,1)}, u32[]{:S(2)}) copy-start(bf16[4,64,128]{2,1,0:T(8,128)(2,1)} %constant.91.clone.bh_ref) | copy-start | bytes 196612
  62.7 35.7 %copy-start.12 = (f32[128,128]{1,0:T(8,128)S(1)}, f32[128,128]{1,0:T(8,128)}, u32[]{:S(2)}) copy-start(f32[128,128]{1,0:T(8,128)} %constant.90.clone.wave_ref) | copy-start | bytes 196612
  62.7 35.7 %copy-start.13 = (bf16[128,192]{1,0:T(8,128)(2,1)S(1)}, bf16[128,192]{1,0:T(8,128)(2,1)}, u32[]{:S(2)}) copy-start(bf16[128,192]{1,0:T(8,128)(2,1)} %constant.89.clone.yl_ref) | copy-start | bytes 147460
  62.7 35.7 %copy-start.14 = (bf16[128,192]{1,0:T(8,128)(2,1)S(1)}, bf16[128,192]{1,0:T(8,128)(2,1)}, u32[]{:S(2)}) copy-start(bf16[128,192]{1,0:T(8,128)(2,1)} %constant.88.clone.yh_ref) | copy-start | bytes 147460
  63.8 34.7 %copy-start.1 = (bf16[128,1024]{1,0:T(8,128)(2,1)S(1)}, bf16[128,1024]{1,0:T(8,128)(2,1)}, u32[]{:S(2)}) copy-start(bf16[128,1024]{1,0:T(8,128)(2,1)} %constant.94.clone.tl_ref) | copy-start | bytes 786436
  63.8 34.7 %copy-start.2 = (bf16[128,1024]{1,0:T(8,128)(2,1)S(1)}, bf16[128,1024]{1,0:T(8,128)(2,1)}, u32[]{:S(2)}) copy-start(bf16[128,1024]{1,0:T(8,128)(2,1)} %constant.93.clone.th_ref) | copy-start | bytes 786436
  63.8 34.7 %copy-start.3 = (bf16[1024,128]{1,0:T(8,128)(2,1)S(1)}, bf16[1024,128]{1,0:T(8,128)(2,1)}, u32[]{:S(2)}) copy-start(bf16[1024,128]{1,0:T(8,128)(2,1)} %constant.87.clone.zl_ref) | copy-start | bytes 786436
  121.1 11.3 %copy-start.8 = (bf16[8,32,128]{2,1,0:T(8,128)(2,1)S(1)}, bf16[8,32,128]{2,1,0:T(8,128)(2,1)}, u32[]{:S(2)}) copy-start(bf16[8,32,128]{2,1,0:T(8,128)(2,1)} %constant.96.clone.low_ref) | copy-start | bytes 196612
  121.1 11.3 %copy-start.9 = (bf16[8,32,128]{2,1,0:T(8,128)(2,1)S(1)}, bf16[8,32,128]{2,1,0:T(8,128)(2,1)}, u32[]{:S(2)}) copy-start(bf16[8,32,128]{2,1,0:T(8,128)(2,1)} %constant.95.clone.high_ref) | copy-start | bytes 196612

commit v3 on v2

--- a/solution.py
+++ b/solution.py
@@ -19,6 +19,7 @@
 FIRST, LAST = 4, 28
 KEPT = LAST - FIRST
 LANES = 128
+CHUNK = 9
 GROUP = 16
 PER = LANES // LX
 
@@ -162,6 +163,37 @@
     )
 
 
+def bring_kernel(orb_ref, out_ref):
+    tiles, chunks = LX // 8, LX * LX // LANES
+    lane = iota((8, LANES), 1)
+    line = LX + 2
+    for h in range(2):
+        out_ref[h * line] = jnp.zeros((LX, LANES), F32)
+        out_ref[h * line + line - 1] = jnp.zeros((LX, LANES), F32)
+
+    def bring(c, carry):
+        here = pl.ds(pl.multiple_of(c * LANES, LANES), LANES)
+        for t in range(tiles):
+            rows = slice(8 * t, 8 * t + 8)
+            for h in range(2):
+                v = [orb_ref[4 * h + g, rows, here].astype(F32) for g in range(4)]
+                for y, value in enumerate(swap_four(v, lane)):
+                    out_ref[h * line + 1 + PER * c + y, rows, :] = value
+        return carry
+
+    lax.fori_loop(0, chunks, bring, 0)
+
+
+def bring_orbitals(orbitals):
+    return call(
+        bring_kernel,
+        jax.ShapeDtypeStruct((2 * (LX + 2), LX, LANES), F32),
+        [VMEM],
+        flops=15000000,
+        name="bring",
+    )(orbitals)
+
+
 def filter_kernel(occ_ref, orb_ref, pot_ref, weight_ref, new_ref, send_ref, ya, yb, coef, flat):
     tiles, chunks = LX // 8, LX * LX // LANES
     line = LX + 2
@@ -178,14 +210,10 @@
             buffer[h * line] = jnp.zeros((LX, LANES), F32)
             buffer[h * line + line - 1] = jnp.zeros((LX, LANES), F32)
 
-    def bring(c, carry):
+    def spread(c, carry):
         here = pl.ds(pl.multiple_of(c * LANES, LANES), LANES)
         for t in range(tiles):
             rows = slice(8 * t, 8 * t + 8)
-            for h in range(2):
-                v = [orb_ref[4 * h + g, rows, here].astype(F32) for g in range(4)]
-                for y, value in enumerate(swap_four(v, lane)):
-                    ya[h * line + 1 + PER * c + y, rows, :] = value
             v = scale * pot_ref[rows, here] + shift
             for y in range(PER):
                 value = jnp.where(lane // LX == y, v, 0.0)
@@ -193,9 +221,9 @@
                 coef[PER * c + y, rows, :] = value + pltpu.roll(value, 2 * LX, 1)
         return carry
 
-    lax.fori_loop(0, chunks, bring, 0)
-
-    def advance(src, dst, start):
+    lax.fori_loop(0, chunks, spread, 0)
+
+    def advance(src, before, dst):
         def one(b, carry):
             for yy in range(GROUP):
                 y = GROUP * b + yy
@@ -213,23 +241,23 @@
                         total += pltpu.roll(jnp.where(first_x, below, cur), 7, 0)
                         total += src[at - 1, rows, :] + src[at + 1, rows, :]
                         result = alpha * total + coef[y, rows, :] * cur
-                        if start:
+                        if before is None:
                             dst[at, rows, :] = 0.5 * result
                         else:
-                            dst[at, rows, :] = result - dst[at, rows, :]
+                            dst[at, rows, :] = result - before[at, rows, :]
             return carry
 
         lax.fori_loop(0, LX // GROUP, one, 0)
 
-    advance(ya, yb, True)
+    advance(orb_ref, None, yb)
+    advance(yb, orb_ref, ya)
 
     def two(m, carry):
-        advance(yb, ya, False)
-        advance(ya, yb, False)
+        advance(ya, yb, yb)
+        advance(yb, ya, ya)
         return carry
 
     lax.fori_loop(0, (DEGREE - 2) // 2, two, 0)
-    advance(yb, ya, False)
 
     pairs = [(n, m) for n in range(NORB) for m in range(n + 1)]
 
@@ -334,21 +362,28 @@
 
 def y_kernel(place_ref, got_ref, high_ref, low_ref, send_ref):
     kept = KEPT // PER
+    part = kept // 2
+    chunk = kept + part
     at = place_ref[0]
+    odd = place_ref[3] == 1
     table = (high_ref[at], low_ref[at])
+    folded = []
     for c in range(kept):
         lines = got_ref[pl.ds(c, PARTS * KEPT, stride=kept), :]
         value = dot3(table, halves(lines))
-        for q in range(2):
-            send_ref[pl.ds(q * 2 * kept + c, LX, stride=4 * kept), :] = value[CORE:]
+        folded.append(value[CORE:])
         for q in range(4):
-            send_ref[pl.ds(q * 2 * kept + kept + c, CORE, stride=8 * kept), :] = value[:CORE]
+            send_ref[pl.ds(q * chunk + part + c, CORE, stride=4 * chunk), :] = value[:CORE]
+    for c in range(part):
+        low, high = folded[c], folded[part + c]
+        send_ref[pl.ds(c, LX, stride=2 * chunk), :] = jnp.where(odd, high, low)
+        send_ref[pl.ds(chunk + c, LX, stride=2 * chunk), :] = jnp.where(odd, low, high)
 
 
 def along_y(place, got):
     return call(
         y_kernel,
-        jax.ShapeDtypeStruct((64 * 2 * KEPT // PER, LANES), F32),
+        jax.ShapeDtypeStruct((64 * CHUNK, LANES), F32),
         [SMEM, VMEM, VMEM, VMEM],
         name="along_y",
     )(place, got, *map(jnp.asarray, TABLES["along"]))
@@ -371,13 +406,14 @@
     work,
 ):
     kept = KEPT // PER
-    chunk = 2 * kept
+    part = kept // 2
+    chunk = kept + part
     out_chunk = 6
     wide = PARTS * LANES
     blocks = []
     for k in range(PARTS):
         rows = [
-            got_ref[pl.ds(chunk * k + kept + c, PARTS, stride=chunk * PARTS), :]
+            got_ref[pl.ds(chunk * k + part + c, PARTS, stride=chunk * PARTS), :]
             for c in range(kept)
         ]
         blocks.append(jnp.concatenate(rows, axis=0))
@@ -403,32 +439,32 @@
                 8 * half : 8 * half + 8, k * LANES : (k + 1) * LANES
             ]
     row = iota((8, LANES), 0)
-    lane = iota((8, LANES), 1) % LX
-    inside = (row >= 1) & (row <= kept)
-    upper = row < 4
-    left = lane < LX // 2
-    second = place_ref[2] == 1
-
-    def load(j, k):
-        at = chunk * (PARTS * j + k)
-        return jnp.where(inside, pltpu.roll(got_ref[at : at + 8, :], 1, 0), 0.0)
+    left = iota((8, LANES), 1) % LX < LX // 2
+    half = LX // 2
+    first, second = row < part, place_ref[2] == 1
+
+    def load(i, k):
+        at = chunk * (PARTS * i + k)
+        return jnp.where(first, got_ref[at : at + 8, :], 0.0)
 
     for k in range(PARTS):
-        column = [load(j, k) for j in range(PARTS)]
-        for j in range(PARTS):
-            beside = jnp.where(upper, column[(j + 1) % PARTS], column[(j - 1) % PARTS])
-            at = 8 * (PARTS * j + k)
-            work[at : at + 8, :] = column[j] + pltpu.roll(beside, 4, 0)
-    for j in range(PARTS):
-        line = [work[8 * (PARTS * j + k) : 8 * (PARTS * j + k) + 8, :] for k in range(PARTS)]
+        column = [load(i, k) for i in range(PARTS)]
+        for m in range(PARTS):
+            at = 8 * (PARTS * m + k)
+            work[at : at + 8, :] = pltpu.roll(column[m], 1, 0) + column[m - 1]
+    for m in range(PARTS):
+        after = (m + 1) % PARTS
+        other = second if m % 2 == 0 else jnp.logical_not(second)
+        line = []
+        for k in range(PARTS):
+            here, there = 8 * (PARTS * m + k), 8 * (PARTS * after + k)
+            line.append(jnp.where(other, work[there : there + 8, :], work[here : here + 8, :]))
         for k in range(PARTS):
             beside = jnp.where(left, line[(k + 1) % PARTS], line[(k - 1) % PARTS])
-            half = LX // 2
             value = line[k] + jnp.where(
                 left, pltpu.roll(beside, LANES - half, 1), pltpu.roll(beside, half, 1)
             )
-            value = jnp.where(second, pltpu.roll(value, 4, 0), value)
-            at = out_chunk * (PARTS * j + k) + 2
+            at = out_chunk * (PARTS * m + k) + 2
             send_ref[at : at + 4, :] = value[0:4]
 
 
@@ -468,16 +504,21 @@
     return slater + wigner
 
 
-def window_kernel(got_ref, ion_ref, send_ref, dens_ref, base_ref, work):
+def window_kernel(place_ref, got_ref, ion_ref, send_ref, dens_ref, base_ref, work):
     for half in range(2):
         value = got_ref[pl.ds(half, 64, stride=6), :]
         for s in range(PARTS):
             send_ref[pl.ds(s * LANES + half, 64, stride=2), :] = value
     row, lane = iota((8, LANES), 0), iota((8, LANES), 1)
+    odd = place_ref[3] == 1
     for q in range(2):
         for h in range(4):
             x = 4 * q + h
-            value = got_ref[pl.ds(6 * q + 2 + h, LX, stride=12), :]
+            value = jnp.where(
+                odd,
+                got_ref[pl.ds(6 * (1 - q) + 2 + h, LX, stride=12), :],
+                got_ref[pl.ds(6 * q + 2 + h, LX, stride=12), :],
+            )
             if 2 <= x < 6:
                 for low in range(PER):
                     core = pltpu.roll(value[BUF : BUF + CORE], LANES - LX * low - BUF, 1)
@@ -492,7 +533,7 @@
     base_ref[...] = ion_ref[...] + exchange_correlation(work[...])
 
 
-def on_window(got, ion_ext):
+def on_window(place, got, ion_ext):
     return call(
         window_kernel,
         (
@@ -500,10 +541,10 @@
             jax.ShapeDtypeStruct((CORE, CORE, CORE), F32),
             jax.ShapeDtypeStruct((LX, LX * LX), F32),
         ),
-        [VMEM, VMEM],
+        [SMEM, VMEM, VMEM],
         [pltpu.VMEM((LX, LX * LX), F32)],
         name="on_window",
-    )(got, ion_ext)
+    )(place, got, ion_ext)
 
 
 def last_kernel(place_ref, got_ref, base_ref, high_ref, low_ref, out_ref):
@@ -538,16 +579,45 @@
     return lax.ppermute(last, axis, up), lax.ppermute(first, axis, down)
 
 
+def pack_kernel(pot_ref, ion_ref, own_ref, up_ref, down_ref):
+    lane = iota((CORE, LANES), 1)
+    third = (lane % LX) // BUF
+    for f, ref in enumerate((pot_ref, ion_ref)):
+        rows = slice(CORE * f, CORE * (f + 1))
+        up, down = jnp.zeros((CORE, LANES), F32), jnp.zeros((CORE, LANES), F32)
+        for c in range(PER):
+            value = jnp.zeros((CORE, LANES), F32)
+            for y in range(PER):
+                line = ref[pl.ds(PER * c + y, CORE, stride=CORE), :]
+                line = jnp.concatenate([line, jnp.zeros((CORE, LANES - CORE), F32)], axis=1)
+                value = value + pltpu.roll(line, LX * y + BUF, 1)
+            own_ref[rows, c * LANES : (c + 1) * LANES] = value
+            up = jnp.where(third == c, pltpu.roll(value, (BUF * c - 2 * BUF) % LANES, 1), up)
+            down = jnp.where(third == c, pltpu.roll(value, (BUF * c - BUF) % LANES, 1), down)
+        up_ref[rows, :] = up
+        down_ref[rows, :] = down
+
+
+def merge_kernel(own_ref, before_ref, after_ref, out_ref):
+    third = (iota((2 * CORE, LANES), 1) % LX) // BUF
+    before, after = before_ref[...], after_ref[...]
+    for c in range(PER):
+        here = slice(c * LANES, (c + 1) * LANES)
+        value = jnp.where(third == 0, pltpu.roll(before, (-BUF * c) % LANES, 1), own_ref[:, here])
+        out_ref[:, here] = jnp.where(
+            third == 3, pltpu.roll(after, (3 * BUF - BUF * c) % LANES, 1), value
+        )
+
+
 def refill(fields):
-    both = jnp.stack(fields)
-    count = both.shape[0] * CORE
-    slab = (count, CORE * BUF)
-    before, after = both_sides(
-        both[..., :BUF].reshape(slab), both[..., CORE - BUF :].reshape(slab), "gz"
-    )
-    shape = (len(fields), CORE, CORE, BUF)
-    both = jnp.concatenate([before.reshape(shape), both, after.reshape(shape)], axis=3)
-    both = both.reshape(count, CORE * LX)
+    count = len(fields) * CORE
+    slab = jax.ShapeDtypeStruct((count, LANES), F32)
+    full = jax.ShapeDtypeStruct((count, CORE * LX), F32)
+    own, up, down = call(pack_kernel, (full, slab, slab), [VMEM, VMEM], name="pack")(
+        *[f.reshape(CORE * CORE, CORE) for f in fields]
+    )
+    before, after = both_sides(down, up, "gz")
+    both = call(merge_kernel, full, [VMEM, VMEM, VMEM], name="merge")(own, before, after)
     width = BUF * LX
     before, after = both_sides(both[:, :width], both[:, CORE * LX - width :], "gy")
     both = jnp.concatenate([before, both, after], axis=1).reshape(len(fields), CORE, LX * LX)
@@ -566,17 +636,18 @@
 
 def on_device(orbitals, potential, ion_potential, occupations):
     gy, member = lax.axis_index("gy"), lax.axis_index(("gx", "gz"))
-    place = jnp.stack([gy, member % 4, member % 2]).astype(jnp.int32)
+    place = jnp.stack([gy, member % 4, member % 2, lax.axis_index("gx") % 2]).astype(jnp.int32)
     wave = jnp.asarray(TABLES["wave"])[gy * CORE + member // 4].reshape(1)
+    orbitals = bring_orbitals(orbitals)
     window = refill((potential, ion_potential))
     window, place, wave = lax.optimization_barrier((window, place, wave))
     new_orbitals, send = filtered_set(occupations, orbitals, window[0])
     got = exchange(send, "gy", KEPT * KEPT // PER)
     send = along_y(place, got)
-    got = exchange(send, ("gx", "gz"), 2 * KEPT // PER)
+    got = exchange(send, ("gx", "gz"), CHUNK)
     send = on_plane(place, wave, got)
     got = exchange(send, ("gx", "gz"), 6)
-    send, density, base = on_window(got, window[1])
+    send, density, base = on_window(place, got, window[1])
     got = exchange(send, "gy", LANES)
     new_potential = last_step(place, got, base)
     return (new_orbitals, density, new_potential)

time: 135 us -> 129 us (0.956)
  blocking collectives: 77.8 us -> 69.3 us
  starting transfers between devices: 28.4 us -> 30.6 us
  Pallas kernels: 18.7 us -> 20.6 us
  other arithmetic: 1.54 us -> 0.11 us
    all_to_all x4, blocking collectives: 77.8 us -> 69.3 us  [exchange(): lax.all_to_all(shaped, axis, split_axis=0, concat_axis=0, tiled=True)]
    ppermute x6, starting transfers between devices: 28.4 us -> 30.6 us  [both_sides(): return (lax.ppermute(last, axis, up), lax.ppermute(first, axis, down))]
    pallas_call x1 -> x4, Pallas kernels: 1 us -> 2.55 us  [the longest x1 1.29 us: bring_orbitals(): call(bring_kernel, jax.ShapeDtypeStruct((2 * (LX + 2), LX, LANES), F32),...]
    unnamed x38 -> x36, local copies, waits for them, and re-layouts: 2.36 us -> 2.93 us
  transfers between devices with their start and end apart: 6 -> 6, of which waited for: 2 -> 3; matrix products, arithmetic and copies ran while one was open for 1% -> 1% of each run, Pallas kernels for 0% -> 1%
where the time goes in v3:
time: 129 us; the launch traced here: 128 us
  blocking collectives  69.3 us (54%)
  starting transfers between devices  30.6 us (24%)
  Pallas kernels  20.6 us (16%)
  local copies, waits for them, and re-layouts  4.25 us (3%)
  waiting for transfers between devices  2.62 us (2%)
    all_to_all x4, blocking collectives, exchange(): lax.all_to_all(shaped, axis, split_axis=0, concat_axis=0, tiled=True)  69.3 us
    ppermute x6, starting transfers between devices, both_sides(): return (lax.ppermute(last, axis, up), lax.ppermute(first, axis, down))  30.6 us
    pallas_call x1, Pallas kernels, filtered_set(): call(filter_kernel, (jax.ShapeDtypeStruct((NORB, LX, LX * LX), BF16), jax...  12.5 us
    unnamed x36, local copies, waits for them, and re-layouts  2.93 us
    ppermute x6, waiting for transfers between devices, both_sides(): return (lax.ppermute(last, axis, up), lax.ppermute(first, axis, down))  2.62 us
  transfers between devices with their start and end apart: 6, of which 3 were waited for; matrix products, arithmetic and copies ran while one was open for 1% of the time, Pallas kernels for 1%

profile of v3, /device:TPU:1, one launch (start us, length us, event | category | flops | bytes accessed | tf_op | source)
XLA Modules:
  0.0 128.5 jit_solution(907751744757677146)
XLA Ops:
  0.6 0.9 copy-done.8
  1.5 0.9 copy-done.9
  2.4 0.2 pack.1
  2.7 5.6 %collective-permute-start = (f32[32,128]{1,0:T(8,128)S(1)}, f32[32,128]{1,0:T(8,128)S(1)}, u32[]{:S(2)}, u32[]{:S(2)}) collective-permute-start(f32[32,128]{1,0:T(8,128)S(1)} %get-tuple-element.15), channel_id=1, source_target_pairs={{0,1},{1,2},{2,3},{3,4},{4,5},{5,6},{6,7},{7,0},{8,9},{9,10},{10,1... | collective-permute-start | bytes 49160 | tf_op jit(solution)/shard_map/ppermute | solution.py:579
  8.3 5.1 %collective-permute-start.1 = (f32[32,128]{1,0:T(8,128)S(1)}, f32[32,128]{1,0:T(8,128)S(1)}, u32[]{:S(2)}, u32[]{:S(2)}) collective-permute-start(f32[32,128]{1,0:T(8,128)S(1)} %get-tuple-element.16), channel_id=1, source_target_pairs={{1,0},{2,1},{3,2},{4,3},{5,4},{6,5},{7,6},{0,7},{9,8},{10,9},{11,1... | collective-permute-start | bytes 49160 | tf_op jit(solution)/shard_map/ppermute | solution.py:579
  13.4 0.9 collective-permute-done.1.after_ref
  14.2 0.1 merge.1
  14.3 3.1 %collective-permute-start.2 = (f32[32,256]{1,0:T(8,128)S(1)}, f32[32,256]{1,0:T(8,128)S(1)}, u32[]{:S(2)}, u32[]{:S(2)}) collective-permute-start(f32[32,256]{1,0:T(8,128)S(1)} %get-tuple-element.29), channel_id=1, source_target_pairs={{0,8},{8,16},{16,24},{24,32},{32,40},{40,48},{48,56},{56,0},{1,9},... | collective-permute-start | bytes 98312 | tf_op jit(solution)/shard_map/ppermute | solution.py:579
  17.5 4.3 %collective-permute-start.3 = (f32[32,256]{1,0:T(8,128)S(1)}, f32[32,256]{1,0:T(8,128)S(1)}, u32[]{:S(2)}, u32[]{:S(2)}) collective-permute-start(f32[32,256]{1,0:T(8,128)S(1)} %get-tuple-element.30), channel_id=1, source_target_pairs={{8,0},{16,8},{24,16},{32,24},{40,32},{48,40},{56,48},{0,56},{9,1},... | collective-permute-start | bytes 98312 | tf_op jit(solution)/shard_map/ppermute | solution.py:579
  21.8 1.3 dynamic_slice.3.own_ref
  23.1 1.0 copy-done
  24.1 1.3 %bring.1.orb_ref = f32[68,32,128]{2,1,0:T(8,128)S(1)} custom-call(bf16[8,32,1024]{2,1,0:T(8,128)(2,1)S(1)} %copy-done), custom_call_target="tpu_custom_call" | custom-call | flops 15000000 | bytes 1000000 | tf_op jit(solution)/shard_map/bring/pallas_call | solution.py:188
  25.5 4.0 %collective-permute-start.4 = (f32[2,8,1024]{2,1,0:T(8,128)S(1)}, f32[2,8,1024]{2,1,0:T(8,128)S(1)}, u32[]{:S(2)}, u32[]{:S(2)}) collective-permute-start(f32[2,8,1024]{2,1,0:T(8,128)S(1)} %get-tuple-element.27), channel_id=1, source_target_pairs={{0,64},{64,128},{128,192},{192,256},{256,320},{320,384},{384,448},... | collective-permute-start | bytes 196616 | tf_op jit(solution)/shard_map/ppermute | solution.py:579
  29.5 8.6 %collective-permute-start.5 = (f32[2,8,1024]{2,1,0:T(8,128)S(1)}, f32[2,8,1024]{2,1,0:T(8,128)S(1)}, u32[]{:S(2)}, u32[]{:S(2)}) collective-permute-start(f32[2,8,1024]{2,1,0:T(8,128)S(1)} %get-tuple-element.28), channel_id=1, source_target_pairs={{64,0},{128,64},{192,128},{256,192},{320,256},{384,320},{448,384},... | collective-permute-start | bytes 196616 | tf_op jit(solution)/shard_map/ppermute | solution.py:579
  38.1 0.1 pad_add_fusion.place_ref
  38.2 0.2 collective-permute-done.4
  38.4 1.6 %collective-permute-done.5 = f32[2,8,1024]{2,1,0:T(8,128)S(1)} collective-permute-done((f32[2,8,1024]{2,1,0:T(8,128)S(1)}, f32[2,8,1024]{2,1,0:T(8,128)S(1)}, u32[]{:S(2)}, u32[]{:S(2)}) %collective-permute-start.5) | collective-permute-done | bytes 65568 | tf_op jit(solution)/shard_map/ppermute | solution.py:579
  40.0 0.0 copy-start.5
  40.0 0.0 copy-start.6
  40.0 12.5 %filter.1 = (bf16[8,32,1024]{2,1,0:T(8,128)(2,1)}, f32[1152,128]{1,0:T(8,128)S(1)}) custom-call(f32[8]{0:T(128)S(1)} %copy-done.17, f32[68,32,128]{2,1,0:T(8,128)S(1)} %bring.1.orb_ref, f32[32,1024]{1,0:T(8,128)S(1)} %get-tuple-element.26.pot_ref, f32[32,1024]{1,0:T(8,128)S(1)} %copy-done.7), custom_call_target="tpu_custom_call" | custom-call | flops 60000000 | bytes 1000000 | tf_op jit(solution)/shard_map/filter/pallas_call | solution.py:345
  52.5 12.4 %all_to_all.20 = f32[144,8,128]{2,1,0:T(8,128)S(1)} all-to-all(f32[144,8,128]{2,1,0:T(8,128)S(1)} %bitcast.27), channel_id=1, replica_groups=mesh['gx'=8,'gy'=8,'gz'=8] {'gy'}, dimensions={0} | all-to-all | bytes 1179648 | tf_op jit(solution)/shard_map/all_to_all | solution.py:632
  65.0 0.0 copy-start.12
  65.0 0.0 copy-start.13
  65.0 0.0 copy-start.15
  65.1 0.0 copy-start.16
  65.1 1.0 along_y.1
  66.1 27.1 %all_to_all.21 = f32[576,1,128]{2,1,0:T(1,128)S(1)} all-to-all(f32[576,1,128]{2,1,0:T(1,128)S(1)} %bitcast.24), channel_id=1, replica_groups=mesh['gx'=8,'gy'=8,'gz'=8] {'gx','gz'}, dimensions={0} | all-to-all | bytes 589824 | tf_op jit(solution)/shard_map/all_to_all | solution.py:632
  93.2 2.3 %on_plane.1 = f32[384,128]{1,0:T(8,128)S(1)} custom-call(s32[4]{0:T(128)S(1)} %pad_add_fusion.place_ref, f32[1]{0:T(128)} %dynamic_slice.3.own_ref, f32[576,128]{1,0:T(8,128)S(1)} %bitcast.23, bf16[1024,128]{1,0:T(8,128)(2,1)S(1)} %copy-done.4, bf16[1024,128]{1,0:T(8,128)(2,1)S(1)} %copy-done.3, bf16[128,192]{1,0:T(8,128)(2,1)S(1)} %copy-done.16, ...), custom_call_target="tpu_custom_call" | custom-call | flops 1000000 | bytes 1000000 | tf_op jit(solution)/shard_map/on_plane/pallas_call | solution.py:473
  95.5 18.6 %all_to_all.22 = f32[192,2,128]{2,1,0:T(2,128)S(1)} all-to-all(f32[192,2,128]{2,1,0:T(2,128)S(1)} %bitcast.25), channel_id=1, replica_groups=mesh['gx'=8,'gy'=8,'gz'=8] {'gx','gz'}, dimensions={0} | all-to-all | bytes 393216 | tf_op jit(solution)/shard_map/all_to_all | solution.py:632
  114.1 1.5 %on_window.1 = (f32[1024,128]{1,0:T(8,128)S(1)}, f32[16,16,16]{2,1,0:T(8,128)}, f32[32,1024]{1,0:T(8,128)S(1)}) custom-call(s32[4]{0:T(128)S(1)} %pad_add_fusion.place_ref, f32[384,128]{1,0:T(8,128)S(1)} %bitcast.26, f32[32,1024]{1,0:T(8,128)S(1)} %get-tuple-element.25.ion_ref), custom_call_target="tpu_custom_call" | custom-call | flops 1000000 | bytes 1000000 | tf_op jit(solution)/shard_map/on_window/pallas_call | solution.py:537
  115.6 11.2 %all_to_all.23 = f32[128,8,128]{2,1,0:T(8,128)S(1)} all-to-all(f32[128,8,128]{2,1,0:T(8,128)S(1)} %bitcast.28), channel_id=1, replica_groups=mesh['gx'=8,'gy'=8,'gz'=8] {'gy'}, dimensions={0} | all-to-all | bytes 1048576 | tf_op jit(solution)/shard_map/all_to_all | solution.py:632
  126.8 1.7 %last_step.1 = f32[32,1024]{1,0:T(8,128)} custom-call(s32[4]{0:T(128)S(1)} %pad_add_fusion.place_ref, f32[1024,128]{1,0:T(8,128)S(1)} %bitcast.22, f32[32,1024]{1,0:T(8,128)S(1)} %get-tuple-element.24.base_ref, bf16[8,32,128]{2,1,0:T(8,128)(2,1)S(1)} %copy-done.11, bf16[8,32,128]{2,1,0:T(8,128)(2,1)S(1)} %copy-done.10), custom_call_target="tpu_custom_call" | custom-call | flops 1000000 | bytes 1000000 | tf_op jit(solution)/shard_map/last_step/pallas_call | solution.py:567
  (35 shorter events, 0.1 us)
Async XLA Ops:
  0.6 0.9 copy-start.8
  1.5 0.9 copy-start.9
  2.7 10.7 %collective-permute-start = (f32[32,128]{1,0:T(8,128)S(1)}, f32[32,128]{1,0:T(8,128)S(1)}, u32[]{:S(2)}, u32[]{:S(2)}) collective-permute-start(f32[32,128]{1,0:T(8,128)S(1)} %get-tuple-element.15), channel_id=1, source_target_pairs={{0,1},{1,2},{2,3},{3,4},{4,5},{5,6},{6,7},{7,0},{8,9},{9,10},{10,1... | collective-permute-start | bytes 49160 | tf_op jit(solution)/shard_map/ppermute | solution.py:579
  8.3 6.0 %collective-permute-start.1 = (f32[32,128]{1,0:T(8,128)S(1)}, f32[32,128]{1,0:T(8,128)S(1)}, u32[]{:S(2)}, u32[]{:S(2)}) collective-permute-start(f32[32,128]{1,0:T(8,128)S(1)} %get-tuple-element.16), channel_id=1, source_target_pairs={{1,0},{2,1},{3,2},{4,3},{5,4},{6,5},{7,6},{0,7},{9,8},{10,9},{11,1... | collective-permute-start | bytes 49160 | tf_op jit(solution)/shard_map/ppermute | solution.py:579
  14.3 11.1 %collective-permute-start.2 = (f32[32,256]{1,0:T(8,128)S(1)}, f32[32,256]{1,0:T(8,128)S(1)}, u32[]{:S(2)}, u32[]{:S(2)}) collective-permute-start(f32[32,256]{1,0:T(8,128)S(1)} %get-tuple-element.29), channel_id=1, source_target_pairs={{0,8},{8,16},{16,24},{24,32},{32,40},{40,48},{48,56},{56,0},{1,9},... | collective-permute-start | bytes 98312 | tf_op jit(solution)/shard_map/ppermute | solution.py:579
  17.5 8.0 %collective-permute-start.3 = (f32[32,256]{1,0:T(8,128)S(1)}, f32[32,256]{1,0:T(8,128)S(1)}, u32[]{:S(2)}, u32[]{:S(2)}) collective-permute-start(f32[32,256]{1,0:T(8,128)S(1)} %get-tuple-element.30), channel_id=1, source_target_pairs={{8,0},{16,8},{24,16},{32,24},{40,32},{48,40},{56,48},{0,56},{9,1},... | collective-permute-start | bytes 98312 | tf_op jit(solution)/shard_map/ppermute | solution.py:579
  23.1 1.0 copy-start
  25.4 14.6 %copy-start.7 = (f32[32,1024]{1,0:T(8,128)S(1)}, f32[32,1024]{1,0:T(8,128)}, u32[]{:S(2)}) copy-start(f32[32,1024]{1,0:T(8,128)} %constant.87.clone.weight_ref) | copy-start | bytes 393220
  25.4 14.6 %copy-start.17 = (f32[8]{0:T(128)S(1)}, f32[8]{0:T(128)}, u32[]{:S(2)}) copy-start(f32[8]{0:T(128)} %occ_ref.1) | copy-start | bytes 100
  25.5 12.9 %collective-permute-start.4 = (f32[2,8,1024]{2,1,0:T(8,128)S(1)}, f32[2,8,1024]{2,1,0:T(8,128)S(1)}, u32[]{:S(2)}, u32[]{:S(2)}) collective-permute-start(f32[2,8,1024]{2,1,0:T(8,128)S(1)} %get-tuple-element.27), channel_id=1, source_target_pairs={{0,64},{64,128},{128,192},{192,256},{256,320},{320,384},{384,448},... | collective-permute-start | bytes 196616 | tf_op jit(solution)/shard_map/ppermute | solution.py:579
  29.5 10.4 %collective-permute-start.5 = (f32[2,8,1024]{2,1,0:T(8,128)S(1)}, f32[2,8,1024]{2,1,0:T(8,128)S(1)}, u32[]{:S(2)}, u32[]{:S(2)}) collective-permute-start(f32[2,8,1024]{2,1,0:T(8,128)S(1)} %get-tuple-element.28), channel_id=1, source_target_pairs={{64,0},{128,64},{192,128},{256,192},{320,256},{384,320},{448,384},... | collective-permute-start | bytes 196616 | tf_op jit(solution)/shard_map/ppermute | solution.py:579
  40.0 25.1 %copy-start.5 = (bf16[8,48,192]{2,1,0:T(8,128)(2,1)S(1)}, bf16[8,48,192]{2,1,0:T(8,128)(2,1)}, u32[]{:S(2)}) copy-start(bf16[8,48,192]{2,1,0:T(8,128)(2,1)} %constant.89.clone.low_ref) | copy-start | bytes 442372
  40.0 25.1 %copy-start.6 = (bf16[8,48,192]{2,1,0:T(8,128)(2,1)S(1)}, bf16[8,48,192]{2,1,0:T(8,128)(2,1)}, u32[]{:S(2)}) copy-start(bf16[8,48,192]{2,1,0:T(8,128)(2,1)} %constant.88.clone.high_ref) | copy-start | bytes 442372
  65.0 28.1 %copy-start.1 = (bf16[128,1024]{1,0:T(8,128)(2,1)S(1)}, bf16[128,1024]{1,0:T(8,128)(2,1)}, u32[]{:S(2)}) copy-start(bf16[128,1024]{1,0:T(8,128)(2,1)} %constant.98.clone.tl_ref) | copy-start | bytes 786436
  65.0 28.1 %copy-start.2 = (bf16[128,1024]{1,0:T(8,128)(2,1)S(1)}, bf16[128,1024]{1,0:T(8,128)(2,1)}, u32[]{:S(2)}) copy-start(bf16[128,1024]{1,0:T(8,128)(2,1)} %constant.97.clone.th_ref) | copy-start | bytes 786436
  65.0 28.1 %copy-start.3 = (bf16[1024,128]{1,0:T(8,128)(2,1)S(1)}, bf16[1024,128]{1,0:T(8,128)(2,1)}, u32[]{:S(2)}) copy-start(bf16[1024,128]{1,0:T(8,128)(2,1)} %constant.91.clone.zl_ref) | copy-start | bytes 786436
  65.0 28.1 %copy-start.4 = (bf16[1024,128]{1,0:T(8,128)(2,1)S(1)}, bf16[1024,128]{1,0:T(8,128)(2,1)}, u32[]{:S(2)}) copy-start(bf16[1024,128]{1,0:T(8,128)(2,1)} %constant.90.clone.zh_ref) | copy-start | bytes 786436
  65.0 28.2 %copy-start.12 = (bf16[4,64,128]{2,1,0:T(8,128)(2,1)S(1)}, bf16[4,64,128]{2,1,0:T(8,128)(2,1)}, u32[]{:S(2)}) copy-start(bf16[4,64,128]{2,1,0:T(8,128)(2,1)} %constant.96.clone.bl_ref) | copy-start | bytes 196612
  65.0 28.2 %copy-start.13 = (bf16[4,64,128]{2,1,0:T(8,128)(2,1)S(1)}, bf16[4,64,128]{2,1,0:T(8,128)(2,1)}, u32[]{:S(2)}) copy-start(bf16[4,64,128]{2,1,0:T(8,128)(2,1)} %constant.95.clone.bh_ref) | copy-start | bytes 196612
  65.0 28.1 %copy-start.14 = (f32[128,128]{1,0:T(8,128)S(1)}, f32[128,128]{1,0:T(8,128)}, u32[]{:S(2)}) copy-start(f32[128,128]{1,0:T(8,128)} %constant.94.clone.wave_ref) | copy-start | bytes 196612
  65.0 28.1 %copy-start.15 = (bf16[128,192]{1,0:T(8,128)(2,1)S(1)}, bf16[128,192]{1,0:T(8,128)(2,1)}, u32[]{:S(2)}) copy-start(bf16[128,192]{1,0:T(8,128)(2,1)} %constant.93.clone.yl_ref) | copy-start | bytes 147460
  65.1 28.1 %copy-start.16 = (bf16[128,192]{1,0:T(8,128)(2,1)S(1)}, bf16[128,192]{1,0:T(8,128)(2,1)}, u32[]{:S(2)}) copy-start(bf16[128,192]{1,0:T(8,128)(2,1)} %constant.92.clone.yh_ref) | copy-start | bytes 147460
  95.5 31.3 %copy-start.10 = (bf16[8,32,128]{2,1,0:T(8,128)(2,1)S(1)}, bf16[8,32,128]{2,1,0:T(8,128)(2,1)}, u32[]{:S(2)}) copy-start(bf16[8,32,128]{2,1,0:T(8,128)(2,1)} %constant.100.clone.low_ref) | copy-start | bytes 196612
  95.5 31.3 %copy-start.11 = (bf16[8,32,128]{2,1,0:T(8,128)(2,1)S(1)}, bf16[8,32,128]{2,1,0:T(8,128)(2,1)}, u32[]{:S(2)}) copy-start(bf16[8,32,128]{2,1,0:T(8,128)(2,1)} %constant.99.clone.high_ref) | copy-start | bytes 196612

commit v4 on v3

--- a/solution.py
+++ b/solution.py
@@ -32,7 +32,7 @@
 
 F32, BF16 = jnp.float32, jnp.bfloat16
 VMEM = pl.BlockSpec(memory_space=pltpu.VMEM)
-SMEM = pl.BlockSpec(memory_space=pltpu.SMEM)
+HBM = pl.BlockSpec(memory_space=pltpu.HBM)
 INTERPRET = False
 
 
@@ -98,7 +98,7 @@
         y_table=_pair(y_table),
         y_back=_pair(back),
         last=_pair(last),
-        wave=wave.astype(np.float32),
+        wave=np.repeat(wave.astype(np.float32)[:, None], LANES, axis=1),
         wave_yz=(wave[:, None] + wave[None, :]).astype(np.float32),
     )
 
@@ -308,6 +308,7 @@
     wide = {pair: jnp.broadcast_to(inverse[pair], (8, LANES)) for pair in pairs}
 
     kept = KEPT // PER
+    occ = [jnp.broadcast_to(occ_ref[n : n + 1, :], (8, LANES)) for n in range(NORB)]
 
     def normal(t, carry):
         rows = pl.ds(pl.multiple_of(8 * t, 8), 8)
@@ -320,7 +321,7 @@
                 for m in range(1, n + 1):
                     value = value + wide[n, m] * f[m]
                 flat[n, rows, here] = value
-                total = total + occ_ref[n] * (value * value)
+                total = total + occ[n] * (value * value)
             if 1 <= c <= kept:
                 coef[c, rows, :] = swap_inner(total * weight_ref[rows, here], row, lane)
         return carry
@@ -348,7 +349,7 @@
             jax.ShapeDtypeStruct((NORB, LX, LX * LX), BF16),
             jax.ShapeDtypeStruct((PARTS * KEPT * KEPT // PER, LANES), F32),
         ),
-        [SMEM, VMEM, VMEM, VMEM],
+        [VMEM, VMEM, VMEM, VMEM],
         [
             pltpu.VMEM((2 * (LX + 2), LX, LANES), F32),
             pltpu.VMEM((2 * (LX + 2), LX, LANES), F32),
@@ -360,12 +361,12 @@
     )(occupations, orbitals, potential_ext, jnp.asarray(WEIGHT))
 
 
-def y_kernel(place_ref, got_ref, high_ref, low_ref, send_ref):
+def y_kernel(got_ref, high_ref, low_ref, send_ref):
     kept = KEPT // PER
     part = kept // 2
     chunk = kept + part
-    at = place_ref[0]
-    odd = place_ref[3] == 1
+    at = lax.axis_index("gy")
+    odd = lax.rem(lax.axis_index("gx"), 2) == 1
     table = (high_ref[at], low_ref[at])
     folded = []
     for c in range(kept):
@@ -380,24 +381,23 @@
         send_ref[pl.ds(chunk + c, LX, stride=2 * chunk), :] = jnp.where(odd, low, high)
 
 
-def along_y(place, got):
+def along_y(got):
     return call(
         y_kernel,
         jax.ShapeDtypeStruct((64 * CHUNK, LANES), F32),
-        [SMEM, VMEM, VMEM, VMEM],
+        [VMEM, VMEM, VMEM],
         name="along_y",
-    )(place, got, *map(jnp.asarray, TABLES["along"]))
+    )(got, *map(jnp.asarray, TABLES["along"]))
 
 
 def plane_kernel(
-    place_ref,
-    own_ref,
     got_ref,
     zh_ref,
     zl_ref,
     yh_ref,
     yl_ref,
     wave_ref,
+    own_ref,
     bh_ref,
     bl_ref,
     th_ref,
@@ -422,11 +422,13 @@
     spread = jnp.concatenate([jnp.where(which == y, lines, 0.0) for y in range(PER)], axis=0)
     along_z = dot3(halves(spread), (zh_ref[...], zl_ref[...]))
     spectrum = dot3((yh_ref[...], yl_ref[...]), halves(along_z))
-    eigen = wave_ref[...] + own_ref[0]
+    member = lax.axis_index("gx") * PARTS + lax.axis_index("gz")
+    number = lax.axis_index("gy") * CORE + lax.div(member, 4)
+    eigen = wave_ref[...] + own_ref[pl.ds(number, 1), :]
     positive = eigen > 0.0
     green = jnp.where(positive, 4.0 * math.pi / jnp.where(positive, eigen, 1.0), 0.0)
     spectrum = spectrum * green
-    quarter = place_ref[1]
+    quarter = lax.rem(member, 4)
     lines = dot3((bh_ref[quarter], bl_ref[quarter]), halves(spectrum))
     spread = dot3(halves(lines), (th_ref[...], tl_ref[...]))
     which = (iota((16, wide), 1) % LANES) // LX
@@ -441,7 +443,7 @@
     row = iota((8, LANES), 0)
     left = iota((8, LANES), 1) % LX < LX // 2
     half = LX // 2
-    first, second = row < part, place_ref[2] == 1
+    first, second = row < part, lax.rem(member, 2) == 1
 
     def load(i, k):
         at = chunk * (PARTS * i + k)
@@ -468,21 +470,20 @@
             send_ref[at : at + 4, :] = value[0:4]
 
 
-def on_plane(place, wave, got):
+def on_plane(got):
     t = TABLES
     return call(
         plane_kernel,
         jax.ShapeDtypeStruct((64 * 6, LANES), F32),
-        [SMEM, SMEM] + [VMEM] * 10,
+        [VMEM] * 11,
         [pltpu.VMEM((64 * 8, LANES), F32)],
         name="on_plane",
     )(
-        place,
-        wave,
         got,
         *map(jnp.asarray, t["z_table"]),
         *map(jnp.asarray, t["y_table"]),
         jnp.asarray(t["wave_yz"]),
+        jnp.asarray(t["wave"]),
         *map(jnp.asarray, t["y_back"]),
         *map(jnp.asarray, t["z_back"]),
     )
@@ -504,13 +505,13 @@
     return slater + wigner
 
 
-def window_kernel(place_ref, got_ref, ion_ref, send_ref, dens_ref, base_ref, work):
+def window_kernel(got_ref, ion_ref, send_ref, dens_ref, base_ref, work):
     for half in range(2):
         value = got_ref[pl.ds(half, 64, stride=6), :]
         for s in range(PARTS):
             send_ref[pl.ds(s * LANES + half, 64, stride=2), :] = value
     row, lane = iota((8, LANES), 0), iota((8, LANES), 1)
-    odd = place_ref[3] == 1
+    odd = lax.rem(lax.axis_index("gx"), 2) == 1
     for q in range(2):
         for h in range(4):
             x = 4 * q + h
@@ -533,7 +534,7 @@
     base_ref[...] = ion_ref[...] + exchange_correlation(work[...])
 
 
-def on_window(place, got, ion_ext):
+def on_window(got, ion_ext):
     return call(
         window_kernel,
         (
@@ -541,14 +542,14 @@
             jax.ShapeDtypeStruct((CORE, CORE, CORE), F32),
             jax.ShapeDtypeStruct((LX, LX * LX), F32),
         ),
-        [SMEM, VMEM, VMEM],
+        [VMEM, VMEM],
         [pltpu.VMEM((LX, LX * LX), F32)],
         name="on_window",
-    )(place, got, ion_ext)
-
-
-def last_kernel(place_ref, got_ref, base_ref, high_ref, low_ref, out_ref):
-    at = place_ref[0]
+    )(got, ion_ext)
+
+
+def last_kernel(got_ref, base_ref, high_ref, low_ref, out_ref):
+    at = lax.axis_index("gy")
     table = (high_ref[at], low_ref[at])
     row, lane = iota((8, LANES), 0), iota((8, LANES), 1)
     for x in range(8):
@@ -563,13 +564,13 @@
                 out_ref[rows, here] = base_ref[rows, here] + piece[PER * half : PER * half + PER]
 
 
-def last_step(place, got, base):
+def last_step(got, base):
     return call(
         last_kernel,
         jax.ShapeDtypeStruct((LX, LX * LX), F32),
-        [SMEM, VMEM, VMEM, VMEM, VMEM],
+        [VMEM, VMEM, VMEM, VMEM],
         name="last_step",
-    )(place, got, base, *map(jnp.asarray, TABLES["last"]))
+    )(got, base, *map(jnp.asarray, TABLES["last"]))
 
 
 def both_sides(first, last, axis):
@@ -579,7 +580,15 @@
     return lax.ppermute(last, axis, up), lax.ppermute(first, axis, down)
 
 
-def pack_kernel(pot_ref, ion_ref, own_ref, up_ref, down_ref):
+def pack_kernel(pot_hbm, ion_hbm, own_ref, up_ref, down_ref, pot_ref, ion_ref, sems):
+    copies = [
+        pltpu.make_async_copy(source, target, sems.at[f])
+        for f, (source, target) in enumerate(((pot_hbm, pot_ref), (ion_hbm, ion_ref)))
+    ]
+    for copy in copies:
+        copy.start()
+    for copy in copies:
+        copy.wait()
     lane = iota((CORE, LANES), 1)
     third = (lane % LX) // BUF
     for f, ref in enumerate((pot_ref, ion_ref)):
@@ -609,20 +618,26 @@
         )
 
 
-def refill(fields):
-    count = len(fields) * CORE
+def refill(potential, ion_potential, orbitals, wide_occ):
+    fields = 2
+    count = fields * CORE
     slab = jax.ShapeDtypeStruct((count, LANES), F32)
     full = jax.ShapeDtypeStruct((count, CORE * LX), F32)
-    own, up, down = call(pack_kernel, (full, slab, slab), [VMEM, VMEM], name="pack")(
-        *[f.reshape(CORE * CORE, CORE) for f in fields]
+    lines = pltpu.VMEM((CORE * CORE, CORE), F32)
+    scratch = [lines, lines, pltpu.SemaphoreType.DMA((2,))]
+    own, up, down = call(pack_kernel, (full, slab, slab), [HBM, HBM], scratch, name="pack")(
+        *[f.reshape(CORE * CORE, CORE) for f in (potential, ion_potential)]
     )
     before, after = both_sides(down, up, "gz")
     both = call(merge_kernel, full, [VMEM, VMEM, VMEM], name="merge")(own, before, after)
     width = BUF * LX
     before, after = both_sides(both[:, :width], both[:, CORE * LX - width :], "gy")
-    both = jnp.concatenate([before, both, after], axis=1).reshape(len(fields), CORE, LX * LX)
+    both = jnp.concatenate([before, both, after], axis=1).reshape(fields, CORE, LX * LX)
+    both, orbitals, wide_occ = lax.optimization_barrier((both, orbitals, wide_occ))
     before, after = both_sides(both[:, :BUF], both[:, CORE - BUF :], "gx")
-    return jnp.concatenate([before, both, after], axis=1)
+    brought = bring_orbitals(orbitals)
+    whole = jnp.concatenate([before, both, after], axis=1)
+    return whole[0], whole[1], brought, wide_occ
 
 
 def exchange(value, axis, rows):
@@ -635,21 +650,17 @@
 
 
 def on_device(orbitals, potential, ion_potential, occupations):
-    gy, member = lax.axis_index("gy"), lax.axis_index(("gx", "gz"))
-    place = jnp.stack([gy, member % 4, member % 2, lax.axis_index("gx") % 2]).astype(jnp.int32)
-    wave = jnp.asarray(TABLES["wave"])[gy * CORE + member // 4].reshape(1)
-    orbitals = bring_orbitals(orbitals)
-    window = refill((potential, ion_potential))
-    window, place, wave = lax.optimization_barrier((window, place, wave))
-    new_orbitals, send = filtered_set(occupations, orbitals, window[0])
+    wide_occ = jnp.broadcast_to(occupations[:, None], (NORB, LANES))
+    pot_ext, ion_ext, brought, wide_occ = refill(potential, ion_potential, orbitals, wide_occ)
+    new_orbitals, send = filtered_set(wide_occ, brought, pot_ext)
     got = exchange(send, "gy", KEPT * KEPT // PER)
-    send = along_y(place, got)
+    send = along_y(got)
     got = exchange(send, ("gx", "gz"), CHUNK)
-    send = on_plane(place, wave, got)
+    send = on_plane(got)
     got = exchange(send, ("gx", "gz"), 6)
-    send, density, base = on_window(place, got, window[1])
+    send, density, base = on_window(got, ion_ext)
     got = exchange(send, "gy", LANES)
-    new_potential = last_step(place, got, base)
+    new_potential = last_step(got, base)
     return (new_orbitals, density, new_potential)
 
 

time: 129 us -> 127 us (0.984)
  blocking collectives: 69.3 us -> 72.5 us
  Pallas kernels: 20.6 us -> 17.6 us
  local copies, waits for them, and re-layouts: 4.25 us -> 2.74 us
    all_to_all x4, blocking collectives: 69.3 us -> 72.5 us  [exchange(): lax.all_to_all(shaped, axis, split_axis=0, concat_axis=0, tiled=True)]
    pallas_call x4, Pallas kernels: 5.14 us -> 3.25 us  [the longest x1 1.14 us: last_step(): call(last_kernel, jax.ShapeDtypeStruct((LX, LX * LX), F32), [VMEM, VMEM,...]
    unnamed x36 -> x38, local copies, waits for them, and re-layouts: 2.93 us -> 1.97 us
  transfers between devices with their start and end apart: 6 -> 6, of which waited for: 3 -> 2; matrix products, arithmetic and copies ran while one was open for 1% -> 0% of each run, Pallas kernels for 1% -> 1%
where the time goes in v4:
time: 127 us; the launch traced here: 126 us
  blocking collectives  72.5 us (57%)
  starting transfers between devices  30.8 us (24%)
  Pallas kernels  17.6 us (14%)
  local copies, waits for them, and re-layouts  2.74 us (2%)
  waiting for transfers between devices  1.87 us (1%)
    all_to_all x4, blocking collectives, exchange(): lax.all_to_all(shaped, axis, split_axis=0, concat_axis=0, tiled=True)  72.5 us
    ppermute x6, starting transfers between devices, both_sides(): return (lax.ppermute(last, axis, up), lax.ppermute(first, axis, down))  30.8 us
    pallas_call x1, Pallas kernels, filtered_set(): call(filter_kernel, (jax.ShapeDtypeStruct((NORB, LX, LX * LX), BF16), jax...  12 us
  transfers between devices with their start and end apart: 6, of which 2 were waited for; matrix products, arithmetic and copies ran while one was open for 0% of the time, Pallas kernels for 1%

profile of v4, /device:TPU:1, one launch (start us, length us, event | category | flops | bytes accessed | tf_op | source)
XLA Modules:
  0.0 126.4 jit_solution(2189727556238995292)
XLA Ops:
  0.7 1.0 copy-done.7
  1.6 0.9 copy-done.8
  2.5 0.5 pack.1
  3.1 5.6 %collective-permute-start = (f32[32,128]{1,0:T(8,128)S(1)}, f32[32,128]{1,0:T(8,128)S(1)}, u32[]{:S(2)}, u32[]{:S(2)}) collective-permute-start(f32[32,128]{1,0:T(8,128)S(1)} %get-tuple-element.15), channel_id=1, source_target_pairs={{0,1},{1,2},{2,3},{3,4},{4,5},{5,6},{6,7},{7,0},{8,9},{9,10},{10,1... | collective-permute-start | bytes 49160 | tf_op jit(solution)/shard_map/ppermute | solution.py:580
  8.7 5.1 %collective-permute-start.1 = (f32[32,128]{1,0:T(8,128)S(1)}, f32[32,128]{1,0:T(8,128)S(1)}, u32[]{:S(2)}, u32[]{:S(2)}) collective-permute-start(f32[32,128]{1,0:T(8,128)S(1)} %get-tuple-element.16), channel_id=1, source_target_pairs={{1,0},{2,1},{3,2},{4,3},{5,4},{6,5},{7,6},{0,7},{9,8},{10,9},{11,1... | collective-permute-start | bytes 49160 | tf_op jit(solution)/shard_map/ppermute | solution.py:580
  13.8 0.9 collective-permute-done.1.after_ref
  14.6 0.1 merge.1
  14.7 3.1 %collective-permute-start.2 = (f32[32,256]{1,0:T(8,128)S(1)}, f32[32,256]{1,0:T(8,128)S(1)}, u32[]{:S(2)}, u32[]{:S(2)}) collective-permute-start(f32[32,256]{1,0:T(8,128)S(1)} %get-tuple-element.29), channel_id=1, source_target_pairs={{0,8},{8,16},{16,24},{24,32},{32,40},{40,48},{48,56},{56,0},{1,9},... | collective-permute-start | bytes 98312 | tf_op jit(solution)/shard_map/ppermute | solution.py:580
  17.9 4.3 %collective-permute-start.3 = (f32[32,256]{1,0:T(8,128)S(1)}, f32[32,256]{1,0:T(8,128)S(1)}, u32[]{:S(2)}, u32[]{:S(2)}) collective-permute-start(f32[32,256]{1,0:T(8,128)S(1)} %get-tuple-element.30), channel_id=1, source_target_pairs={{8,0},{16,8},{24,16},{32,24},{40,32},{48,40},{56,48},{0,56},{9,1},... | collective-permute-start | bytes 98312 | tf_op jit(solution)/shard_map/ppermute | solution.py:580
  22.1 1.0 collective-permute-done.3
  23.2 0.7 broadcast_in_dim.2.occ_ref
  23.9 4.0 %collective-permute-start.4 = (f32[2,8,1024]{2,1,0:T(8,128)S(1)}, f32[2,8,1024]{2,1,0:T(8,128)S(1)}, u32[]{:S(2)}, u32[]{:S(2)}) collective-permute-start(f32[2,8,1024]{2,1,0:T(8,128)S(1)} %get-tuple-element.28), channel_id=1, source_target_pairs={{0,64},{64,128},{128,192},{192,256},{256,320},{320,384},{384,448},... | collective-permute-start | bytes 196616 | tf_op jit(solution)/shard_map/ppermute | solution.py:580
  27.9 0.0 copy-start.9
  27.9 8.7 %collective-permute-start.5 = (f32[2,8,1024]{2,1,0:T(8,128)S(1)}, f32[2,8,1024]{2,1,0:T(8,128)S(1)}, u32[]{:S(2)}, u32[]{:S(2)}) collective-permute-start(f32[2,8,1024]{2,1,0:T(8,128)S(1)} %get-tuple-element.27), channel_id=1, source_target_pairs={{64,0},{128,64},{192,128},{256,192},{320,256},{384,320},{448,384},... | collective-permute-start | bytes 196616 | tf_op jit(solution)/shard_map/ppermute | solution.py:580
  36.7 1.3 %bring.1.orb_ref = f32[68,32,128]{2,1,0:T(8,128)S(1)} custom-call(bf16[8,32,1024]{2,1,0:T(8,128)(2,1)S(1)} %copy-done), custom_call_target="tpu_custom_call" | custom-call | flops 15000000 | bytes 1000000 | tf_op jit(solution)/shard_map/bring/pallas_call | solution.py:188
  38.0 0.0 copy-start.5
  38.1 12.0 %filter.1 = (bf16[8,32,1024]{2,1,0:T(8,128)(2,1)}, f32[1152,128]{1,0:T(8,128)S(1)}) custom-call(f32[8,128]{1,0:T(8,128)S(1)} %broadcast_in_dim.2.occ_ref, f32[68,32,128]{2,1,0:T(8,128)S(1)} %bring.1.orb_ref, f32[32,1024]{1,0:T(8,128)S(1)} %get-tuple-element.26.pot_ref, f32[32,1024]{1,0:T(8,128)S(1)} %copy-done.9), custom_call_target="tpu_custom_call" | custom-call | flops 60000000 | bytes 1000000 | tf_op jit(solution)/shard_map/filter/pallas_call | solution.py:346
  50.1 14.3 %all_to_all.20 = f32[144,8,128]{2,1,0:T(8,128)S(1)} all-to-all(f32[144,8,128]{2,1,0:T(8,128)S(1)} %bitcast.23), channel_id=1, replica_groups=mesh['gx'=8,'gy'=8,'gz'=8] {'gy'}, dimensions={0} | all-to-all | bytes 1179648 | tf_op jit(solution)/shard_map/all_to_all | solution.py:647
  64.4 0.0 copy-start.12
  64.4 0.0 copy-start.13
  64.4 0.0 copy-start.14
  64.4 0.0 copy-start.15
  64.4 0.0 copy-start.16
  64.4 0.0 copy-start.17
  64.5 0.4 along_y.1
  64.9 28.4 %all_to_all.21 = f32[576,1,128]{2,1,0:T(1,128)S(1)} all-to-all(f32[576,1,128]{2,1,0:T(1,128)S(1)} %bitcast.19), channel_id=1, replica_groups=mesh['gx'=8,'gy'=8,'gz'=8] {'gx','gz'}, dimensions={0} | all-to-all | bytes 589824 | tf_op jit(solution)/shard_map/all_to_all | solution.py:647
  93.4 1.1 on_plane.1
  94.5 0.0 copy-start.10
  94.5 18.6 %all_to_all.22 = f32[192,2,128]{2,1,0:T(2,128)S(1)} all-to-all(f32[192,2,128]{2,1,0:T(2,128)S(1)} %bitcast.21), channel_id=1, replica_groups=mesh['gx'=8,'gy'=8,'gz'=8] {'gx','gz'}, dimensions={0} | all-to-all | bytes 393216 | tf_op jit(solution)/shard_map/all_to_all | solution.py:647
  113.1 1.0 on_window.1
  114.1 11.2 %all_to_all.23 = f32[128,8,128]{2,1,0:T(8,128)S(1)} all-to-all(f32[128,8,128]{2,1,0:T(8,128)S(1)} %bitcast.24), channel_id=1, replica_groups=mesh['gx'=8,'gy'=8,'gz'=8] {'gy'}, dimensions={0} | all-to-all | bytes 1048576 | tf_op jit(solution)/shard_map/all_to_all | solution.py:647
  125.3 1.1 last_step.1
  (36 shorter events, 0.1 us)
Async XLA Ops:
  0.6 36.0 %copy-start = (bf16[8,32,1024]{2,1,0:T(8,128)(2,1)S(1)}, bf16[8,32,1024]{2,1,0:T(8,128)(2,1)}, u32[]{:S(2)}) copy-start(bf16[8,32,1024]{2,1,0:T(8,128)(2,1)} %orb_ref) | copy-start | bytes 1572868
  0.6 1.0 copy-start.7
  1.6 0.9 copy-start.8
  3.1 10.7 %collective-permute-start = (f32[32,128]{1,0:T(8,128)S(1)}, f32[32,128]{1,0:T(8,128)S(1)}, u32[]{:S(2)}, u32[]{:S(2)}) collective-permute-start(f32[32,128]{1,0:T(8,128)S(1)} %get-tuple-element.15), channel_id=1, source_target_pairs={{0,1},{1,2},{2,3},{3,4},{4,5},{5,6},{6,7},{7,0},{8,9},{9,10},{10,1... | collective-permute-start | bytes 49160 | tf_op jit(solution)/shard_map/ppermute | solution.py:580
  8.7 6.0 %collective-permute-start.1 = (f32[32,128]{1,0:T(8,128)S(1)}, f32[32,128]{1,0:T(8,128)S(1)}, u32[]{:S(2)}, u32[]{:S(2)}) collective-permute-start(f32[32,128]{1,0:T(8,128)S(1)} %get-tuple-element.16), channel_id=1, source_target_pairs={{1,0},{2,1},{3,2},{4,3},{5,4},{6,5},{7,6},{0,7},{9,8},{10,9},{11,1... | collective-permute-start | bytes 49160 | tf_op jit(solution)/shard_map/ppermute | solution.py:580
  14.7 7.4 %collective-permute-start.2 = (f32[32,256]{1,0:T(8,128)S(1)}, f32[32,256]{1,0:T(8,128)S(1)}, u32[]{:S(2)}, u32[]{:S(2)}) collective-permute-start(f32[32,256]{1,0:T(8,128)S(1)} %get-tuple-element.29), channel_id=1, source_target_pairs={{0,8},{8,16},{16,24},{24,32},{32,40},{40,48},{48,56},{56,0},{1,9},... | collective-permute-start | bytes 98312 | tf_op jit(solution)/shard_map/ppermute | solution.py:580
  17.9 5.3 %collective-permute-start.3 = (f32[32,256]{1,0:T(8,128)S(1)}, f32[32,256]{1,0:T(8,128)S(1)}, u32[]{:S(2)}, u32[]{:S(2)}) collective-permute-start(f32[32,256]{1,0:T(8,128)S(1)} %get-tuple-element.30), channel_id=1, source_target_pairs={{8,0},{16,8},{24,16},{32,24},{40,32},{48,40},{56,48},{0,56},{9,1},... | collective-permute-start | bytes 98312 | tf_op jit(solution)/shard_map/ppermute | solution.py:580
  23.9 14.1 %collective-permute-start.4 = (f32[2,8,1024]{2,1,0:T(8,128)S(1)}, f32[2,8,1024]{2,1,0:T(8,128)S(1)}, u32[]{:S(2)}, u32[]{:S(2)}) collective-permute-start(f32[2,8,1024]{2,1,0:T(8,128)S(1)} %get-tuple-element.28), channel_id=1, source_target_pairs={{0,64},{64,128},{128,192},{192,256},{256,320},{320,384},{384,448},... | collective-permute-start | bytes 196616 | tf_op jit(solution)/shard_map/ppermute | solution.py:580
  27.9 10.1 %copy-start.9 = (f32[32,1024]{1,0:T(8,128)S(1)}, f32[32,1024]{1,0:T(8,128)}, u32[]{:S(2)}) copy-start(f32[32,1024]{1,0:T(8,128)} %constant.30.clone.weight_ref) | copy-start | bytes 393220
  27.9 10.1 %collective-permute-start.5 = (f32[2,8,1024]{2,1,0:T(8,128)S(1)}, f32[2,8,1024]{2,1,0:T(8,128)S(1)}, u32[]{:S(2)}, u32[]{:S(2)}) collective-permute-start(f32[2,8,1024]{2,1,0:T(8,128)S(1)} %get-tuple-element.27), channel_id=1, source_target_pairs={{64,0},{128,64},{192,128},{256,192},{320,256},{384,320},{448,384},... | collective-permute-start | bytes 196616 | tf_op jit(solution)/shard_map/ppermute | solution.py:580
  38.0 26.4 %copy-start.5 = (bf16[8,48,192]{2,1,0:T(8,128)(2,1)S(1)}, bf16[8,48,192]{2,1,0:T(8,128)(2,1)}, u32[]{:S(2)}) copy-start(bf16[8,48,192]{2,1,0:T(8,128)(2,1)} %constant.32.clone.low_ref) | copy-start | bytes 442372
  38.1 26.4 %copy-start.6 = (bf16[8,48,192]{2,1,0:T(8,128)(2,1)S(1)}, bf16[8,48,192]{2,1,0:T(8,128)(2,1)}, u32[]{:S(2)}) copy-start(bf16[8,48,192]{2,1,0:T(8,128)(2,1)} %constant.31.clone.high_ref) | copy-start | bytes 442372
  64.4 28.9 %copy-start.1 = (bf16[128,1024]{1,0:T(8,128)(2,1)S(1)}, bf16[128,1024]{1,0:T(8,128)(2,1)}, u32[]{:S(2)}) copy-start(bf16[128,1024]{1,0:T(8,128)(2,1)} %constant.42.clone.tl_ref) | copy-start | bytes 786436
  64.4 28.9 %copy-start.2 = (bf16[128,1024]{1,0:T(8,128)(2,1)S(1)}, bf16[128,1024]{1,0:T(8,128)(2,1)}, u32[]{:S(2)}) copy-start(bf16[128,1024]{1,0:T(8,128)(2,1)} %constant.41.clone.th_ref) | copy-start | bytes 786436
  64.4 28.9 %copy-start.3 = (bf16[1024,128]{1,0:T(8,128)(2,1)S(1)}, bf16[1024,128]{1,0:T(8,128)(2,1)}, u32[]{:S(2)}) copy-start(bf16[1024,128]{1,0:T(8,128)(2,1)} %constant.34.clone.zl_ref) | copy-start | bytes 786436
  64.4 28.9 %copy-start.4 = (bf16[1024,128]{1,0:T(8,128)(2,1)S(1)}, bf16[1024,128]{1,0:T(8,128)(2,1)}, u32[]{:S(2)}) copy-start(bf16[1024,128]{1,0:T(8,128)(2,1)} %constant.33.clone.zh_ref) | copy-start | bytes 786436
  64.4 28.9 %copy-start.12 = (bf16[4,64,128]{2,1,0:T(8,128)(2,1)S(1)}, bf16[4,64,128]{2,1,0:T(8,128)(2,1)}, u32[]{:S(2)}) copy-start(bf16[4,64,128]{2,1,0:T(8,128)(2,1)} %constant.40.clone.bl_ref) | copy-start | bytes 196612
  64.4 28.9 %copy-start.13 = (bf16[4,64,128]{2,1,0:T(8,128)(2,1)S(1)}, bf16[4,64,128]{2,1,0:T(8,128)(2,1)}, u32[]{:S(2)}) copy-start(bf16[4,64,128]{2,1,0:T(8,128)(2,1)} %constant.39.clone.bh_ref) | copy-start | bytes 196612
  64.4 28.9 %copy-start.14 = (f32[128,128]{1,0:T(8,128)S(1)}, f32[128,128]{1,0:T(8,128)}, u32[]{:S(2)}) copy-start(f32[128,128]{1,0:T(8,128)} %constant.38.clone.own_ref) | copy-start | bytes 196612
  64.4 28.9 %copy-start.15 = (f32[128,128]{1,0:T(8,128)S(1)}, f32[128,128]{1,0:T(8,128)}, u32[]{:S(2)}) copy-start(f32[128,128]{1,0:T(8,128)} %constant.37.clone.wave_ref) | copy-start | bytes 196612
  64.4 28.9 %copy-start.16 = (bf16[128,192]{1,0:T(8,128)(2,1)S(1)}, bf16[128,192]{1,0:T(8,128)(2,1)}, u32[]{:S(2)}) copy-start(bf16[128,192]{1,0:T(8,128)(2,1)} %constant.36.clone.yl_ref) | copy-start | bytes 147460
  64.4 28.9 %copy-start.17 = (bf16[128,192]{1,0:T(8,128)(2,1)S(1)}, bf16[128,192]{1,0:T(8,128)(2,1)}, u32[]{:S(2)}) copy-start(bf16[128,192]{1,0:T(8,128)(2,1)} %constant.35.clone.yh_ref) | copy-start | bytes 147460
  94.5 30.8 %copy-start.10 = (bf16[8,32,128]{2,1,0:T(8,128)(2,1)S(1)}, bf16[8,32,128]{2,1,0:T(8,128)(2,1)}, u32[]{:S(2)}) copy-start(bf16[8,32,128]{2,1,0:T(8,128)(2,1)} %constant.44.clone.low_ref) | copy-start | bytes 196612
  94.5 30.8 %copy-start.11 = (bf16[8,32,128]{2,1,0:T(8,128)(2,1)S(1)}, bf16[8,32,128]{2,1,0:T(8,128)(2,1)}, u32[]{:S(2)}) copy-start(bf16[8,32,128]{2,1,0:T(8,128)(2,1)} %constant.43.clone.high_ref) | copy-start | bytes 196612

commit v5 on v4

--- a/solution.py
+++ b/solution.py
@@ -19,7 +19,7 @@
 FIRST, LAST = 4, 28
 KEPT = LAST - FIRST
 LANES = 128
-CHUNK = 9
+CHUNK = 7
 GROUP = 16
 PER = LANES // LX
 
@@ -32,7 +32,7 @@
 
 F32, BF16 = jnp.float32, jnp.bfloat16
 VMEM = pl.BlockSpec(memory_space=pltpu.VMEM)
-HBM = pl.BlockSpec(memory_space=pltpu.HBM)
+SMEM = pl.BlockSpec(memory_space=pltpu.SMEM)
 INTERPRET = False
 
 
@@ -79,7 +79,7 @@
                 along[i, :CORE, column] = basis[CORE * i : CORE * (i + 1), cell]
                 for a in range(LX):
                     if _cell(i, a) == cell and min((other - i) % PARTS, (i - other) % PARTS) <= 1:
-                        along[i, CORE + a, column] = 1.0
+                        along[i, CORE + (a % 2) * CORE + a // 2, column] = 1.0
     lane = np.arange(PARTS * LANES)
     z_cell = _cell(lane // LANES, lane % LX)
     z_table = basis[z_cell, :]
@@ -163,10 +163,12 @@
     )
 
 
-def bring_kernel(orb_ref, out_ref):
+def bring_kernel(occ_ref, orb_ref, out_ref, wide_ref):
     tiles, chunks = LX // 8, LX * LX // LANES
     lane = iota((8, LANES), 1)
     line = LX + 2
+    for n in range(NORB):
+        wide_ref[n : n + 1, :] = jnp.full((1, LANES), occ_ref[n], F32)
     for h in range(2):
         out_ref[h * line] = jnp.zeros((LX, LANES), F32)
         out_ref[h * line + line - 1] = jnp.zeros((LX, LANES), F32)
@@ -184,14 +186,17 @@
     lax.fori_loop(0, chunks, bring, 0)
 
 
-def bring_orbitals(orbitals):
+def bring_orbitals(occupations, orbitals):
     return call(
         bring_kernel,
-        jax.ShapeDtypeStruct((2 * (LX + 2), LX, LANES), F32),
-        [VMEM],
+        (
+            jax.ShapeDtypeStruct((2 * (LX + 2), LX, LANES), F32),
+            jax.ShapeDtypeStruct((NORB, LANES), F32),
+        ),
+        [SMEM, VMEM],
         flops=15000000,
         name="bring",
-    )(orbitals)
+    )(occupations, orbitals)
 
 
 def filter_kernel(occ_ref, orb_ref, pot_ref, weight_ref, new_ref, send_ref, ya, yb, coef, flat):
@@ -361,24 +366,49 @@
     )(occupations, orbitals, potential_ext, jnp.asarray(WEIGHT))
 
 
+def crop(value, lane):
+    out = pltpu.roll(value, LANES - FIRST, 1)
+    for x in range(1, PER):
+        moved = pltpu.roll(value, LANES - FIRST - 8 * x, 1)
+        out = jnp.where(lane < KEPT * x, out, moved)
+    return out
+
+
+def uncrop(value, lane):
+    out = jnp.zeros_like(value)
+    inside = (lane % LX >= FIRST) & (lane % LX < LAST)
+    for x in range(PER):
+        here = inside & (lane // LX == x)
+        out = jnp.where(here, pltpu.roll(value, FIRST + 8 * x, 1), out)
+    return out
+
+
 def y_kernel(got_ref, high_ref, low_ref, send_ref):
     kept = KEPT // PER
     part = kept // 2
-    chunk = kept + part
     at = lax.axis_index("gy")
     odd = lax.rem(lax.axis_index("gx"), 2) == 1
+    lane = iota((CORE, LANES), 1)
     table = (high_ref[at], low_ref[at])
-    folded = []
+    waves, folded = [], ([], [])
     for c in range(kept):
         lines = got_ref[pl.ds(c, PARTS * KEPT, stride=kept), :]
         value = dot3(table, halves(lines))
-        folded.append(value[CORE:])
-        for q in range(4):
-            send_ref[pl.ds(q * chunk + part + c, CORE, stride=4 * chunk), :] = value[:CORE]
-    for c in range(part):
-        low, high = folded[c], folded[part + c]
-        send_ref[pl.ds(c, LX, stride=2 * chunk), :] = jnp.where(odd, high, low)
-        send_ref[pl.ds(chunk + c, LX, stride=2 * chunk), :] = jnp.where(odd, low, high)
+        waves.append(crop(value[:CORE], lane))
+        for s in range(2):
+            folded[s].append(crop(value[CORE * (1 + s) : CORE * (2 + s)], lane))
+    for q in range(4):
+        planes = folded[q // 2]
+        thirds = []
+        for c in range(part):
+            low, high = planes[c], planes[part + c]
+            first, second = (low, high) if q % 2 == 0 else (high, low)
+            thirds.append(jnp.where(odd, second, first))
+        for c in range(kept):
+            piece = pltpu.roll(thirds[1 + c // part], 3 * LX - LX * (c % part), 1)
+            row = jnp.where(lane < 3 * LX, waves[c], piece)
+            send_ref[pl.ds(q * CHUNK + c, CORE, stride=4 * CHUNK), :] = row
+        send_ref[pl.ds(q * CHUNK + kept, CORE, stride=4 * CHUNK), :] = thirds[0]
 
 
 def along_y(got):
@@ -403,20 +433,24 @@
     th_ref,
     tl_ref,
     send_ref,
-    work,
 ):
     kept = KEPT // PER
     part = kept // 2
-    chunk = kept + part
     out_chunk = 6
     wide = PARTS * LANES
-    blocks = []
+    lane = iota((PARTS, LANES), 1)
+    blocks, thirds = [], []
     for k in range(PARTS):
-        rows = [
-            got_ref[pl.ds(chunk * k + part + c, PARTS, stride=chunk * PARTS), :]
-            for c in range(kept)
-        ]
-        blocks.append(jnp.concatenate(rows, axis=0))
+        rows = [got_ref[pl.ds(CHUNK * k + c, PARTS, stride=CHUNK * PARTS), :] for c in range(CHUNK)]
+        blocks.append(jnp.concatenate([uncrop(rows[c], lane) for c in range(kept)], axis=0))
+        units = [rows[kept]]
+        for u in range(2):
+            unit = pltpu.roll(rows[part * u], LX, 1)
+            for c in range(1, part):
+                moved = pltpu.roll(rows[part * u + c], LX + LX * c, 1)
+                unit = jnp.where(lane < LX * c, unit, moved)
+            units.append(unit)
+        thirds.append([uncrop(unit, lane) for unit in units])
     lines = jnp.concatenate(blocks, axis=1)
     which = (iota(lines.shape, 1) % LANES) // LX
     spread = jnp.concatenate([jnp.where(which == y, lines, 0.0) for y in range(PER)], axis=0)
@@ -440,34 +474,25 @@
             send_ref[pl.ds(out_chunk * k + half, PARTS, stride=out_chunk * PARTS), :] = packed[
                 8 * half : 8 * half + 8, k * LANES : (k + 1) * LANES
             ]
-    row = iota((8, LANES), 0)
-    left = iota((8, LANES), 1) % LX < LX // 2
+    left = lane % LX < LX // 2
     half = LX // 2
-    first, second = row < part, lax.rem(member, 2) == 1
-
-    def load(i, k):
-        at = chunk * (PARTS * i + k)
-        return jnp.where(first, got_ref[at : at + 8, :], 0.0)
-
-    for k in range(PARTS):
-        column = [load(i, k) for i in range(PARTS)]
-        for m in range(PARTS):
-            at = 8 * (PARTS * m + k)
-            work[at : at + 8, :] = pltpu.roll(column[m], 1, 0) + column[m - 1]
-    for m in range(PARTS):
-        after = (m + 1) % PARTS
-        other = second if m % 2 == 0 else jnp.logical_not(second)
+    own = iota((PARTS, LANES), 0) % 2 == lax.rem(member, 2)
+    for h in range(4):
         line = []
         for k in range(PARTS):
-            here, there = 8 * (PARTS * m + k), 8 * (PARTS * after + k)
-            line.append(jnp.where(other, work[there : there + 8, :], work[here : here + 8, :]))
+            if h == 0:
+                line.append(pltpu.roll(thirds[k][0], 1, 0))
+            elif h == part:
+                line.append(thirds[k][part - 1])
+            else:
+                line.append(thirds[k][h - 1] + pltpu.roll(thirds[k][h], 1, 0))
         for k in range(PARTS):
             beside = jnp.where(left, line[(k + 1) % PARTS], line[(k - 1) % PARTS])
             value = line[k] + jnp.where(
                 left, pltpu.roll(beside, LANES - half, 1), pltpu.roll(beside, half, 1)
             )
-            at = out_chunk * (PARTS * m + k) + 2
-            send_ref[at : at + 4, :] = value[0:4]
+            value = jnp.where(own, value, pltpu.roll(value, PARTS - 1, 0))
+            send_ref[pl.ds(out_chunk * k + 2 + h, PARTS, stride=out_chunk * PARTS), :] = value
 
 
 def on_plane(got):
@@ -476,7 +501,6 @@
         plane_kernel,
         jax.ShapeDtypeStruct((64 * 6, LANES), F32),
         [VMEM] * 11,
-        [pltpu.VMEM((64 * 8, LANES), F32)],
         name="on_plane",
     )(
         got,
@@ -580,24 +604,16 @@
     return lax.ppermute(last, axis, up), lax.ppermute(first, axis, down)
 
 
-def pack_kernel(pot_hbm, ion_hbm, own_ref, up_ref, down_ref, pot_ref, ion_ref, sems):
-    copies = [
-        pltpu.make_async_copy(source, target, sems.at[f])
-        for f, (source, target) in enumerate(((pot_hbm, pot_ref), (ion_hbm, ion_ref)))
-    ]
-    for copy in copies:
-        copy.start()
-    for copy in copies:
-        copy.wait()
+def pack_kernel(fields_ref, own_ref, up_ref, down_ref):
     lane = iota((CORE, LANES), 1)
     third = (lane % LX) // BUF
-    for f, ref in enumerate((pot_ref, ion_ref)):
+    for f in range(2):
         rows = slice(CORE * f, CORE * (f + 1))
         up, down = jnp.zeros((CORE, LANES), F32), jnp.zeros((CORE, LANES), F32)
         for c in range(PER):
             value = jnp.zeros((CORE, LANES), F32)
             for y in range(PER):
-                line = ref[pl.ds(PER * c + y, CORE, stride=CORE), :]
+                line = fields_ref[pl.ds(f * CORE * CORE + PER * c + y, CORE, stride=CORE), :]
                 line = jnp.concatenate([line, jnp.zeros((CORE, LANES - CORE), F32)], axis=1)
                 value = value + pltpu.roll(line, LX * y + BUF, 1)
             own_ref[rows, c * LANES : (c + 1) * LANES] = value
@@ -618,24 +634,21 @@
         )
 
 
-def refill(potential, ion_potential, orbitals, wide_occ):
+def refill(potential, ion_potential, orbitals, occupations):
     fields = 2
     count = fields * CORE
     slab = jax.ShapeDtypeStruct((count, LANES), F32)
     full = jax.ShapeDtypeStruct((count, CORE * LX), F32)
-    lines = pltpu.VMEM((CORE * CORE, CORE), F32)
-    scratch = [lines, lines, pltpu.SemaphoreType.DMA((2,))]
-    own, up, down = call(pack_kernel, (full, slab, slab), [HBM, HBM], scratch, name="pack")(
-        *[f.reshape(CORE * CORE, CORE) for f in (potential, ion_potential)]
-    )
+    lines = jnp.concatenate([potential, ion_potential]).reshape(fields * CORE * CORE, CORE)
+    own, up, down = call(pack_kernel, (full, slab, slab), [VMEM], name="pack")(lines)
     before, after = both_sides(down, up, "gz")
     both = call(merge_kernel, full, [VMEM, VMEM, VMEM], name="merge")(own, before, after)
     width = BUF * LX
     before, after = both_sides(both[:, :width], both[:, CORE * LX - width :], "gy")
     both = jnp.concatenate([before, both, after], axis=1).reshape(fields, CORE, LX * LX)
-    both, orbitals, wide_occ = lax.optimization_barrier((both, orbitals, wide_occ))
+    both, orbitals = lax.optimization_barrier((both, orbitals))
     before, after = both_sides(both[:, :BUF], both[:, CORE - BUF :], "gx")
-    brought = bring_orbitals(orbitals)
+    brought, wide_occ = bring_orbitals(occupations, orbitals)
     whole = jnp.concatenate([before, both, after], axis=1)
     return whole[0], whole[1], brought, wide_occ
 
@@ -650,8 +663,9 @@
 
 
 def on_device(orbitals, potential, ion_potential, occupations):
-    wide_occ = jnp.broadcast_to(occupations[:, None], (NORB, LANES))
-    pot_ext, ion_ext, brought, wide_occ = refill(potential, ion_potential, orbitals, wide_occ)
+    pot_ext, ion_ext, brought, wide_occ = refill(
+        potential, ion_potential, orbitals, occupations
+    )
     new_orbitals, send = filtered_set(wide_occ, brought, pot_ext)
     got = exchange(send, "gy", KEPT * KEPT // PER)
     send = along_y(got)

time: 127 us -> 124 us (0.976)
  local copies, waits for them, and re-layouts: 2.74 us -> 0.16 us
  blocking collectives: 72.5 us -> 70.3 us
    all_to_all x4, blocking collectives: 72.5 us -> 70.3 us  [exchange(): lax.all_to_all(shaped, axis, split_axis=0, concat_axis=0, tiled=True)]
    unnamed x38 -> x36, local copies, waits for them, and re-layouts: 1.97 us -> 0.12 us
where the time goes in v5:
time: 124 us; the launch traced here: 123 us
  blocking collectives  70.3 us (57%)
  starting transfers between devices  30.8 us (25%)
  Pallas kernels  18.2 us (15%)
  waiting for transfers between devices  1.87 us (2%)
    all_to_all x4, blocking collectives, exchange(): lax.all_to_all(shaped, axis, split_axis=0, concat_axis=0, tiled=True)  70.3 us
    ppermute x6, starting transfers between devices, both_sides(): return (lax.ppermute(last, axis, up), lax.ppermute(first, axis, down))  30.8 us
    pallas_call x1, Pallas kernels, filtered_set(): call(filter_kernel, (jax.ShapeDtypeStruct((NORB, LX, LX * LX), BF16), jax...  12 us
  transfers between devices with their start and end apart: 6, of which 2 were waited for; matrix products, arithmetic and copies ran while one was open for 0% of the time, Pallas kernels for 1%

profile of v5, /device:TPU:1, one launch (start us, length us, event | category | flops | bytes accessed | tf_op | source)
XLA Modules:
  0.0 123.3 jit_solution(17152178238431679739)
XLA Ops:
  0.7 1.0 pad_maximum_fusion
  1.7 0.2 pack.1
  1.9 5.6 %collective-permute-start = (f32[32,128]{1,0:T(8,128)S(1)}, f32[32,128]{1,0:T(8,128)S(1)}, u32[]{:S(2)}, u32[]{:S(2)}) collective-permute-start(f32[32,128]{1,0:T(8,128)S(1)} %get-tuple-element.16), channel_id=1, source_target_pairs={{0,1},{1,2},{2,3},{3,4},{4,5},{5,6},{6,7},{7,0},{8,9},{9,10},{10,1... | collective-permute-start | bytes 49160 | tf_op jit(solution)/shard_map/ppermute | solution.py:604
  7.5 5.1 %collective-permute-start.1 = (f32[32,128]{1,0:T(8,128)S(1)}, f32[32,128]{1,0:T(8,128)S(1)}, u32[]{:S(2)}, u32[]{:S(2)}) collective-permute-start(f32[32,128]{1,0:T(8,128)S(1)} %get-tuple-element.17), channel_id=1, source_target_pairs={{1,0},{2,1},{3,2},{4,3},{5,4},{6,5},{7,6},{0,7},{9,8},{10,9},{11,1... | collective-permute-start | bytes 49160 | tf_op jit(solution)/shard_map/ppermute | solution.py:604
  12.6 0.9 collective-permute-done.1.after_ref
  13.5 0.1 merge.1
  13.6 0.0 copy-start.7
  13.6 3.3 %collective-permute-start.2 = (f32[32,256]{1,0:T(8,128)S(1)}, f32[32,256]{1,0:T(8,128)S(1)}, u32[]{:S(2)}, u32[]{:S(2)}) collective-permute-start(f32[32,256]{1,0:T(8,128)S(1)} %get-tuple-element.31), channel_id=1, source_target_pairs={{0,8},{8,16},{16,24},{24,32},{32,40},{40,48},{48,56},{56,0},{1,9},... | collective-permute-start | bytes 98312 | tf_op jit(solution)/shard_map/ppermute | solution.py:604
  16.9 4.3 %collective-permute-start.3 = (f32[32,256]{1,0:T(8,128)S(1)}, f32[32,256]{1,0:T(8,128)S(1)}, u32[]{:S(2)}, u32[]{:S(2)}) collective-permute-start(f32[32,256]{1,0:T(8,128)S(1)} %get-tuple-element.32), channel_id=1, source_target_pairs={{8,0},{16,8},{24,16},{32,24},{40,32},{48,40},{56,48},{0,56},{9,1},... | collective-permute-start | bytes 98312 | tf_op jit(solution)/shard_map/ppermute | solution.py:604
  21.2 1.0 collective-permute-done.3
  22.2 4.0 %collective-permute-start.4 = (f32[2,8,1024]{2,1,0:T(8,128)S(1)}, f32[2,8,1024]{2,1,0:T(8,128)S(1)}, u32[]{:S(2)}, u32[]{:S(2)}) collective-permute-start(f32[2,8,1024]{2,1,0:T(8,128)S(1)} %get-tuple-element.30), channel_id=1, source_target_pairs={{0,64},{64,128},{128,192},{192,256},{256,320},{320,384},{384,448},... | collective-permute-start | bytes 196616 | tf_op jit(solution)/shard_map/ppermute | solution.py:604
  26.2 8.6 %collective-permute-start.5 = (f32[2,8,1024]{2,1,0:T(8,128)S(1)}, f32[2,8,1024]{2,1,0:T(8,128)S(1)}, u32[]{:S(2)}, u32[]{:S(2)}) collective-permute-start(f32[2,8,1024]{2,1,0:T(8,128)S(1)} %get-tuple-element.29), channel_id=1, source_target_pairs={{64,0},{128,64},{192,128},{256,192},{320,256},{384,320},{448,384},... | collective-permute-start | bytes 196616 | tf_op jit(solution)/shard_map/ppermute | solution.py:604
  34.8 1.8 %bring.1 = (f32[68,32,128]{2,1,0:T(8,128)S(1)}, f32[8,128]{1,0:T(8,128)S(1)}) custom-call(f32[8]{0:T(128)S(1)} %copy-done.16, bf16[8,32,1024]{2,1,0:T(8,128)(2,1)S(1)} %copy-done), custom_call_target="tpu_custom_call" | custom-call | flops 15000000 | bytes 1000000 | tf_op jit(solution)/shard_map/bring/pallas_call | solution.py:190
  36.7 0.0 copy-start.5
  36.8 0.0 copy-start.6
  36.8 12.0 %filter.1 = (bf16[8,32,1024]{2,1,0:T(8,128)(2,1)}, f32[1152,128]{1,0:T(8,128)S(1)}) custom-call(f32[8,128]{1,0:T(8,128)S(1)} %get-tuple-element.19.occ_ref, f32[68,32,128]{2,1,0:T(8,128)S(1)} %get-tuple-element.20.orb_ref, f32[32,1024]{1,0:T(8,128)S(1)} %get-tuple-element.28.pot_ref, f32[32,1024]{1,0:T(8,128)S(1)} %copy-done.7), custom_call_target="tpu_custom_call" | custom-call | flops 60000000 | bytes 1000000 | tf_op jit(solution)/shard_map/filter/pallas_call | solution.py:351
  48.8 14.9 %all_to_all.20 = f32[144,8,128]{2,1,0:T(8,128)S(1)} all-to-all(f32[144,8,128]{2,1,0:T(8,128)S(1)} %bitcast.23), channel_id=1, replica_groups=mesh['gx'=8,'gy'=8,'gz'=8] {'gy'}, dimensions={0} | all-to-all | bytes 1179648 | tf_op jit(solution)/shard_map/all_to_all | solution.py:660
  63.6 0.0 copy-start.10
  63.6 0.0 copy-start.11
  63.7 0.0 copy-start.12
  63.7 0.0 copy-start.13
  63.7 0.0 copy-start.14
  63.7 0.0 copy-start.15
  63.7 0.6 along_y.1
  64.4 25.9 %all_to_all.21 = f32[448,1,128]{2,1,0:T(1,128)S(1)} all-to-all(f32[448,1,128]{2,1,0:T(1,128)S(1)} %bitcast.20), channel_id=1, replica_groups=mesh['gx'=8,'gy'=8,'gz'=8] {'gx','gz'}, dimensions={0} | all-to-all | bytes 458752 | tf_op jit(solution)/shard_map/all_to_all | solution.py:660
  90.3 1.3 %on_plane.1 = f32[384,128]{1,0:T(8,128)S(1)} custom-call(f32[448,128]{1,0:T(8,128)S(1)} %bitcast.19, bf16[1024,128]{1,0:T(8,128)(2,1)S(1)} %copy-done.4, bf16[1024,128]{1,0:T(8,128)(2,1)S(1)} %copy-done.3, bf16[128,192]{1,0:T(8,128)(2,1)S(1)} %copy-done.15, bf16[128,192]{1,0:T(8,128)(2,1)S(1)} %copy-done.14, f32[128,128]{1,0:T(8,128)S(1)} %copy-done.13, ...), custom_call_target="tpu_custom_call" | custom-call | flops 1000000 | bytes 1000000 | tf_op jit(solution)/shard_map/on_plane/pallas_call | solution.py:500
  91.7 0.0 copy-start.8
  91.7 0.0 copy-start.9
  91.7 18.4 %all_to_all.22 = f32[192,2,128]{2,1,0:T(2,128)S(1)} all-to-all(f32[192,2,128]{2,1,0:T(2,128)S(1)} %bitcast.21), channel_id=1, replica_groups=mesh['gx'=8,'gy'=8,'gz'=8] {'gx','gz'}, dimensions={0} | all-to-all | bytes 393216 | tf_op jit(solution)/shard_map/all_to_all | solution.py:660
  110.1 1.0 on_window.1
  111.0 11.2 %all_to_all.23 = f32[128,8,128]{2,1,0:T(8,128)S(1)} all-to-all(f32[128,8,128]{2,1,0:T(8,128)S(1)} %bitcast.24), channel_id=1, replica_groups=mesh['gx'=8,'gy'=8,'gz'=8] {'gy'}, dimensions={0} | all-to-all | bytes 1048576 | tf_op jit(solution)/shard_map/all_to_all | solution.py:660
  122.2 1.1 last_step.1
  (34 shorter events, 0.1 us)
Async XLA Ops:
  0.6 34.2 %copy-start = (bf16[8,32,1024]{2,1,0:T(8,128)(2,1)S(1)}, bf16[8,32,1024]{2,1,0:T(8,128)(2,1)}, u32[]{:S(2)}) copy-start(bf16[8,32,1024]{2,1,0:T(8,128)(2,1)} %orb_ref) | copy-start | bytes 1572868
  0.6 34.2 %copy-start.16 = (f32[8]{0:T(128)S(1)}, f32[8]{0:T(128)}, u32[]{:S(2)}) copy-start(f32[8]{0:T(128)} %occ_ref.1) | copy-start | bytes 100
  1.9 10.7 %collective-permute-start = (f32[32,128]{1,0:T(8,128)S(1)}, f32[32,128]{1,0:T(8,128)S(1)}, u32[]{:S(2)}, u32[]{:S(2)}) collective-permute-start(f32[32,128]{1,0:T(8,128)S(1)} %get-tuple-element.16), channel_id=1, source_target_pairs={{0,1},{1,2},{2,3},{3,4},{4,5},{5,6},{6,7},{7,0},{8,9},{9,10},{10,1... | collective-permute-start | bytes 49160 | tf_op jit(solution)/shard_map/ppermute | solution.py:604
  7.5 6.0 %collective-permute-start.1 = (f32[32,128]{1,0:T(8,128)S(1)}, f32[32,128]{1,0:T(8,128)S(1)}, u32[]{:S(2)}, u32[]{:S(2)}) collective-permute-start(f32[32,128]{1,0:T(8,128)S(1)} %get-tuple-element.17), channel_id=1, source_target_pairs={{1,0},{2,1},{3,2},{4,3},{5,4},{6,5},{7,6},{0,7},{9,8},{10,9},{11,1... | collective-permute-start | bytes 49160 | tf_op jit(solution)/shard_map/ppermute | solution.py:604
  13.6 23.2 %copy-start.7 = (f32[32,1024]{1,0:T(8,128)S(1)}, f32[32,1024]{1,0:T(8,128)}, u32[]{:S(2)}) copy-start(f32[32,1024]{1,0:T(8,128)} %constant.30.clone.weight_ref) | copy-start | bytes 393220
  13.6 7.5 %collective-permute-start.2 = (f32[32,256]{1,0:T(8,128)S(1)}, f32[32,256]{1,0:T(8,128)S(1)}, u32[]{:S(2)}, u32[]{:S(2)}) collective-permute-start(f32[32,256]{1,0:T(8,128)S(1)} %get-tuple-element.31), channel_id=1, source_target_pairs={{0,8},{8,16},{16,24},{24,32},{32,40},{40,48},{48,56},{56,0},{1,9},... | collective-permute-start | bytes 98312 | tf_op jit(solution)/shard_map/ppermute | solution.py:604
  16.9 5.3 %collective-permute-start.3 = (f32[32,256]{1,0:T(8,128)S(1)}, f32[32,256]{1,0:T(8,128)S(1)}, u32[]{:S(2)}, u32[]{:S(2)}) collective-permute-start(f32[32,256]{1,0:T(8,128)S(1)} %get-tuple-element.32), channel_id=1, source_target_pairs={{8,0},{16,8},{24,16},{32,24},{40,32},{48,40},{56,48},{0,56},{9,1},... | collective-permute-start | bytes 98312 | tf_op jit(solution)/shard_map/ppermute | solution.py:604
  22.2 14.5 %collective-permute-start.4 = (f32[2,8,1024]{2,1,0:T(8,128)S(1)}, f32[2,8,1024]{2,1,0:T(8,128)S(1)}, u32[]{:S(2)}, u32[]{:S(2)}) collective-permute-start(f32[2,8,1024]{2,1,0:T(8,128)S(1)} %get-tuple-element.30), channel_id=1, source_target_pairs={{0,64},{64,128},{128,192},{192,256},{256,320},{320,384},{384,448},... | collective-permute-start | bytes 196616 | tf_op jit(solution)/shard_map/ppermute | solution.py:604
  26.2 10.5 %collective-permute-start.5 = (f32[2,8,1024]{2,1,0:T(8,128)S(1)}, f32[2,8,1024]{2,1,0:T(8,128)S(1)}, u32[]{:S(2)}, u32[]{:S(2)}) collective-permute-start(f32[2,8,1024]{2,1,0:T(8,128)S(1)} %get-tuple-element.29), channel_id=1, source_target_pairs={{64,0},{128,64},{192,128},{256,192},{320,256},{384,320},{448,384},... | collective-permute-start | bytes 196616 | tf_op jit(solution)/shard_map/ppermute | solution.py:604
  36.7 27.0 %copy-start.5 = (bf16[8,48,192]{2,1,0:T(8,128)(2,1)S(1)}, bf16[8,48,192]{2,1,0:T(8,128)(2,1)}, u32[]{:S(2)}) copy-start(bf16[8,48,192]{2,1,0:T(8,128)(2,1)} %constant.32.clone.low_ref) | copy-start | bytes 442372
  36.8 27.0 %copy-start.6 = (bf16[8,48,192]{2,1,0:T(8,128)(2,1)S(1)}, bf16[8,48,192]{2,1,0:T(8,128)(2,1)}, u32[]{:S(2)}) copy-start(bf16[8,48,192]{2,1,0:T(8,128)(2,1)} %constant.31.clone.high_ref) | copy-start | bytes 442372
  63.6 26.6 %copy-start.1 = (bf16[128,1024]{1,0:T(8,128)(2,1)S(1)}, bf16[128,1024]{1,0:T(8,128)(2,1)}, u32[]{:S(2)}) copy-start(bf16[128,1024]{1,0:T(8,128)(2,1)} %constant.42.clone.tl_ref) | copy-start | bytes 786436
  63.6 26.6 %copy-start.2 = (bf16[128,1024]{1,0:T(8,128)(2,1)S(1)}, bf16[128,1024]{1,0:T(8,128)(2,1)}, u32[]{:S(2)}) copy-start(bf16[128,1024]{1,0:T(8,128)(2,1)} %constant.41.clone.th_ref) | copy-start | bytes 786436
  63.6 26.6 %copy-start.3 = (bf16[1024,128]{1,0:T(8,128)(2,1)S(1)}, bf16[1024,128]{1,0:T(8,128)(2,1)}, u32[]{:S(2)}) copy-start(bf16[1024,128]{1,0:T(8,128)(2,1)} %constant.34.clone.zl_ref) | copy-start | bytes 786436
  63.6 26.6 %copy-start.4 = (bf16[1024,128]{1,0:T(8,128)(2,1)S(1)}, bf16[1024,128]{1,0:T(8,128)(2,1)}, u32[]{:S(2)}) copy-start(bf16[1024,128]{1,0:T(8,128)(2,1)} %constant.33.clone.zh_ref) | copy-start | bytes 786436
  63.6 26.6 %copy-start.10 = (bf16[4,64,128]{2,1,0:T(8,128)(2,1)S(1)}, bf16[4,64,128]{2,1,0:T(8,128)(2,1)}, u32[]{:S(2)}) copy-start(bf16[4,64,128]{2,1,0:T(8,128)(2,1)} %constant.40.clone.bl_ref) | copy-start | bytes 196612
  63.6 26.6 %copy-start.11 = (bf16[4,64,128]{2,1,0:T(8,128)(2,1)S(1)}, bf16[4,64,128]{2,1,0:T(8,128)(2,1)}, u32[]{:S(2)}) copy-start(bf16[4,64,128]{2,1,0:T(8,128)(2,1)} %constant.39.clone.bh_ref) | copy-start | bytes 196612
  63.7 26.6 %copy-start.12 = (f32[128,128]{1,0:T(8,128)S(1)}, f32[128,128]{1,0:T(8,128)}, u32[]{:S(2)}) copy-start(f32[128,128]{1,0:T(8,128)} %constant.38.clone.own_ref) | copy-start | bytes 196612
  63.7 26.6 %copy-start.13 = (f32[128,128]{1,0:T(8,128)S(1)}, f32[128,128]{1,0:T(8,128)}, u32[]{:S(2)}) copy-start(f32[128,128]{1,0:T(8,128)} %constant.37.clone.wave_ref) | copy-start | bytes 196612
  63.7 26.6 %copy-start.14 = (bf16[128,192]{1,0:T(8,128)(2,1)S(1)}, bf16[128,192]{1,0:T(8,128)(2,1)}, u32[]{:S(2)}) copy-start(bf16[128,192]{1,0:T(8,128)(2,1)} %constant.36.clone.yl_ref) | copy-start | bytes 147460
  63.7 26.6 %copy-start.15 = (bf16[128,192]{1,0:T(8,128)(2,1)S(1)}, bf16[128,192]{1,0:T(8,128)(2,1)}, u32[]{:S(2)}) copy-start(bf16[128,192]{1,0:T(8,128)(2,1)} %constant.35.clone.yh_ref) | copy-start | bytes 147460
  91.7 30.5 %copy-start.8 = (bf16[8,32,128]{2,1,0:T(8,128)(2,1)S(1)}, bf16[8,32,128]{2,1,0:T(8,128)(2,1)}, u32[]{:S(2)}) copy-start(bf16[8,32,128]{2,1,0:T(8,128)(2,1)} %constant.44.clone.low_ref) | copy-start | bytes 196612
  91.7 30.5 %copy-start.9 = (bf16[8,32,128]{2,1,0:T(8,128)(2,1)S(1)}, bf16[8,32,128]{2,1,0:T(8,128)(2,1)}, u32[]{:S(2)}) copy-start(bf16[8,32,128]{2,1,0:T(8,128)(2,1)} %constant.43.clone.high_ref) | copy-start | bytes 196612

commit v6 on v5

--- a/solution.py
+++ b/solution.py
@@ -20,7 +20,7 @@
 KEPT = LAST - FIRST
 LANES = 128
 CHUNK = 7
-GROUP = 16
+GROUP = 32
 PER = LANES // LX
 
 spacing = 0.2

time: 124 us -> 123 us (level)
  no operation moved by 1% of the time
where the time goes in v6:
time: 123 us; the launch traced here: 122 us
  blocking collectives  70.3 us (57%)
  starting transfers between devices  30.8 us (25%)
  Pallas kernels  17 us (14%)
  waiting for transfers between devices  1.87 us (2%)
    all_to_all x4, blocking collectives, exchange(): lax.all_to_all(shaped, axis, split_axis=0, concat_axis=0, tiled=True)  70.3 us
    ppermute x6, starting transfers between devices, both_sides(): return (lax.ppermute(last, axis, up), lax.ppermute(first, axis, down))  30.8 us
    pallas_call x1, Pallas kernels, filtered_set(): call(filter_kernel, (jax.ShapeDtypeStruct((NORB, LX, LX * LX), BF16), jax...  10.8 us
  transfers between devices with their start and end apart: 6, of which 2 were waited for; matrix products, arithmetic and copies ran while one was open for 0% of the time, Pallas kernels for 1%

profile of v6, /device:TPU:1, one launch (start us, length us, event | category | flops | bytes accessed | tf_op | source)
XLA Modules:
  0.0 122.2 jit_solution(11496323037841559341)
XLA Ops:
  0.7 1.0 pad_maximum_fusion
  1.7 0.2 pack.1
  1.9 5.6 %collective-permute-start = (f32[32,128]{1,0:T(8,128)S(1)}, f32[32,128]{1,0:T(8,128)S(1)}, u32[]{:S(2)}, u32[]{:S(2)}) collective-permute-start(f32[32,128]{1,0:T(8,128)S(1)} %get-tuple-element.16), channel_id=1, source_target_pairs={{0,1},{1,2},{2,3},{3,4},{4,5},{5,6},{6,7},{7,0},{8,9},{9,10},{10,1... | collective-permute-start | bytes 49160 | tf_op jit(solution)/shard_map/ppermute | solution.py:604
  7.5 5.1 %collective-permute-start.1 = (f32[32,128]{1,0:T(8,128)S(1)}, f32[32,128]{1,0:T(8,128)S(1)}, u32[]{:S(2)}, u32[]{:S(2)}) collective-permute-start(f32[32,128]{1,0:T(8,128)S(1)} %get-tuple-element.17), channel_id=1, source_target_pairs={{1,0},{2,1},{3,2},{4,3},{5,4},{6,5},{7,6},{0,7},{9,8},{10,9},{11,1... | collective-permute-start | bytes 49160 | tf_op jit(solution)/shard_map/ppermute | solution.py:604
  12.6 0.9 collective-permute-done.1.after_ref
  13.5 0.1 merge.1
  13.6 0.0 copy-start.7
  13.6 3.3 %collective-permute-start.2 = (f32[32,256]{1,0:T(8,128)S(1)}, f32[32,256]{1,0:T(8,128)S(1)}, u32[]{:S(2)}, u32[]{:S(2)}) collective-permute-start(f32[32,256]{1,0:T(8,128)S(1)} %get-tuple-element.31), channel_id=1, source_target_pairs={{0,8},{8,16},{16,24},{24,32},{32,40},{40,48},{48,56},{56,0},{1,9},... | collective-permute-start | bytes 98312 | tf_op jit(solution)/shard_map/ppermute | solution.py:604
  16.9 4.3 %collective-permute-start.3 = (f32[32,256]{1,0:T(8,128)S(1)}, f32[32,256]{1,0:T(8,128)S(1)}, u32[]{:S(2)}, u32[]{:S(2)}) collective-permute-start(f32[32,256]{1,0:T(8,128)S(1)} %get-tuple-element.32), channel_id=1, source_target_pairs={{8,0},{16,8},{24,16},{32,24},{40,32},{48,40},{56,48},{0,56},{9,1},... | collective-permute-start | bytes 98312 | tf_op jit(solution)/shard_map/ppermute | solution.py:604
  21.2 1.0 collective-permute-done.3
  22.2 4.0 %collective-permute-start.4 = (f32[2,8,1024]{2,1,0:T(8,128)S(1)}, f32[2,8,1024]{2,1,0:T(8,128)S(1)}, u32[]{:S(2)}, u32[]{:S(2)}) collective-permute-start(f32[2,8,1024]{2,1,0:T(8,128)S(1)} %get-tuple-element.30), channel_id=1, source_target_pairs={{0,64},{64,128},{128,192},{192,256},{256,320},{320,384},{384,448},... | collective-permute-start | bytes 196616 | tf_op jit(solution)/shard_map/ppermute | solution.py:604
  26.2 8.6 %collective-permute-start.5 = (f32[2,8,1024]{2,1,0:T(8,128)S(1)}, f32[2,8,1024]{2,1,0:T(8,128)S(1)}, u32[]{:S(2)}, u32[]{:S(2)}) collective-permute-start(f32[2,8,1024]{2,1,0:T(8,128)S(1)} %get-tuple-element.29), channel_id=1, source_target_pairs={{64,0},{128,64},{192,128},{256,192},{320,256},{384,320},{448,384},... | collective-permute-start | bytes 196616 | tf_op jit(solution)/shard_map/ppermute | solution.py:604
  34.8 1.8 %bring.1 = (f32[68,32,128]{2,1,0:T(8,128)S(1)}, f32[8,128]{1,0:T(8,128)S(1)}) custom-call(f32[8]{0:T(128)S(1)} %copy-done.16, bf16[8,32,1024]{2,1,0:T(8,128)(2,1)S(1)} %copy-done), custom_call_target="tpu_custom_call" | custom-call | flops 15000000 | bytes 1000000 | tf_op jit(solution)/shard_map/bring/pallas_call | solution.py:190
  36.7 0.0 copy-start.5
  36.8 0.0 copy-start.6
  36.8 10.8 %filter.1 = (bf16[8,32,1024]{2,1,0:T(8,128)(2,1)}, f32[1152,128]{1,0:T(8,128)S(1)}) custom-call(f32[8,128]{1,0:T(8,128)S(1)} %get-tuple-element.19.occ_ref, f32[68,32,128]{2,1,0:T(8,128)S(1)} %get-tuple-element.20.orb_ref, f32[32,1024]{1,0:T(8,128)S(1)} %get-tuple-element.28.pot_ref, f32[32,1024]{1,0:T(8,128)S(1)} %copy-done.7), custom_call_target="tpu_custom_call" | custom-call | flops 60000000 | bytes 1000000 | tf_op jit(solution)/shard_map/filter/pallas_call | solution.py:351
  47.6 14.9 %all_to_all.20 = f32[144,8,128]{2,1,0:T(8,128)S(1)} all-to-all(f32[144,8,128]{2,1,0:T(8,128)S(1)} %bitcast.23), channel_id=1, replica_groups=mesh['gx'=8,'gy'=8,'gz'=8] {'gy'}, dimensions={0} | all-to-all | bytes 1179648 | tf_op jit(solution)/shard_map/all_to_all | solution.py:660
  62.5 0.0 copy-start.10
  62.5 0.0 copy-start.11
  62.5 0.0 copy-start.12
  62.5 0.0 copy-start.13
  62.5 0.0 copy-start.14
  62.5 0.0 copy-start.15
  62.6 0.6 along_y.1
  63.2 25.9 %all_to_all.21 = f32[448,1,128]{2,1,0:T(1,128)S(1)} all-to-all(f32[448,1,128]{2,1,0:T(1,128)S(1)} %bitcast.20), channel_id=1, replica_groups=mesh['gx'=8,'gy'=8,'gz'=8] {'gx','gz'}, dimensions={0} | all-to-all | bytes 458752 | tf_op jit(solution)/shard_map/all_to_all | solution.py:660
  89.2 1.3 %on_plane.1 = f32[384,128]{1,0:T(8,128)S(1)} custom-call(f32[448,128]{1,0:T(8,128)S(1)} %bitcast.19, bf16[1024,128]{1,0:T(8,128)(2,1)S(1)} %copy-done.4, bf16[1024,128]{1,0:T(8,128)(2,1)S(1)} %copy-done.3, bf16[128,192]{1,0:T(8,128)(2,1)S(1)} %copy-done.15, bf16[128,192]{1,0:T(8,128)(2,1)S(1)} %copy-done.14, f32[128,128]{1,0:T(8,128)S(1)} %copy-done.13, ...), custom_call_target="tpu_custom_call" | custom-call | flops 1000000 | bytes 1000000 | tf_op jit(solution)/shard_map/on_plane/pallas_call | solution.py:500
  90.5 0.0 copy-start.8
  90.5 0.0 copy-start.9
  90.5 18.4 %all_to_all.22 = f32[192,2,128]{2,1,0:T(2,128)S(1)} all-to-all(f32[192,2,128]{2,1,0:T(2,128)S(1)} %bitcast.21), channel_id=1, replica_groups=mesh['gx'=8,'gy'=8,'gz'=8] {'gx','gz'}, dimensions={0} | all-to-all | bytes 393216 | tf_op jit(solution)/shard_map/all_to_all | solution.py:660
  108.9 1.0 on_window.1
  109.9 11.2 %all_to_all.23 = f32[128,8,128]{2,1,0:T(8,128)S(1)} all-to-all(f32[128,8,128]{2,1,0:T(8,128)S(1)} %bitcast.24), channel_id=1, replica_groups=mesh['gx'=8,'gy'=8,'gz'=8] {'gy'}, dimensions={0} | all-to-all | bytes 1048576 | tf_op jit(solution)/shard_map/all_to_all | solution.py:660
  121.1 1.1 last_step.1
  (34 shorter events, 0.1 us)
Async XLA Ops:
  0.6 34.2 %copy-start = (bf16[8,32,1024]{2,1,0:T(8,128)(2,1)S(1)}, bf16[8,32,1024]{2,1,0:T(8,128)(2,1)}, u32[]{:S(2)}) copy-start(bf16[8,32,1024]{2,1,0:T(8,128)(2,1)} %orb_ref) | copy-start | bytes 1572868
  0.6 34.2 %copy-start.16 = (f32[8]{0:T(128)S(1)}, f32[8]{0:T(128)}, u32[]{:S(2)}) copy-start(f32[8]{0:T(128)} %occ_ref.1) | copy-start | bytes 100
  1.9 10.7 %collective-permute-start = (f32[32,128]{1,0:T(8,128)S(1)}, f32[32,128]{1,0:T(8,128)S(1)}, u32[]{:S(2)}, u32[]{:S(2)}) collective-permute-start(f32[32,128]{1,0:T(8,128)S(1)} %get-tuple-element.16), channel_id=1, source_target_pairs={{0,1},{1,2},{2,3},{3,4},{4,5},{5,6},{6,7},{7,0},{8,9},{9,10},{10,1... | collective-permute-start | bytes 49160 | tf_op jit(solution)/shard_map/ppermute | solution.py:604
  7.5 6.0 %collective-permute-start.1 = (f32[32,128]{1,0:T(8,128)S(1)}, f32[32,128]{1,0:T(8,128)S(1)}, u32[]{:S(2)}, u32[]{:S(2)}) collective-permute-start(f32[32,128]{1,0:T(8,128)S(1)} %get-tuple-element.17), channel_id=1, source_target_pairs={{1,0},{2,1},{3,2},{4,3},{5,4},{6,5},{7,6},{0,7},{9,8},{10,9},{11,1... | collective-permute-start | bytes 49160 | tf_op jit(solution)/shard_map/ppermute | solution.py:604
  13.6 23.2 %copy-start.7 = (f32[32,1024]{1,0:T(8,128)S(1)}, f32[32,1024]{1,0:T(8,128)}, u32[]{:S(2)}) copy-start(f32[32,1024]{1,0:T(8,128)} %constant.30.clone.weight_ref) | copy-start | bytes 393220
  13.6 7.5 %collective-permute-start.2 = (f32[32,256]{1,0:T(8,128)S(1)}, f32[32,256]{1,0:T(8,128)S(1)}, u32[]{:S(2)}, u32[]{:S(2)}) collective-permute-start(f32[32,256]{1,0:T(8,128)S(1)} %get-tuple-element.31), channel_id=1, source_target_pairs={{0,8},{8,16},{16,24},{24,32},{32,40},{40,48},{48,56},{56,0},{1,9},... | collective-permute-start | bytes 98312 | tf_op jit(solution)/shard_map/ppermute | solution.py:604
  16.9 5.3 %collective-permute-start.3 = (f32[32,256]{1,0:T(8,128)S(1)}, f32[32,256]{1,0:T(8,128)S(1)}, u32[]{:S(2)}, u32[]{:S(2)}) collective-permute-start(f32[32,256]{1,0:T(8,128)S(1)} %get-tuple-element.32), channel_id=1, source_target_pairs={{8,0},{16,8},{24,16},{32,24},{40,32},{48,40},{56,48},{0,56},{9,1},... | collective-permute-start | bytes 98312 | tf_op jit(solution)/shard_map/ppermute | solution.py:604
  22.2 14.5 %collective-permute-start.4 = (f32[2,8,1024]{2,1,0:T(8,128)S(1)}, f32[2,8,1024]{2,1,0:T(8,128)S(1)}, u32[]{:S(2)}, u32[]{:S(2)}) collective-permute-start(f32[2,8,1024]{2,1,0:T(8,128)S(1)} %get-tuple-element.30), channel_id=1, source_target_pairs={{0,64},{64,128},{128,192},{192,256},{256,320},{320,384},{384,448},... | collective-permute-start | bytes 196616 | tf_op jit(solution)/shard_map/ppermute | solution.py:604
  26.2 10.5 %collective-permute-start.5 = (f32[2,8,1024]{2,1,0:T(8,128)S(1)}, f32[2,8,1024]{2,1,0:T(8,128)S(1)}, u32[]{:S(2)}, u32[]{:S(2)}) collective-permute-start(f32[2,8,1024]{2,1,0:T(8,128)S(1)} %get-tuple-element.29), channel_id=1, source_target_pairs={{64,0},{128,64},{192,128},{256,192},{320,256},{384,320},{448,384},... | collective-permute-start | bytes 196616 | tf_op jit(solution)/shard_map/ppermute | solution.py:604
  36.7 25.8 %copy-start.5 = (bf16[8,48,192]{2,1,0:T(8,128)(2,1)S(1)}, bf16[8,48,192]{2,1,0:T(8,128)(2,1)}, u32[]{:S(2)}) copy-start(bf16[8,48,192]{2,1,0:T(8,128)(2,1)} %constant.32.clone.low_ref) | copy-start | bytes 442372
  36.8 25.8 %copy-start.6 = (bf16[8,48,192]{2,1,0:T(8,128)(2,1)S(1)}, bf16[8,48,192]{2,1,0:T(8,128)(2,1)}, u32[]{:S(2)}) copy-start(bf16[8,48,192]{2,1,0:T(8,128)(2,1)} %constant.31.clone.high_ref) | copy-start | bytes 442372
  62.5 26.6 %copy-start.1 = (bf16[128,1024]{1,0:T(8,128)(2,1)S(1)}, bf16[128,1024]{1,0:T(8,128)(2,1)}, u32[]{:S(2)}) copy-start(bf16[128,1024]{1,0:T(8,128)(2,1)} %constant.42.clone.tl_ref) | copy-start | bytes 786436
  62.5 26.6 %copy-start.2 = (bf16[128,1024]{1,0:T(8,128)(2,1)S(1)}, bf16[128,1024]{1,0:T(8,128)(2,1)}, u32[]{:S(2)}) copy-start(bf16[128,1024]{1,0:T(8,128)(2,1)} %constant.41.clone.th_ref) | copy-start | bytes 786436
  62.5 26.6 %copy-start.3 = (bf16[1024,128]{1,0:T(8,128)(2,1)S(1)}, bf16[1024,128]{1,0:T(8,128)(2,1)}, u32[]{:S(2)}) copy-start(bf16[1024,128]{1,0:T(8,128)(2,1)} %constant.34.clone.zl_ref) | copy-start | bytes 786436
  62.5 26.6 %copy-start.4 = (bf16[1024,128]{1,0:T(8,128)(2,1)S(1)}, bf16[1024,128]{1,0:T(8,128)(2,1)}, u32[]{:S(2)}) copy-start(bf16[1024,128]{1,0:T(8,128)(2,1)} %constant.33.clone.zh_ref) | copy-start | bytes 786436
  62.5 26.6 %copy-start.10 = (bf16[4,64,128]{2,1,0:T(8,128)(2,1)S(1)}, bf16[4,64,128]{2,1,0:T(8,128)(2,1)}, u32[]{:S(2)}) copy-start(bf16[4,64,128]{2,1,0:T(8,128)(2,1)} %constant.40.clone.bl_ref) | copy-start | bytes 196612
  62.5 26.6 %copy-start.11 = (bf16[4,64,128]{2,1,0:T(8,128)(2,1)S(1)}, bf16[4,64,128]{2,1,0:T(8,128)(2,1)}, u32[]{:S(2)}) copy-start(bf16[4,64,128]{2,1,0:T(8,128)(2,1)} %constant.39.clone.bh_ref) | copy-start | bytes 196612
  62.5 26.6 %copy-start.12 = (f32[128,128]{1,0:T(8,128)S(1)}, f32[128,128]{1,0:T(8,128)}, u32[]{:S(2)}) copy-start(f32[128,128]{1,0:T(8,128)} %constant.38.clone.own_ref) | copy-start | bytes 196612
  62.5 26.6 %copy-start.13 = (f32[128,128]{1,0:T(8,128)S(1)}, f32[128,128]{1,0:T(8,128)}, u32[]{:S(2)}) copy-start(f32[128,128]{1,0:T(8,128)} %constant.37.clone.wave_ref) | copy-start | bytes 196612
  62.5 26.6 %copy-start.14 = (bf16[128,192]{1,0:T(8,128)(2,1)S(1)}, bf16[128,192]{1,0:T(8,128)(2,1)}, u32[]{:S(2)}) copy-start(bf16[128,192]{1,0:T(8,128)(2,1)} %constant.36.clone.yl_ref) | copy-start | bytes 147460
  62.5 26.6 %copy-start.15 = (bf16[128,192]{1,0:T(8,128)(2,1)S(1)}, bf16[128,192]{1,0:T(8,128)(2,1)}, u32[]{:S(2)}) copy-start(bf16[128,192]{1,0:T(8,128)(2,1)} %constant.35.clone.yh_ref) | copy-start | bytes 147460
  90.5 30.5 %copy-start.8 = (bf16[8,32,128]{2,1,0:T(8,128)(2,1)S(1)}, bf16[8,32,128]{2,1,0:T(8,128)(2,1)}, u32[]{:S(2)}) copy-start(bf16[8,32,128]{2,1,0:T(8,128)(2,1)} %constant.44.clone.low_ref) | copy-start | bytes 196612
  90.5 30.5 %copy-start.9 = (bf16[8,32,128]{2,1,0:T(8,128)(2,1)S(1)}, bf16[8,32,128]{2,1,0:T(8,128)(2,1)}, u32[]{:S(2)}) copy-start(bf16[8,32,128]{2,1,0:T(8,128)(2,1)} %constant.43.clone.high_ref) | copy-start | bytes 196612
